TPU v7x, 16 devices: a 4x2x1 block of a 4x4x8 slice. The times are simulated.
16 devices in a mesh: dp: 2 (over y, z), tp: 8 (over x, core).
Axes of the slice: x: 4, y: 2, z: 1, core: 2. Of those that a mesh axis runs over, the one named last changes fastest.
The devices are a block of a 4x4x8 slice.
Arguments:
- x_in: bfloat16 [2, 2048, 3072], P('dp', 'tp'), parts along dimension 0
- x_mid: bfloat16 [2, 2048, 3072], P('dp', 'tp'), parts along dimension 0
- d_out: bfloat16 [2, 2048, 3072], P('dp', 'tp'), parts along dimension 0
- q_saved: bfloat16 [2, 2048, 32, 96], P('dp', None, 'tp'), parts along dimension 0
- k_saved: bfloat16 [2, 2048, 32, 96], P('dp', None, 'tp'), parts along dimension 0
- v_saved: bfloat16 [2, 2048, 32, 96], P('dp', None, 'tp'), parts along dimension 0
- z_saved: bfloat16 [2, 2048, 12288], P('dp', None, 'tp'), parts along dimension 0
- ln1_gain: float32 [3072], replicated
- ln1_bias: float32 [3072], replicated
- ln2_gain: float32 [3072], replicated
- ln2_bias: float32 [3072], replicated
- w_qkv: bfloat16 [3, 3072, 32, 96], P(None, None, 'tp')
- w_proj: bfloat16 [32, 96, 3072], P('tp')
- w_fc1: bfloat16 [3072, 12288], P(None, 'tp')
- w_fc2: bfloat16 [12288, 3072], P('tp')
Outputs:
- output 1: bfloat16 [2, 2048, 3072], P('dp', 'tp'), parts along dimension 0
- output 2: float32 [6, 3072, 32, 96], P('dp', None, 'tp'), parts along dimension 0
- output 3: float32 [6, 32, 96], P('dp', 'tp'), parts along dimension 0
- output 4: float32 [64, 96, 3072], P(('dp', 'tp')), parts along dimension 0
- output 5: float32 [6144, 12288], P('dp', 'tp'), parts along dimension 0
- output 6: float32 [24576], P(('dp', 'tp')), parts along dimension 0
- output 7: float32 [24576, 3072], P(('dp', 'tp')), parts along dimension 0
- output 8: float32 [12, 3072], P('dp'), parts along dimension 0
There are 2 independent parts. A program takes and returns all parts, laid end to end along the dimension named above; an argument that names none is the same for every part.
All inputs are finite; a program needn't handle non-finite values.
Results may differ from a plain program's by a relative error of at most 0.0117503.
Values are sent between devices in bfloat16 or wider.
A program may use at most 768 MiB of HBM per device.

v0:
```python
import jax
import jax.numpy as jnp
from jax import lax
from jax.sharding import PartitionSpec as P

LN_EPS = 1e-5
GELU_COEF = 0.044715
GELU_SCALE = 0.7978845608028654


def layer_norm_fwd(token_rows, norm_gain, norm_bias):
    rows_f32 = token_rows.astype(jnp.float32)
    centered = rows_f32 - jnp.mean(rows_f32, axis=-1, keepdims=True)
    inv_std = lax.rsqrt(jnp.mean(centered * centered, axis=-1, keepdims=True) + LN_EPS)
    x_hat = centered * inv_std
    return x_hat, inv_std, (x_hat * norm_gain + norm_bias).astype(jnp.bfloat16)


def layer_norm_bwd(grad_norm, x_hat, inv_std, norm_gain):
    grad_hat = grad_norm * norm_gain
    centered_grad = grad_hat - jnp.mean(grad_hat, axis=-1, keepdims=True)
    return inv_std * (centered_grad - x_hat * jnp.mean(grad_hat * x_hat, axis=-1, keepdims=True))


def gelu_parts(pre_act):
    tanh_val = jnp.tanh(GELU_SCALE * (pre_act + GELU_COEF * pre_act * pre_act * pre_act))
    act_value = 0.5 * pre_act * (1.0 + tanh_val)
    act_slope = 0.5 * (1.0 + tanh_val) + 0.5 * pre_act * (1.0 - tanh_val * tanh_val) * GELU_SCALE * (1.0 + 3.0 * GELU_COEF * pre_act * pre_act)
    return act_value, act_slope


def attention_grads(q_heads, k_heads, v_heads, grad_ctx):
    seq_len = q_heads.shape[1]
    score_scale = q_heads.shape[-1] ** -0.5
    scores = jnp.einsum('bqhe,bkhe->bhqk', q_heads, k_heads, preferred_element_type=jnp.float32) * score_scale
    row_ids = lax.broadcasted_iota(jnp.int32, (seq_len, seq_len), 0)
    col_ids = lax.broadcasted_iota(jnp.int32, (seq_len, seq_len), 1)
    scores = jnp.where(row_ids >= col_ids, scores, -1e30)
    attn_probs = jax.nn.softmax(scores, axis=-1)
    probs_low = attn_probs.astype(jnp.bfloat16)
    context = jnp.einsum('bhqk,bkhe->bqhe', probs_low, v_heads, preferred_element_type=jnp.float32).astype(jnp.bfloat16)
    grad_probs = jnp.einsum('bqhe,bkhe->bhqk', grad_ctx, v_heads, preferred_element_type=jnp.float32)
    grad_scores = (attn_probs * (grad_probs - jnp.sum(grad_probs * attn_probs, axis=-1, keepdims=True)) * score_scale).astype(jnp.bfloat16)
    grad_q = jnp.einsum('bhqk,bkhe->bqhe', grad_scores, k_heads, preferred_element_type=jnp.float32).astype(jnp.bfloat16)
    grad_k = jnp.einsum('bhqk,bqhe->bkhe', grad_scores, q_heads, preferred_element_type=jnp.float32).astype(jnp.bfloat16)
    grad_v = jnp.einsum('bhqk,bqhe->bkhe', probs_low, grad_ctx, preferred_element_type=jnp.float32).astype(jnp.bfloat16)
    return context, grad_q, grad_k, grad_v


def solution(mesh):
    def local_backward(x_in, x_mid, d_out, q_saved, k_saved, v_saved, z_saved, ln1_gain, ln1_bias, ln2_gain, ln2_bias, w_qkv, w_proj, w_fc1, w_fc2):
        norm2_hat, norm2_rstd, h2_local = layer_norm_fwd(x_mid, ln2_gain, ln2_bias)
        h2_full = lax.all_gather(h2_local, 'tp', axis=1, tiled=True)
        dout_full = lax.all_gather(d_out, 'tp', axis=1, tiled=True)
        act_value, act_slope = gelu_parts(z_saved.astype(jnp.float32))
        grad_wfc2 = jnp.einsum('bsf,bsd->fd', act_value.astype(jnp.bfloat16), dout_full, preferred_element_type=jnp.float32)
        grad_pre = (jnp.einsum('bsd,fd->bsf', dout_full, w_fc2, preferred_element_type=jnp.float32) * act_slope).astype(jnp.bfloat16)
        grad_wfc1 = jnp.einsum('bsd,bsf->df', h2_full, grad_pre, preferred_element_type=jnp.float32)
        grad_bfc1 = jnp.sum(grad_pre, axis=(0, 1), dtype=jnp.float32)
        h2_partial = jnp.einsum('bsf,df->bsd', grad_pre, w_fc1, preferred_element_type=jnp.float32).astype(jnp.bfloat16)
        grad_h2 = lax.psum_scatter(h2_partial, 'tp', scatter_dimension=1, tiled=True).astype(jnp.float32)
        grad_mid = (d_out.astype(jnp.float32) + layer_norm_bwd(grad_h2, norm2_hat, norm2_rstd, ln2_gain)).astype(jnp.bfloat16)
        mid_full = lax.all_gather(grad_mid, 'tp', axis=1, tiled=True)
        norm1_hat, norm1_rstd, h1_local = layer_norm_fwd(x_in, ln1_gain, ln1_bias)
        h1_full = lax.all_gather(h1_local, 'tp', axis=1, tiled=True)
        grad_ctx = jnp.einsum('bsd,hed->bshe', mid_full, w_proj, preferred_element_type=jnp.float32).astype(jnp.bfloat16)
        context, grad_q, grad_k, grad_v = attention_grads(q_saved, k_saved, v_saved, grad_ctx)
        grad_wproj = jnp.einsum('bshe,bsd->hed', context, mid_full, preferred_element_type=jnp.float32)
        qkv_grads = jnp.stack([grad_q, grad_k, grad_v])
        grad_wqkv = jnp.einsum('bsd,ibshe->idhe', h1_full, qkv_grads, preferred_element_type=jnp.float32)
        grad_bqkv = jnp.sum(qkv_grads, axis=(1, 2), dtype=jnp.float32)
        h1_partial = jnp.einsum('ibshe,idhe->bsd', qkv_grads, w_qkv, preferred_element_type=jnp.float32).astype(jnp.bfloat16)
        grad_h1 = lax.psum_scatter(h1_partial, 'tp', scatter_dimension=1, tiled=True).astype(jnp.float32)
        grad_x = (grad_mid.astype(jnp.float32) + layer_norm_bwd(grad_h1, norm1_hat, norm1_rstd, ln1_gain)).astype(jnp.bfloat16)
        vec_partial = jnp.stack([
            jnp.sum(grad_h1 * norm1_hat, axis=(0, 1)),
            jnp.sum(grad_h1, axis=(0, 1)),
            jnp.sum(grad_h2 * norm2_hat, axis=(0, 1)),
            jnp.sum(grad_h2, axis=(0, 1)),
            jnp.sum(grad_mid, axis=(0, 1), dtype=jnp.float32),
            jnp.sum(d_out, axis=(0, 1), dtype=jnp.float32),
        ])
        grad_vecs = lax.psum(vec_partial, 'tp')
        return grad_x, grad_wqkv, grad_bqkv, grad_wproj, grad_wfc1, grad_bfc1, grad_wfc2, grad_vecs

    tok_spec = P('dp', 'tp', None)
    head_spec = P('dp', None, 'tp', None)
    in_specs = (tok_spec, tok_spec, tok_spec, head_spec, head_spec, head_spec, P('dp', None, 'tp'),
                P(None), P(None), P(None), P(None),
                P(None, None, 'tp', None), P('tp', None, None), P(None, 'tp'), P('tp', None))
    out_specs = (tok_spec, P('dp', None, 'tp', None), P('dp', 'tp', None), P(('dp', 'tp'), None, None),
                 P('dp', 'tp'), P(('dp', 'tp')), P(('dp', 'tp'), None), P('dp', None))
    return jax.shard_map(local_backward, mesh=mesh, in_specs=in_specs, out_specs=out_specs, check_vma=False)
```

profile of v0, /device:TPU:113, one launch (start us, length us, event | category | flops | bytes accessed | tf_op | source)
XLA Modules:
  0.0 783.7 jit_solution(10824171024343732247)
XLA Ops:
  7.2 0.0 copy-start
  7.2 0.1 all-gather.5.cloned.1.call-start
  7.3 0.7 all-gather.5.cloned.1.call-update
  8.0 0.1 reduce-scatter.3.cloned.1.call-start
  8.1 68.1 %all-gather.5.cloned.1.call-done = bf16[1,2048,3072]{2,1,0:T(8,128)(2,1)} async-done(((bf16[1,256,3072]{2,1,0:T(8,128)(2,1)}), bf16[1,2048,3072]{2,1,0:T(8,128)(2,1)}) %all-gather.5.cloned.1.call-update) | async-done | bytes 12582928 | tf_op jit(solution)/shard_map/all_gather | solution.py:54
  76.2 33.5 %convert_reduce_fusion = (f32[1536]{0:T(1024)}, bf16[1,2048,1536]{2,1,0:T(8,128)(2,1)S(1)}) fusion(bf16[1,2048,1536]{2,1,0:T(8,128)(2,1)} %param.21, bf16[1536,3072]{1,0:T(8,128)(2,1)} %param.29, bf16[1,2048,3072]{2,1,0:T(8,128)(2,1)} %all-gather.5.cloned.1.call-done), kind=kOutput, calls=%fused_computation.50 | convolution fusion | flops 19396556800 | bytes 34609152 | tf_op jit(solution)/shard_map/bsd,fd->bsf/dot_general | solution.py:57
  109.7 2.7 copy-done.21
  112.4 25.2 %convert_bitcast_fusion = bf16[1,2048,3072]{2,1,0:T(8,128)(2,1)} fusion(bf16[3072,1536]{1,0:T(8,128)(2,1)} %param.28, bf16[1,2048,1536]{2,1,0:T(8,128)(2,1)S(1)} %get-tuple-element.24), kind=kOutput, calls=%fused_computation.51 | convolution fusion | flops 19333644288 | bytes 28311552 | tf_op jit(solution)/shard_map/bsf,df->bsd/dot_general | solution.py:60
  137.6 0.1 reduce-scatter.3.cloned.1.call-update
  137.7 0.4 all-gather.7.cloned.1.call-start
  138.1 1.7 convert_reduce_fusion.6
  139.8 2.0 fusion.83
  141.8 63.9 %reduce-scatter.3.cloned.1.call-done = bf16[1,256,3072]{2,1,0:T(8,128)(2,1)} async-done(((bf16[1,2048,3072]{2,1,0:T(8,128)(2,1)}), bf16[1,256,3072]{2,1,0:T(8,128)(2,1)}) %reduce-scatter.3.cloned.1.call-update) | async-done | bytes 1572880 | tf_op jit(solution)/shard_map/reduce_scatter | solution.py:61
  205.7 0.0 copy-done.14
  205.7 0.0 copy-done.18
  205.8 0.0 copy-start.5
  205.8 5.2 fusion.88
  211.0 0.0 copy-done.2
  211.0 0.0 copy-done.4
  211.0 0.0 copy-done.5
  211.0 3.6 convert_reduce_fusion.5
  214.7 0.1 all-gather.7.cloned.1.call-update
  214.7 0.1 reduce-scatter.5.cloned.1.call-start
  214.8 4.1 iota_compare_fusion
  218.9 37.1 %fusion.149 = (f32[4,2048]{1,0:T(4,128)S(1)}, f32[4,2048,2048]{1,2,0:T(8,128)}) fusion(pred[2048,2048]{0,1:T(8,128)(4,1)} %iota_compare_fusion, bf16[1,2048,4,96]{1,3,2,0:T(8,128)(2,1)} %param.19, bf16[1,2048,4,96]{1,3,2,0:T(8,128)(2,1)} %param.18), kind=kOutput, calls=%fused_computation.148 | convolution fusion | flops 3288336384 | bytes 74481664 | tf_op jit(solution)/shard_map/sub | solution.py:39
  256.0 22.7 %all-gather.7.cloned.1.call-done = bf16[1,2048,3072]{2,1,0:T(8,128)(2,1)} async-done(((bf16[1,256,3072]{2,1,0:T(8,128)(2,1)}), bf16[1,2048,3072]{2,1,0:T(8,128)(2,1)}) %all-gather.7.cloned.1.call-update) | async-done | bytes 12582928 | tf_op jit(solution)/shard_map/all_gather | solution.py:63
  278.6 0.0 copy-done
  278.6 8.4 %fusion.90 = bf16[2048,4,96]{0,2,1:T(8,128)(2,1)S(1)} fusion(bf16[4,96,3072]{2,1,0:T(8,128)(2,1)S(1)} %copy-done, bf16[1,2048,3072]{2,1,0:T(8,128)(2,1)} %all-gather.7.cloned.1.call-done), kind=kOutput, calls=%fused_computation.110 | convolution fusion | flops 4832624640 | bytes 16515072 | tf_op jit(solution)/shard_map/bsd,hed->bshe/dot_general | solution.py:66
  287.1 0.0 copy-done.7
  287.1 0.0 copy-start.6
  287.1 23.1 %fusion.122 = f32[4,2048,2048]{1,2,0:T(8,128)} fusion(bf16[2048,4,96]{0,2,1:T(8,128)(2,1)S(1)} %fusion.90, bf16[1,2048,4,96]{1,3,2,0:T(8,128)(2,1)S(1)} %copy-done.7), kind=kOutput, calls=%fused_computation.121 | convolution fusion | flops 3221225472 | bytes 70254592 | tf_op jit(solution)/shard_map/bqhe,bkhe->bhqk/dot_general | solution.py:42
  310.2 24.9 %fusion.116 = bf16[1,1,2048,4,96]{2,4,3,1,0:T(8,128)(2,1)} fusion(bf16[2048,4,96]{0,2,1:T(8,128)(2,1)} %copy-done.6, f32[4,2048,2048]{1,2,0:T(8,128)} %get-tuple-element.22, f32[4,2048]{1,0:T(4,128)S(1)} %get-tuple-element.21), kind=kOutput, calls=%fused_computation.118 | convolution fusion | flops 3255566336 | bytes 70287360 | tf_op jit(solution)/shard_map/bhqk,bqhe->bkhe/dot_general | solution.py:46
  335.2 83.0 %fusion.105 = bf16[1,1,2048,4,96]{2,4,3,1,0:T(8,128)(2,1)} fusion(f32[4,2048,2048]{1,2,0:T(8,128)} %fusion.122, bf16[1,2048,4,96]{1,3,2,0:T(8,128)(2,1)S(1)} %copy-done.20, f32[4,2048,2048]{1,2,0:T(8,128)} %get-tuple-element.22, f32[4,2048]{1,0:T(4,128)S(1)} %get-tuple-element.21), kind=kOutput, calls=%fused_computation.115 | convolution fusion | flops 3339462656 | bytes 137396224 | tf_op jit(solution)/shard_map/bhqk,bqhe->bkhe/dot_general | solution.py:45
  418.1 83.0 %fusion.108 = bf16[1,1,2048,4,96]{2,4,3,1,0:T(8,128)(2,1)} fusion(f32[4,2048,2048]{1,2,0:T(8,128)} %fusion.122, bf16[1,2048,4,96]{1,3,2,0:T(8,128)(2,1)} %param.19, f32[4,2048,2048]{1,2,0:T(8,128)} %get-tuple-element.22, f32[4,2048]{1,0:T(4,128)S(1)} %get-tuple-element.21), kind=kOutput, calls=%fused_computation.116 | convolution fusion | flops 3339462656 | bytes 137396224 | tf_op jit(solution)/shard_map/bhqk,bkhe->bqhe/dot_general | solution.py:44
  501.2 22.2 %fusion.44 = bf16[1,2048,3072]{2,1,0:T(8,128)(2,1)} fusion(bf16[3,3072,4,96]{1,3,2,0:T(8,128)(2,1)} %param.26, bf16[1,1,2048,4,96]{2,4,3,1,0:T(8,128)(2,1)S(1)} %copy-done.8, bf16[1,1,2048,4,96]{2,4,3,1,0:T(8,128)(2,1)} %fusion.105, bf16[1,1,2048,4,96]{2,4,3,1,0:T(8,128)(2,1)} %fusion.108), kind=kOutput, calls=%fused_computation.52 | convolution fusion | flops 14506524672 | bytes 24379392 | tf_op jit(solution)/shard_map/ibshe,idhe->bsd/dot_general | solution.py:72
  523.4 0.1 reduce-scatter.5.cloned.1.call-update
  523.5 0.0 copy-start.15
  523.5 0.0 copy-start.19
  523.5 0.1 all-gather.11.cloned.1.call-start
  523.6 0.6 all-gather.11.cloned.1.call-update
  524.1 0.1 all-gather.9.cloned.1.call-start
  524.2 0.6 copy-done.3
  524.8 0.3 convert_reduce_fusion.4
  525.1 0.6 fusion.78
  525.7 65.8 %reduce-scatter.5.cloned.1.call-done = bf16[1,256,3072]{2,1,0:T(8,128)(2,1)} async-done(((bf16[1,2048,3072]{2,1,0:T(8,128)(2,1)}), bf16[1,256,3072]{2,1,0:T(8,128)(2,1)}) %reduce-scatter.5.cloned.1.call-update) | async-done | bytes 1572880 | tf_op jit(solution)/shard_map/reduce_scatter | solution.py:73
  591.5 0.0 copy-done.15
  591.5 4.3 fusion.89
  595.8 0.1 all-gather.9.cloned.1.call-update
  595.9 0.1 all-reduce.2.cloned.1.call-start
  596.0 36.3 %fusion.38 = f32[1536,3072]{1,0:T(8,128)} fusion(bf16[1,2048,3072]{2,1,0:T(8,128)(2,1)} %all-gather.5.cloned.1.call-done, bf16[1,2048,1536]{2,1,0:T(8,128)(2,1)} %param.21), kind=kOutput, calls=%fused_computation.46 | convolution fusion | flops 19358810112 | bytes 37748736 | tf_op jit(solution)/shard_map/bsf,bsd->fd/dot_general | solution.py:56
  632.3 0.0 copy-done.9
  632.3 1.4 convert_reduce_fusion.1
  633.7 23.6 %all-gather.11.cloned.1.call-done = bf16[1,2048,3072]{2,1,0:T(8,128)(2,1)} async-done(((bf16[1,256,3072]{2,1,0:T(8,128)(2,1)}), bf16[1,2048,3072]{2,1,0:T(8,128)(2,1)}) %all-gather.11.cloned.1.call-update) | async-done | bytes 12582928 | tf_op jit(solution)/shard_map/all_gather | solution.py:53
  657.3 26.4 %fusion.32 = f32[3072,1536]{1,0:T(8,128)} fusion(bf16[1,2048,3072]{2,1,0:T(8,128)(2,1)} %all-gather.11.cloned.1.call-done, bf16[1,2048,1536]{2,1,0:T(8,128)(2,1)} %copy-done.21), kind=kOutput, calls=%fused_computation.40 | convolution fusion | flops 19327352832 | bytes 37748736 | tf_op jit(solution)/shard_map/bsd,bsf->df/dot_general | solution.py:58
  683.7 0.0 copy-start.17
  683.7 30.3 %fusion.34 = f32[4,96,3072]{2,1,0:T(8,128)} fusion(bf16[1,2048,3072]{2,1,0:T(8,128)(2,1)} %all-gather.7.cloned.1.call-done, bf16[1,2048,4,96]{1,3,2,0:T(8,128)(2,1)} %param.20, f32[4,2048,2048]{1,2,0:T(8,128)} %get-tuple-element.22, f32[4,2048]{1,0:T(4,128)S(1)} %get-tuple-element.21), kind=kOutput, calls=%fused_computation.42 | convolution fusion | flops 8087404544 | bytes 86016000 | tf_op jit(solution)/shard_map/bshe,bsd->hed/dot_general | solution.py:68
  714.1 0.8 stack.43
  714.8 0.1 all-reduce.2.cloned.1.call-update
  714.9 4.7 fusion.85
  719.5 3.5 all-gather.9.cloned.1.call-done
  723.0 21.2 %fusion.48 = f32[3,3072,4,96]{1,3,2,0:T(8,128)} fusion(bf16[1,2048,3072]{2,1,0:T(8,128)(2,1)} %all-gather.9.cloned.1.call-done, bf16[1,1,2048,4,96]{2,4,3,1,0:T(8,128)(2,1)} %fusion.116, bf16[1,1,2048,4,96]{2,4,3,1,0:T(8,128)(2,1)} %fusion.105, bf16[1,1,2048,4,96]{2,4,3,1,0:T(8,128)(2,1)} %fusion.108), kind=kOutput, calls=%fused_computation.56 | convolution fusion | flops 14500233216 | bytes 31457280 | tf_op jit(solution)/shard_map/bsd,ibshe->idhe/dot_general | solution.py:70
  744.2 30.7 %all-reduce.2.cloned.1.call-done = f32[6,3072]{1,0:T(8,128)} async-done(((f32[6,3072]{1,0:T(8,128)}), f32[6,3072]{1,0:T(8,128)}) %all-reduce.2.cloned.1.call-update) | async-done | bytes 73744 | tf_op jit(solution)/shard_map/psum | solution.py:83
  774.8 1.5 copy.40
  776.4 0.0 copy-done.1
  (33 shorter events, 0.1 us)
Async XLA Ops:
  7.2 271.5 %copy-start = (bf16[4,96,3072]{2,1,0:T(8,128)(2,1)S(1)}, bf16[4,96,3072]{2,1,0:T(8,128)(2,1)}, u32[]{:S(2)}) copy-start(bf16[4,96,3072]{2,1,0:T(8,128)(2,1)} %param.27) | copy-start | bytes 7077892
  7.2 69.0 %all-gather.5.cloned.1.call-start = ((), (), s32[]{:S(2)}) async-start(), calls=%async_computation.2 | async-start | bytes 14155776 | tf_op jit(solution)/shard_map/all_gather | solution.py:54
  8.0 197.7 %reduce-scatter.3.cloned.1.call-start = ((), (), s32[]{:S(2)}) async-start(), calls=%async_computation.3 | async-start | bytes 14155776 | tf_op jit(solution)/shard_map/reduce_scatter | solution.py:61
  109.7 2.7 copy-start.21
  137.6 68.1 %copy-start.14 = (f32[3072]{0:T(1024)S(1)}, f32[3072]{0:T(1024)}, u32[]{:S(2)}) copy-start(f32[3072]{0:T(1024)} %param.24) | copy-start | bytes 36868
  137.6 68.1 %copy-start.18 = (f32[3072]{0:T(1024)S(1)}, f32[3072]{0:T(1024)}, u32[]{:S(2)}) copy-start(f32[3072]{0:T(1024)} %param.25) | copy-start | bytes 36868
  137.7 141.0 %all-gather.7.cloned.1.call-start = ((), (), s32[]{:S(2)}) async-start(), calls=%async_computation.4 | async-start | bytes 14155776 | tf_op jit(solution)/shard_map/all_gather | solution.py:63
  205.7 5.2 copy-start.2
  205.7 5.2 copy-start.4
  205.8 5.2 copy-start.5
  214.7 376.8 %reduce-scatter.5.cloned.1.call-start = ((), (), s32[]{:S(2)}) async-start(), calls=%async_computation.5 | async-start | bytes 14155776 | tf_op jit(solution)/shard_map/reduce_scatter | solution.py:73
  278.6 8.4 %copy-start.7 = (bf16[1,2048,4,96]{1,3,2,0:T(8,128)(2,1)S(1)}, bf16[1,2048,4,96]{1,3,2,0:T(8,128)(2,1)}, u32[]{:S(2)}) copy-start(bf16[1,2048,4,96]{1,3,2,0:T(8,128)(2,1)} %param.20) | copy-start | bytes 4718596
  287.1 23.1 %copy-start.6 = (bf16[2048,4,96]{0,2,1:T(8,128)(2,1)}, bf16[2048,4,96]{0,2,1:T(8,128)(2,1)S(1)}, u32[]{:S(2)}) copy-start(bf16[2048,4,96]{0,2,1:T(8,128)(2,1)S(1)} %fusion.90) | copy-start | bytes 4718596
  310.2 24.9 %copy-start.20 = (bf16[1,2048,4,96]{1,3,2,0:T(8,128)(2,1)S(1)}, bf16[1,2048,4,96]{1,3,2,0:T(8,128)(2,1)}, u32[]{:S(2)}) copy-start(bf16[1,2048,4,96]{1,3,2,0:T(8,128)(2,1)} %param.18) | copy-start | bytes 4718596
  418.1 83.0 %copy-start.8 = (bf16[1,1,2048,4,96]{2,4,3,1,0:T(8,128)(2,1)S(1)}, bf16[1,1,2048,4,96]{2,4,3,1,0:T(8,128)(2,1)}, u32[]{:S(2)}) copy-start(bf16[1,1,2048,4,96]{2,4,3,1,0:T(8,128)(2,1)} %fusion.116) | copy-start | bytes 4718596
  523.4 1.4 copy-start.3
  523.5 68.0 %copy-start.15 = (f32[3072]{0:T(1024)S(1)}, f32[3072]{0:T(1024)}, u32[]{:S(2)}) copy-start(f32[3072]{0:T(1024)} %param.22) | copy-start | bytes 36868
  523.5 68.0 %copy-start.19 = (f32[3072]{0:T(1024)S(1)}, f32[3072]{0:T(1024)}, u32[]{:S(2)}) copy-start(f32[3072]{0:T(1024)} %param.23) | copy-start | bytes 36868
  523.5 133.8 %all-gather.11.cloned.1.call-start = ((), (), s32[]{:S(2)}) async-start(), calls=%async_computation.7 | async-start | bytes 14155776 | tf_op jit(solution)/shard_map/all_gather | solution.py:53
  524.1 198.8 %all-gather.9.cloned.1.call-start = ((), (), s32[]{:S(2)}) async-start(), calls=%async_computation.6 | async-start | bytes 14155776 | tf_op jit(solution)/shard_map/all_gather | solution.py:65
  595.9 178.9 %all-reduce.2.cloned.1.call-start = ((), (), s32[]{:S(2)}) async-start(), calls=%async_computation.8 | async-start | bytes 196608 | tf_op jit(solution)/shard_map/psum | solution.py:83
  596.0 36.3 %copy-start.9 = (bf16[1,1,2048,4,96]{2,4,3,1,0:T(8,128)(2,1)S(1)}, bf16[1,1,2048,4,96]{2,4,3,1,0:T(8,128)(2,1)}, u32[]{:S(2)}) copy-start(bf16[1,1,2048,4,96]{2,4,3,1,0:T(8,128)(2,1)} %fusion.116) | copy-start | bytes 4718596
  596.0 36.3 %copy-start.10 = (bf16[1,1,2048,4,96]{2,4,3,1,0:T(8,128)(2,1)S(1)}, bf16[1,1,2048,4,96]{2,4,3,1,0:T(8,128)(2,1)}, u32[]{:S(2)}) copy-start(bf16[1,1,2048,4,96]{2,4,3,1,0:T(8,128)(2,1)} %fusion.105) | copy-start | bytes 4718596
  596.0 36.3 %copy-start.11 = (bf16[1,1,2048,4,96]{2,4,3,1,0:T(8,128)(2,1)S(1)}, bf16[1,1,2048,4,96]{2,4,3,1,0:T(8,128)(2,1)}, u32[]{:S(2)}) copy-start(bf16[1,1,2048,4,96]{2,4,3,1,0:T(8,128)(2,1)} %fusion.108) | copy-start | bytes 4718596
  683.7 30.3 %copy-start.12 = (f32[3072]{0:T(1024)S(1)}, f32[3072]{0:T(1024)}, u32[]{:S(2)}) copy-start(f32[3072]{0:T(1024)} %get-tuple-element.16) | copy-start | bytes 36868
  683.7 30.3 %copy-start.13 = (f32[3072]{0:T(1024)S(1)}, f32[3072]{0:T(1024)}, u32[]{:S(2)}) copy-start(f32[3072]{0:T(1024)} %get-tuple-element.20) | copy-start | bytes 36868
  683.7 30.3 %copy-start.16 = (f32[3072]{0:T(1024)S(1)}, f32[3072]{0:T(1024)}, u32[]{:S(2)}) copy-start(f32[3072]{0:T(1024)} %get-tuple-element.8) | copy-start | bytes 36868
  683.7 30.4 %copy-start.17 = (f32[3072]{0:T(1024)S(1)}, f32[3072]{0:T(1024)}, u32[]{:S(2)}) copy-start(f32[3072]{0:T(1024)} %get-tuple-element.14) | copy-start | bytes 36868
  723.0 53.4 %copy-start.1 = (bf16[4,96,3072]{2,1,0:T(8,128)(2,1)S(1)}, bf16[4,96,3072]{2,1,0:T(8,128)(2,1)}, u32[]{:S(2)}) copy-start(bf16[4,96,3072]{2,1,0:T(8,128)(2,1)} %param.27) | copy-start | bytes 7077892
Sparse Core Ops, SparseCore 0:
  9.6 66.5 all-gather.4
  137.8 67.8 reduce-scatter.2
  214.8 63.7 all-gather.6
  523.6 67.8 reduce-scatter.4
  593.5 63.7 all-gather.10
  659.3 63.6 all-gather.8
  725.9 48.8 all-reduce.1
where the time goes:
time: 794 us; the launch traced here: 784 us
  matrix products  455 us (57%)
  waiting for transfers between devices  280 us (35%)
  other arithmetic  27.9 us (4%)
  between operations  14.8 us (2%)
    dot_general x1, matrix products, attention_grads(): jnp.einsum('bhqk,bkhe->bqhe', grad_scores, k_heads, preferred_element_typ...  83 us
    dot_general x1, matrix products, attention_grads(): jnp.einsum('bhqk,bqhe->bkhe', grad_scores, q_heads, preferred_element_typ...  83 us
    all_gather x1, waiting for transfers between devices, local_backward(): dout_full = lax.all_gather(d_out, 'tp', axis=1, tiled=True)  68.1 us
    reduce_scatter x1, waiting for transfers between devices, local_backward(): lax.psum_scatter(h1_partial, 'tp', scatter_dimension=1, tiled=True)  65.8 us
    reduce_scatter x1, waiting for transfers between devices, local_backward(): lax.psum_scatter(h2_partial, 'tp', scatter_dimension=1, tiled=True)  63.9 us
    sub x1, matrix products, attention_grads(): attn_probs = jax.nn.softmax(scores, axis=-1)  37.1 us
    dot_general x1, matrix products, local_backward(): jnp.einsum('bsf,bsd->fd', act_value.astype(jnp.bfloat16), dout_full, pref...  36.3 us
    dot_general x1, matrix products, local_backward(): jnp.einsum('bsd,fd->bsf', dout_full, w_fc2, preferred_element_type=jnp.fl...  33.5 us
  transfers between devices with their start and end apart: 7, of which 7 were waited for; matrix products, arithmetic and copies ran while one was open for 22% of the time, Pallas kernels for 0%

commit v1 on v0

--- a/solution.py
+++ b/solution.py
@@ -1,6 +1,10 @@
+import functools
+import math
 import jax
 import jax.numpy as jnp
 from jax import lax
+from jax.experimental import pallas as pl
+from jax.experimental.pallas import tpu as pltpu
 from jax.sharding import PartitionSpec as P
 
 LN_EPS = 1e-5
@@ -29,22 +33,134 @@
     return act_value, act_slope
 
 
-def attention_grads(q_heads, k_heads, v_heads, grad_ctx):
-    seq_len = q_heads.shape[1]
-    score_scale = q_heads.shape[-1] ** -0.5
-    scores = jnp.einsum('bqhe,bkhe->bhqk', q_heads, k_heads, preferred_element_type=jnp.float32) * score_scale
-    row_ids = lax.broadcasted_iota(jnp.int32, (seq_len, seq_len), 0)
-    col_ids = lax.broadcasted_iota(jnp.int32, (seq_len, seq_len), 1)
-    scores = jnp.where(row_ids >= col_ids, scores, -1e30)
-    attn_probs = jax.nn.softmax(scores, axis=-1)
-    probs_low = attn_probs.astype(jnp.bfloat16)
-    context = jnp.einsum('bhqk,bkhe->bqhe', probs_low, v_heads, preferred_element_type=jnp.float32).astype(jnp.bfloat16)
-    grad_probs = jnp.einsum('bqhe,bkhe->bhqk', grad_ctx, v_heads, preferred_element_type=jnp.float32)
-    grad_scores = (attn_probs * (grad_probs - jnp.sum(grad_probs * attn_probs, axis=-1, keepdims=True)) * score_scale).astype(jnp.bfloat16)
-    grad_q = jnp.einsum('bhqk,bkhe->bqhe', grad_scores, k_heads, preferred_element_type=jnp.float32).astype(jnp.bfloat16)
-    grad_k = jnp.einsum('bhqk,bqhe->bkhe', grad_scores, q_heads, preferred_element_type=jnp.float32).astype(jnp.bfloat16)
-    grad_v = jnp.einsum('bhqk,bqhe->bkhe', probs_low, grad_ctx, preferred_element_type=jnp.float32).astype(jnp.bfloat16)
-    return context, grad_q, grad_k, grad_v
+LANES = 128
+NT = (((1,), (1,)), ((), ()))
+NN = (((1,), (0,)), ((), ()))
+TN = (((0,), (0,)), ((), ()))
+
+
+def dot(lhs, rhs, dims):
+    return lax.dot_general(lhs, rhs, dims, preferred_element_type=jnp.float32)
+
+
+def attention_kernel(head_dim, q_ref, k_ref, v_ref, mid_ref, wo_ref, ctx_ref, dq_ref, dk_ref, dv_ref,
+                     s_scr, dp_scr, dk_acc, dv_acc, dctx_scr, ctx_scr, dq_scr, m_scr, l_scr, d_scr):
+    n_heads, blk, _ = q_ref.shape
+    q_idx = pl.program_id(0)
+    scale = head_dim ** -0.5
+    exp_scale = scale * math.log2(math.e)
+
+    @pl.when(q_idx == 0)
+    def _():
+        dk_acc[...] = jnp.zeros_like(dk_acc)
+        dv_acc[...] = jnp.zeros_like(dv_acc)
+
+    dctx_all = dot(mid_ref[...], wo_ref[...], NT).astype(jnp.bfloat16)
+    for head in range(n_heads):
+        dctx_scr[head] = dctx_all[:, head * LANES:(head + 1) * LANES]
+
+    def lane_fold(vals, op):
+        out = vals[:, :LANES]
+        for piece in range(1, vals.shape[1] // LANES):
+            out = op(out, vals[:, piece * LANES:(piece + 1) * LANES])
+        return out
+
+    def per_head(head, carry):
+        q_blk = q_ref[head]
+        dctx_blk = dctx_scr[head]
+
+        def scores(j):
+            rows = pl.ds(pl.multiple_of(j * blk, blk), blk)
+            dp_scr[j] = dot(dctx_blk, v_ref[head, rows, :], NT)
+            return dot(q_blk, k_ref[head, rows, :], NT)
+
+        row_ids = lax.broadcasted_iota(jnp.int32, (blk, blk), 0)
+        col_ids = lax.broadcasted_iota(jnp.int32, (blk, blk), 1)
+        diag = jnp.where(row_ids >= col_ids, scores(q_idx), -1e30)
+        s_scr[q_idx] = diag
+        m_scr[...] = lane_fold(diag, jnp.maximum)
+
+        def pass_max(j, c):
+            s_blk = scores(j)
+            s_scr[j] = s_blk
+            m_scr[...] = jnp.maximum(m_scr[...], lane_fold(s_blk, jnp.maximum))
+            return c
+
+        lax.fori_loop(0, q_idx, pass_max, 0)
+        row_max = jnp.max(m_scr[...], axis=1, keepdims=True)
+        l_scr[...] = jnp.zeros_like(l_scr)
+        d_scr[...] = jnp.zeros_like(d_scr)
+
+        def pass_exp(j, c):
+            prob = jnp.exp2((s_scr[j] - row_max) * exp_scale)
+            s_scr[j] = prob
+            l_scr[...] += lane_fold(prob, jnp.add)
+            d_scr[...] += lane_fold(prob * dp_scr[j], jnp.add)
+            return c
+
+        lax.fori_loop(0, q_idx + 1, pass_exp, 0)
+        inv_sum = 1.0 / jnp.sum(l_scr[...], axis=1, keepdims=True)
+        delta = jnp.sum(d_scr[...], axis=1, keepdims=True) * inv_sum
+        ctx_scr[head] = jnp.zeros((blk, LANES), jnp.float32)
+        dq_scr[head] = jnp.zeros((blk, LANES), jnp.float32)
+
+        def pass_grad(j, c):
+            rows = pl.ds(pl.multiple_of(j * blk, blk), blk)
+            prob = s_scr[j] * inv_sum
+            prob_low = prob.astype(jnp.bfloat16)
+            ds_low = (prob * (dp_scr[j] - delta) * scale).astype(jnp.bfloat16)
+            ctx_scr[head] += dot(prob_low, v_ref[head, rows, :], NN)
+            dq_scr[head] += dot(ds_low, k_ref[head, rows, :], NN)
+            dk_acc[head, rows, :] += dot(ds_low, q_blk, TN)
+            dv_acc[head, rows, :] += dot(prob_low, dctx_blk, TN)
+            return c
+
+        lax.fori_loop(0, q_idx + 1, pass_grad, 0)
+        return carry
+
+    lax.fori_loop(0, n_heads, per_head, 0)
+
+    def pack(scr):
+        return jnp.concatenate([scr[head][:, :head_dim] for head in range(n_heads)], axis=1).astype(jnp.bfloat16)
+
+    ctx_ref[...] = pack(ctx_scr)
+    dq_ref[...] = pack(dq_scr)
+
+    @pl.when(q_idx == pl.num_programs(0) - 1)
+    def _():
+        dk_ref[...] = pack(dk_acc)
+        dv_ref[...] = pack(dv_acc)
+
+
+def attention_grads(q_heads, k_heads, v_heads, mid_rows, w_proj):
+    _, seq, n_heads, head_dim = q_heads.shape
+    d_model = mid_rows.shape[-1]
+    blk = 256
+    n_blk = seq // blk
+    pad = LANES - head_dim
+    qp, kp, vp = (jnp.pad(jnp.moveaxis(a[0], 1, 0), ((0, 0), (0, 0), (0, pad))) for a in (q_heads, k_heads, v_heads))
+    wo = jnp.pad(w_proj, ((0, 0), (0, pad), (0, 0))).reshape(n_heads * LANES, d_model)
+    width = n_heads * head_dim
+    out = jax.ShapeDtypeStruct((seq, width), jnp.bfloat16)
+    full = lambda *shape: pl.BlockSpec(shape, lambda i: (0,) * len(shape))
+    flops = 6 * n_heads * seq * seq * LANES + 2 * seq * d_model * n_heads * LANES
+    return pl.pallas_call(
+        functools.partial(attention_kernel, head_dim),
+        grid=(n_blk,),
+        in_specs=[pl.BlockSpec((n_heads, blk, LANES), lambda i: (0, i, 0)), full(n_heads, seq, LANES), full(n_heads, seq, LANES),
+                  pl.BlockSpec((blk, d_model), lambda i: (i, 0)), full(n_heads * LANES, d_model)],
+        out_specs=[pl.BlockSpec((blk, width), lambda i: (i, 0)), pl.BlockSpec((blk, width), lambda i: (i, 0)),
+                   full(seq, width), full(seq, width)],
+        out_shape=[out] * 4,
+        scratch_shapes=[pltpu.VMEM((n_blk, blk, blk), jnp.float32), pltpu.VMEM((n_blk, blk, blk), jnp.float32),
+                        pltpu.VMEM((n_heads, seq, LANES), jnp.float32), pltpu.VMEM((n_heads, seq, LANES), jnp.float32),
+                        pltpu.VMEM((n_heads, blk, LANES), jnp.bfloat16),
+                        pltpu.VMEM((n_heads, blk, LANES), jnp.float32), pltpu.VMEM((n_heads, blk, LANES), jnp.float32),
+                        pltpu.VMEM((blk, LANES), jnp.float32), pltpu.VMEM((blk, LANES), jnp.float32), pltpu.VMEM((blk, LANES), jnp.float32)],
+        compiler_params=pltpu.CompilerParams(dimension_semantics=("arbitrary",), vmem_limit_bytes=56 * 2 ** 20),
+        cost_estimate=pl.CostEstimate(flops=flops, bytes_accessed=40 * 2 ** 20, transcendentals=n_heads * seq * seq // 2),
+        name="attention_grads",
+    )(qp, kp, vp, mid_rows, wo)
 
 
 def solution(mesh):
@@ -63,13 +179,17 @@
         mid_full = lax.all_gather(grad_mid, 'tp', axis=1, tiled=True)
         norm1_hat, norm1_rstd, h1_local = layer_norm_fwd(x_in, ln1_gain, ln1_bias)
         h1_full = lax.all_gather(h1_local, 'tp', axis=1, tiled=True)
-        grad_ctx = jnp.einsum('bsd,hed->bshe', mid_full, w_proj, preferred_element_type=jnp.float32).astype(jnp.bfloat16)
-        context, grad_q, grad_k, grad_v = attention_grads(q_saved, k_saved, v_saved, grad_ctx)
-        grad_wproj = jnp.einsum('bshe,bsd->hed', context, mid_full, preferred_element_type=jnp.float32)
-        qkv_grads = jnp.stack([grad_q, grad_k, grad_v])
-        grad_wqkv = jnp.einsum('bsd,ibshe->idhe', h1_full, qkv_grads, preferred_element_type=jnp.float32)
-        grad_bqkv = jnp.sum(qkv_grads, axis=(1, 2), dtype=jnp.float32)
-        h1_partial = jnp.einsum('ibshe,idhe->bsd', qkv_grads, w_qkv, preferred_element_type=jnp.float32).astype(jnp.bfloat16)
+        mid_rows = mid_full[0]
+        context, grad_q, grad_k, grad_v = attention_grads(q_saved, k_saved, v_saved, mid_rows, w_proj)
+        n_heads, head_dim = q_saved.shape[2:]
+        width = n_heads * head_dim
+        d_model = mid_rows.shape[-1]
+        grad_wproj = jnp.einsum('se,sd->ed', context, mid_rows, preferred_element_type=jnp.float32).reshape(n_heads, head_dim, d_model)
+        qkv_grads = jnp.concatenate([grad_q, grad_k, grad_v], axis=1)
+        wqkv_rows = jnp.moveaxis(w_qkv.reshape(3, d_model, width), 1, 2).reshape(3 * width, d_model)
+        grad_wqkv = jnp.einsum('sd,sie->ide', h1_full[0], qkv_grads.reshape(-1, 3, width), preferred_element_type=jnp.float32).reshape(3, d_model, n_heads, head_dim)
+        grad_bqkv = jnp.sum(qkv_grads, axis=0, dtype=jnp.float32).reshape(3, n_heads, head_dim)
+        h1_partial = jnp.dot(qkv_grads, wqkv_rows, preferred_element_type=jnp.float32).astype(jnp.bfloat16)[None]
         grad_h1 = lax.psum_scatter(h1_partial, 'tp', scatter_dimension=1, tiled=True).astype(jnp.float32)
         grad_x = (grad_mid.astype(jnp.float32) + layer_norm_bwd(grad_h1, norm1_hat, norm1_rstd, ln1_gain)).astype(jnp.bfloat16)
         vec_partial = jnp.stack([

time: 794 us -> 684 us (0.86)
  matrix products: 455 us -> 171 us
  Pallas kernels: 0 us -> 111 us
  local copies, waits for them, and re-layouts: 5.7 us -> 39.4 us
  waiting for transfers between devices: 280 us -> 303 us
  starting transfers between devices: 0.79 us -> 12.8 us
    dot_general x8 -> x3, matrix products: 296 us -> 49.6 us  [the longest x1 21 us: local_backward(): jnp.einsum('sd,sie->ide', h1_full[0], qkv_grads.reshape(-1, 3, width), pr...]
    pallas_call x0 -> x1, Pallas kernels: none -> 111 us  [attention_grads(): pl.pallas_call(functools.partial(attention_kernel, head_dim), grid=(n_blk...]
    sub x1 -> x0, matrix products: 37.1 us -> none  [attention_grads(): attn_probs = jax.nn.softmax(scores, axis=-1)]
    all_gather x1, waiting for transfers between devices: 3.45 us -> 34.1 us  [local_backward(): h1_full = lax.all_gather(h1_local, 'tp', axis=1, tiled=True)]
    all_gather x1, waiting for transfers between devices: 22.7 us -> 44.8 us  [local_backward(): mid_full = lax.all_gather(grad_mid, 'tp', axis=1, tiled=True)]
    all_gather x1, waiting for transfers between devices: 23.6 us -> 2.97 us  [local_backward(): h2_full = lax.all_gather(h2_local, 'tp', axis=1, tiled=True)]
    unnamed x45 -> x38, local copies, waits for them, and re-layouts: 4.95 us -> 20.5 us
    all_gather x1, starting transfers between devices: 0.41 us -> 12 us  [local_backward(): mid_full = lax.all_gather(grad_mid, 'tp', axis=1, tiled=True)]
  transfers between devices with their start and end apart: 7 -> 7, of which waited for: 7 -> 7; matrix products, arithmetic and copies ran while one was open for 22% -> 20% of each run, Pallas kernels for 0% -> 0%
where the time goes in v1:
time: 684 us; the launch traced here: 673 us
  waiting for transfers between devices  303 us (44%)
  matrix products  171 us (25%)
  Pallas kernels  111 us (16%)
  local copies, waits for them, and re-layouts  39.4 us (6%)
  other arithmetic  20.8 us (3%)
  between operations  14.5 us (2%)
  starting transfers between devices  12.8 us (2%)
    pallas_call x1, Pallas kernels, attention_grads(): pl.pallas_call(functools.partial(attention_kernel, head_dim), grid=(n_blk...  111 us
    all_gather x1, waiting for transfers between devices, local_backward(): dout_full = lax.all_gather(d_out, 'tp', axis=1, tiled=True)  68.1 us
    reduce_scatter x1, waiting for transfers between devices, local_backward(): lax.psum_scatter(h1_partial, 'tp', scatter_dimension=1, tiled=True)  65.8 us
    reduce_scatter x1, waiting for transfers between devices, local_backward(): lax.psum_scatter(h2_partial, 'tp', scatter_dimension=1, tiled=True)  55.1 us
    all_gather x1, waiting for transfers between devices, local_backward(): mid_full = lax.all_gather(grad_mid, 'tp', axis=1, tiled=True)  44.8 us
    dot_general x1, matrix products, local_backward(): jnp.einsum('bsf,bsd->fd', act_value.astype(jnp.bfloat16), dout_full, pref...  35.9 us
    all_gather x1, waiting for transfers between devices, local_backward(): h1_full = lax.all_gather(h1_local, 'tp', axis=1, tiled=True)  34.1 us
    dot_general x1, matrix products, local_backward(): jnp.einsum('bsd,fd->bsf', dout_full, w_fc2, preferred_element_type=jnp.fl...  33.5 us
  transfers between devices with their start and end apart: 7, of which 7 were waited for; matrix products, arithmetic and copies ran while one was open for 20% of the time, Pallas kernels for 0%

profile of v1, /device:TPU:113, one launch (start us, length us, event | category | flops | bytes accessed | tf_op | source)
XLA Modules:
  0.0 673.0 jit_solution(406225637716332043)
XLA Ops:
  7.2 0.1 all-gather.5.cloned.1.call-start
  7.2 0.7 all-gather.5.cloned.1.call-update
  8.0 0.1 reduce-scatter.3.cloned.1.call-start
  8.0 68.1 %all-gather.5.cloned.1.call-done = bf16[1,2048,3072]{2,1,0:T(8,128)(2,1)} async-done(((bf16[1,256,3072]{2,1,0:T(8,128)(2,1)}), bf16[1,2048,3072]{2,1,0:T(8,128)(2,1)}) %all-gather.5.cloned.1.call-update) | async-done | bytes 12582928 | tf_op jit(solution)/shard_map/all_gather | solution.py:170
  76.2 33.5 %convert_reduce_fusion = (f32[1536]{0:T(1024)}, bf16[1,2048,1536]{2,1,0:T(8,128)(2,1)S(1)}) fusion(bf16[1,2048,1536]{2,1,0:T(8,128)(2,1)} %param.21, bf16[1536,3072]{1,0:T(8,128)(2,1)} %param.29, bf16[1,2048,3072]{2,1,0:T(8,128)(2,1)} %all-gather.5.cloned.1.call-done), kind=kOutput, calls=%fused_computation.28 | convolution fusion | flops 19396556800 | bytes 34609152 | tf_op jit(solution)/shard_map/bsd,fd->bsf/dot_general | solution.py:173
  109.6 2.6 copy-done.13
  112.2 25.3 %convert_bitcast_fusion.1 = bf16[1,2048,3072]{2,1,0:T(8,128)(2,1)} fusion(bf16[3072,1536]{1,0:T(8,128)(2,1)} %param.28, bf16[1,2048,1536]{2,1,0:T(8,128)(2,1)S(1)} %get-tuple-element.30), kind=kOutput, calls=%fused_computation.30 | convolution fusion | flops 19333644288 | bytes 28311552 | tf_op jit(solution)/shard_map/bsf,df->bsd/dot_general | solution.py:176
  137.5 0.1 reduce-scatter.3.cloned.1.call-update
  137.5 0.0 copy-start.4
  137.6 12.0 %all-gather.7.cloned.1.call-start = ((), (), s32[]{:S(2)}) async-start(), calls=%async_computation.4 | async-start | bytes 14155776 | tf_op jit(solution)/shard_map/all_gather | solution.py:179
  149.6 0.3 convert_reduce_fusion.6
  149.9 0.6 fusion.54
  150.5 55.1 %reduce-scatter.3.cloned.1.call-done = bf16[1,256,3072]{2,1,0:T(8,128)(2,1)} async-done(((bf16[1,2048,3072]{2,1,0:T(8,128)(2,1)}), bf16[1,256,3072]{2,1,0:T(8,128)(2,1)}) %reduce-scatter.3.cloned.1.call-update) | async-done | bytes 1572880 | tf_op jit(solution)/shard_map/reduce_scatter | solution.py:177
  205.6 0.0 copy-done.11
  205.6 4.4 fusion.59
  210.0 0.0 copy-done.4
  210.1 3.0 convert_reduce_fusion.5
  213.1 0.1 all-gather.7.cloned.1.call-update
  213.1 0.1 reduce-scatter.5.cloned.1.call-start
  213.2 3.7 copy.28
  216.9 2.9 copy.29
  219.8 3.3 pad.14.q_ref
  223.2 1.7 pad.15.k_ref
  224.9 2.9 copy.30
  227.8 0.0 copy-start.6
  227.8 1.7 pad.16.v_ref
  229.6 0.6 copy-done.6
  230.2 2.1 pad.17
  232.2 44.8 %all-gather.7.cloned.1.call-done = bf16[1,2048,3072]{2,1,0:T(8,128)(2,1)} async-done(((bf16[1,256,3072]{2,1,0:T(8,128)(2,1)}), bf16[1,2048,3072]{2,1,0:T(8,128)(2,1)}) %all-gather.7.cloned.1.call-update) | async-done | bytes 12582928 | tf_op jit(solution)/shard_map/all_gather | solution.py:179
  277.1 111.2 %attention_grads.1 = (bf16[2048,384]{1,0:T(8,128)(2,1)}, bf16[2048,384]{1,0:T(8,128)(2,1)}, bf16[2048,384]{1,0:T(8,128)(2,1)}, bf16[2048,384]{1,0:T(8,128)(2,1)}) custom-call(bf16[4,2048,128]{2,1,0:T(8,128)(2,1)} %pad.14.q_ref, bf16[4,2048,128]{2,1,0:T(8,128)(2,1)} %pad.15.k_ref, bf16[4,2048,128]{2,1,0:T(8,128)(2,1)} %pad.16.v_ref, ...), custom_call_target="tpu_custom_call" | custom-call | flops 19327352832 | bytes 41943040 | tf_op jit(solution)/shard_map/attention_grads/pallas_call | solution.py:147
  388.3 1.7 constant_dynamic-update-slice_fusion.2
  390.0 1.7 constant_dynamic-update-slice_fusion.1
  391.7 0.3 constant_dynamic-update-slice_fusion
  392.0 0.0 copy-start
  392.1 2.2 copy-done
  394.2 18.7 %convert_bitcast_fusion = bf16[1,2048,3072]{2,1,0:T(8,128)(2,1)} fusion(bf16[2048,1152]{1,0:T(8,128)(2,1)S(1)} %constant_dynamic-update-slice_fusion, bf16[1152,3072]{1,0:T(8,128)(2,1)S(1)} %bitcast.83), kind=kOutput, calls=%fused_computation.29 | convolution fusion | flops 14501806080 | bytes 24379392 | tf_op jit(solution)/shard_map/dot_general | solution.py:192
  412.9 0.1 reduce-scatter.5.cloned.1.call-update
  413.0 0.0 copy-start.10
  413.0 0.0 copy-start.12
  413.0 0.1 all-gather.11.cloned.1.call-start
  413.1 0.6 all-gather.11.cloned.1.call-update
  413.7 0.1 all-gather.9.cloned.1.call-start
  413.8 0.6 copy-done.2
  414.4 0.3 convert_reduce_fusion.4
  414.6 0.6 fusion.49
  415.2 65.8 %reduce-scatter.5.cloned.1.call-done = bf16[1,256,3072]{2,1,0:T(8,128)(2,1)} async-done(((bf16[1,2048,3072]{2,1,0:T(8,128)(2,1)}), bf16[1,256,3072]{2,1,0:T(8,128)(2,1)}) %reduce-scatter.5.cloned.1.call-update) | async-done | bytes 1572880 | tf_op jit(solution)/shard_map/reduce_scatter | solution.py:193
  481.1 4.3 fusion.60
  485.4 0.1 all-gather.9.cloned.1.call-update
  485.4 0.5 all-reduce.6.cloned.1.call-start
  485.9 35.9 %fusion.17 = f32[1536,3072]{1,0:T(8,128)} fusion(bf16[1,2048,3072]{2,1,0:T(8,128)(2,1)} %all-gather.5.cloned.1.call-done, bf16[1,2048,1536]{2,1,0:T(8,128)(2,1)} %param.21), kind=kOutput, calls=%fused_computation.24 | convolution fusion | flops 19358810112 | bytes 37748736 | tf_op jit(solution)/shard_map/bsf,bsd->fd/dot_general | solution.py:172
  521.8 6.7 copy.31
  528.5 3.2 convert_reduce_fusion.1
  531.7 0.7 reshape.152
  532.4 1.6 copy.32
  534.0 9.9 %fusion.13 = f32[4,96,3072]{2,1,0:T(8,128)} fusion(bf16[4,96,2048]{2,1,0:T(8,128)(2,1)} %bitcast.73, bf16[1,2048,3072]{2,1,0:T(8,128)(2,1)} %all-gather.7.cloned.1.call-done), kind=kOutput, calls=%fused_computation.20 | convolution fusion | flops 4831838208 | bytes 18874368 | tf_op jit(solution)/shard_map/se,sd->ed/dot_general | solution.py:187
  543.9 3.0 all-gather.11.cloned.1.call-done
  546.9 26.5 %fusion.11 = f32[3072,1536]{1,0:T(8,128)} fusion(bf16[1,2048,3072]{2,1,0:T(8,128)(2,1)} %all-gather.11.cloned.1.call-done, bf16[1,2048,1536]{2,1,0:T(8,128)(2,1)} %copy-done.13), kind=kOutput, calls=%fused_computation.18 | convolution fusion | flops 19327352832 | bytes 37748736 | tf_op jit(solution)/shard_map/bsd,bsf->df/dot_general | solution.py:174
  573.4 0.7 stack.27
  574.1 0.1 all-reduce.6.cloned.1.call-update
  574.2 4.2 fusion.56
  578.4 34.1 %all-gather.9.cloned.1.call-done = bf16[1,2048,3072]{2,1,0:T(8,128)(2,1)} async-done(((bf16[1,256,3072]{2,1,0:T(8,128)(2,1)}), bf16[1,2048,3072]{2,1,0:T(8,128)(2,1)}) %all-gather.9.cloned.1.call-update) | async-done | bytes 12582928 | tf_op jit(solution)/shard_map/all_gather | solution.py:181
  612.5 21.0 %fusion.15 = f32[3,384,3072]{2,1,0:T(8,128)} fusion(bf16[2048,3,384]{0,2,1:T(8,128)(2,1)} %bitcast.70, bf16[1,2048,3072]{2,1,0:T(8,128)(2,1)} %all-gather.9.cloned.1.call-done), kind=kOutput, calls=%fused_computation.22 | convolution fusion | flops 14495514624 | bytes 31457280 | tf_op jit(solution)/shard_map/sd,sie->ide/dot_general | solution.py:190
  633.6 30.9 %all-reduce.6.cloned.1.call-done = f32[6,3072]{1,0:T(8,128)} async-done(((f32[6,3072]{1,0:T(8,128)}), f32[6,3072]{1,0:T(8,128)}) %all-reduce.6.cloned.1.call-update) | async-done | bytes 73744 | tf_op jit(solution)/shard_map/psum | solution.py:203
  664.4 1.5 copy.36
  (29 shorter events, 0.1 us)
Async XLA Ops:
  7.2 69.0 %all-gather.5.cloned.1.call-start = ((), (), s32[]{:S(2)}) async-start(), calls=%async_computation.2 | async-start | bytes 14155776 | tf_op jit(solution)/shard_map/all_gather | solution.py:170
  8.0 197.6 %reduce-scatter.3.cloned.1.call-start = ((), (), s32[]{:S(2)}) async-start(), calls=%async_computation.3 | async-start | bytes 14155776 | tf_op jit(solution)/shard_map/reduce_scatter | solution.py:177
  109.6 2.6 copy-start.13
  137.5 12.1 %copy-start.1 = (bf16[1,256,3072]{2,1,0:T(8,128)(2,1)S(1)}, bf16[1,256,3072]{2,1,0:T(8,128)(2,1)}, u32[]{:S(2)}) copy-start(bf16[1,256,3072]{2,1,0:T(8,128)(2,1)} %param.16) | copy-start | bytes 4718596
  137.5 68.1 %copy-start.9 = (f32[3072]{0:T(1024)S(1)}, f32[3072]{0:T(1024)}, u32[]{:S(2)}) copy-start(f32[3072]{0:T(1024)} %param.24) | copy-start | bytes 36868
  137.5 68.1 %copy-start.11 = (f32[3072]{0:T(1024)S(1)}, f32[3072]{0:T(1024)}, u32[]{:S(2)}) copy-start(f32[3072]{0:T(1024)} %param.25) | copy-start | bytes 36868
  137.5 72.5 %copy-start.4 = (bf16[1,256,3072]{2,1,0:T(8,128)(2,1)S(1)}, bf16[1,256,3072]{2,1,0:T(8,128)(2,1)}, u32[]{:S(2)}) copy-start(bf16[1,256,3072]{2,1,0:T(8,128)(2,1)} %param.17) | copy-start | bytes 4718596
  137.6 139.5 %all-gather.7.cloned.1.call-start = ((), (), s32[]{:S(2)}) async-start(), calls=%async_computation.4 | async-start | bytes 14155776 | tf_op jit(solution)/shard_map/all_gather | solution.py:179
  205.6 4.5 copy-start.5
  213.1 267.9 %reduce-scatter.5.cloned.1.call-start = ((), (), s32[]{:S(2)}) async-start(), calls=%async_computation.5 | async-start | bytes 14155776 | tf_op jit(solution)/shard_map/reduce_scatter | solution.py:193
  227.8 2.4 copy-start.6
  230.2 164.1 %slice-start = ((s8[7077888]{0:T(1024)(128)(4,1)}), s8[2883584]{0:T(1024)(128)(4,1)S(1)}, s32[]{:S(2)}) async-start(s8[7077888]{0:T(1024)(128)(4,1)} %bitcast.81), calls=%async_computation.9 | async-start | bytes 5767168
  277.1 117.2 %slice-start.1 = ((s8[7077888]{0:T(1024)(128)(4,1)}), s8[4194304]{0:T(1024)(128)(4,1)S(1)}, s32[]{:S(2)}) async-start(s8[7077888]{0:T(1024)(128)(4,1)} %bitcast.81), calls=%async_computation.10 | async-start | bytes 8388608
  388.3 3.4 copy-start.8
  392.0 2.2 copy-start
  412.9 1.4 copy-start.2
  413.0 68.0 %copy-start.10 = (f32[3072]{0:T(1024)S(1)}, f32[3072]{0:T(1024)}, u32[]{:S(2)}) copy-start(f32[3072]{0:T(1024)} %param.22) | copy-start | bytes 36868
  413.0 68.0 %copy-start.12 = (f32[3072]{0:T(1024)S(1)}, f32[3072]{0:T(1024)}, u32[]{:S(2)}) copy-start(f32[3072]{0:T(1024)} %param.23) | copy-start | bytes 36868
  413.0 133.8 %all-gather.11.cloned.1.call-start = ((), (), s32[]{:S(2)}) async-start(), calls=%async_computation.7 | async-start | bytes 14155776 | tf_op jit(solution)/shard_map/all_gather | solution.py:169
  413.7 198.9 %all-gather.9.cloned.1.call-start = ((), (), s32[]{:S(2)}) async-start(), calls=%async_computation.6 | async-start | bytes 14155776 | tf_op jit(solution)/shard_map/all_gather | solution.py:181
  485.4 179.0 %all-reduce.6.cloned.1.call-start = ((), (), s32[]{:S(2)}) async-start(), calls=%async_computation.8 | async-start | bytes 196608 | tf_op jit(solution)/shard_map/psum | solution.py:203
  528.5 3.8 copy-start.7
  543.9 30.3 %copy-start.3 = (bf16[1,256,3072]{2,1,0:T(8,128)(2,1)S(1)}, bf16[1,256,3072]{2,1,0:T(8,128)(2,1)}, u32[]{:S(2)}) copy-start(bf16[1,256,3072]{2,1,0:T(8,128)(2,1)} %get-tuple-element.25) | copy-start | bytes 4718596
Sparse Core Ops, SparseCore 0:
  9.6 66.5 all-gather.4
  137.7 67.8 reduce-scatter.2
  213.2 63.7 all-gather.6
  413.1 67.8 reduce-scatter.4
  483.1 63.7 all-gather.10
  548.9 63.6 all-gather.8
  615.5 48.9 all-reduce.5

commit v2 on v1

--- a/solution.py
+++ b/solution.py
@@ -163,19 +163,460 @@
     )(qp, kp, vp, mid_rows, wo)
 
 
+MESH_IDS = pl.DeviceIdType.MESH
+ANY = pl.BlockSpec(memory_space=pl.ANY)
+
+
+class Ring:
+    def __init__(self, axis_name, size):
+        me = lax.axis_index(axis_name)
+        self.axis_name, self.size, self.me = axis_name, size, me
+        self.core = me % 2
+        self.chip = me // 2
+        self.partner = 2 * self.chip + 1 - self.core
+        self.right = (me + 2) % size
+        self.left = (me + size - 2) % size
+
+    def barrier(self):
+        sem = pltpu.get_barrier_semaphore()
+        for peer in (self.left, self.right, self.partner):
+            pl.semaphore_signal(sem, inc=1, device_id={self.axis_name: peer}, device_id_type=MESH_IDS)
+        pl.semaphore_wait(sem, 3)
+
+    def copy(self, src, dst, send_sem, recv_sem, peer):
+        return pltpu.make_async_remote_copy(src_ref=src, dst_ref=dst, send_sem=send_sem, recv_sem=recv_sem,
+                                            device_id={self.axis_name: peer}, device_id_type=MESH_IDS)
+
+    def block_owner(self, rel):
+        n_chips = self.size // 2
+        shift = (0, n_chips - 1, 1, 2)[rel // 2]
+        chip = (self.chip + shift) % n_chips
+        core = self.core if rel % 2 == 0 else 1 - self.core
+        return 2 * chip + core
+
+
+OWN, PARTNER, LEFT, RIGHT, OPP = 0, 1, 2, 4, 6
+
+
+class Gather:
+    N_COPIES = 13
+
+    def __init__(self, ring, src, dst, send_sem, recv_sem):
+        self.ring, self.src, self.dst, self.send_sem, self.recv_sem = ring, src, dst, send_sem, recv_sem
+        self.rows = src.shape[0]
+        self.half = self.rows // 2
+
+    def piece(self, rel, half):
+        return self.dst.at[pl.ds(rel * self.rows + half * self.half, self.half)]
+
+    def own_piece(self, half):
+        return self.src.at[pl.ds(half * self.half, self.half)]
+
+    def block(self, rel):
+        return self.dst.at[pl.ds(rel * self.rows, self.rows)]
+
+    def descriptor(self, idx):
+        r = self.ring
+        if idx == 0:
+            src, dst, peer = self.src, self.block(PARTNER), r.partner
+        elif idx <= 4:
+            rel, half, peer = ((LEFT, 0, r.right), (LEFT, 1, r.right), (RIGHT, 1, r.left), (RIGHT, 0, r.left))[idx - 1]
+            src, dst = self.own_piece(half), self.piece(rel, half)
+        elif idx == 5:
+            src, dst, peer = self.piece(LEFT, 0), self.piece(OPP, 0), r.right
+        elif idx == 6:
+            src, dst, peer = self.piece(RIGHT, 1), self.piece(OPP, 1), r.left
+        else:
+            rel, half = ((LEFT, 0), (RIGHT, 1), (LEFT, 1), (RIGHT, 0), (OPP, 0), (OPP, 1))[idx - 7]
+            src, dst, peer = self.piece(rel, half), self.piece(rel + 1, half), r.partner
+        return r.copy(src, dst, self.send_sem.at[idx], self.recv_sem.at[idx], peer)
+
+    def send(self, *ids):
+        for idx in ids:
+            self.descriptor(idx).start()
+
+    def recv(self, *ids):
+        for idx in ids:
+            self.descriptor(idx).wait_recv()
+
+    def start(self):
+        self.send(1, 3, 0, 2, 4)
+
+    def first_halves(self):
+        self.recv(1, 3)
+        self.send(5, 6, 7, 8)
+
+    def second_halves(self):
+        self.recv(2, 4)
+        self.send(9, 10)
+
+    def opposite(self):
+        self.recv(5, 6)
+        self.send(11, 12)
+
+    def drain(self):
+        for idx in range(self.N_COPIES):
+            self.descriptor(idx).wait_send()
+
+
+class Scatter:
+    N_COPIES = 14
+
+    def __init__(self, ring, partial, peer_part, outbox, inbox, send_sem, recv_sem):
+        self.ring, self.partial, self.peer_part, self.outbox, self.inbox = ring, partial, peer_part, outbox, inbox
+        self.send_sem, self.recv_sem = send_sem, recv_sem
+        self.rows = partial.shape[0] // ring.size
+        self.half = self.rows // 2
+
+    def piece(self, rel, half):
+        return pl.ds(rel * self.rows + half * self.half, self.half)
+
+    def swap(self, rel):
+        idx = 6 + rel // 2
+        rows = pl.ds((rel + 1) * self.rows, self.rows)
+        return self.ring.copy(self.partial.at[rows], self.peer_part.at[pl.ds(rel // 2 * self.rows, self.rows)],
+                              self.send_sem.at[idx], self.recv_sem.at[idx], self.ring.partner)
+
+    def hop(self, idx):
+        peer = self.ring.right if idx % 2 == 0 else self.ring.left
+        return self.ring.copy(self.outbox.at[idx], self.inbox.at[idx], self.send_sem.at[idx], self.recv_sem.at[idx], peer)
+
+    def chip_sum(self, rel, half):
+        mine = self.partial[self.piece(rel, half), :].astype(jnp.float32)
+        other = self.peer_part[pl.ds(rel // 2 * self.rows + half * self.half, self.half), :].astype(jnp.float32)
+        return mine + other
+
+    def put(self, idx, value):
+        self.outbox[idx] = value.astype(jnp.bfloat16)
+        self.hop(idx).start()
+
+    def send_opposite(self):
+        self.swap(OPP).wait_recv()
+        self.put(0, self.chip_sum(OPP, 0))
+        self.put(1, self.chip_sum(OPP, 1))
+
+    def send_direct(self):
+        self.swap(LEFT).wait_recv()
+        self.swap(RIGHT).wait_recv()
+        self.put(2, self.chip_sum(RIGHT, 1))
+        self.put(3, self.chip_sum(LEFT, 0))
+
+    def send_relayed(self):
+        self.hop(0).wait_recv()
+        self.put(4, self.chip_sum(RIGHT, 0) + self.inbox[0].astype(jnp.float32))
+        self.hop(1).wait_recv()
+        self.put(5, self.chip_sum(LEFT, 1) + self.inbox[1].astype(jnp.float32))
+
+    def arrive(self):
+        self.swap(OWN).wait_recv()
+        for idx in (2, 3, 4, 5):
+            self.hop(idx).wait_recv()
+
+    def own_sum(self, half, rows, sl):
+        idx_l, idx_r = ((4, 3), (2, 5))[half]
+        total = self.partial[sl, :].astype(jnp.float32) + self.peer_part[sl, :].astype(jnp.float32)
+        return total + self.inbox[idx_l, rows, :].astype(jnp.float32) + self.inbox[idx_r, rows, :].astype(jnp.float32)
+
+    def drain(self):
+        for idx in range(6):
+            self.hop(idx).wait_send()
+        for rel in (OWN, LEFT, RIGHT, OPP):
+            self.swap(rel).wait_send()
+
+
+def gather_mlp_kernel(axis_name, size, dout_ref, z_ref, w2_ref, xmid_ref, gain_ref, bias_ref,
+                      dz_hbm, h2_hbm, dw2_hbm,
+                      dout_all, zu, dz, w2, xmid, h2, dw2_tile, local_sem, send_sem, recv_sem, h2_send_sem, h2_recv_sem, out_sem):
+    ring = Ring(axis_name, size)
+    rows = dout_ref.shape[0]
+    units = w2.shape[0]
+    ring.barrier()
+    gather = Gather(ring, dout_ref, dout_all, send_sem, recv_sem)
+    gather.start()
+    own_copy = pltpu.make_async_copy(dout_ref, gather.block(OWN), local_sem.at[0])
+    w2_copy = pltpu.make_async_copy(w2_ref, w2, local_sem.at[1])
+    xmid_copy = pltpu.make_async_copy(xmid_ref, xmid, local_sem.at[2])
+    own_copy.start()
+    z_copies = []
+    for rel in range(size):
+        src = z_ref.at[pl.ds(pl.multiple_of(ring.block_owner(rel) * rows, rows), rows)]
+        z_copies.append(pltpu.make_async_copy(src, zu.at[pl.ds(rel * rows, rows)], local_sem.at[4 + rel]))
+    xmid_copy.start()
+    w2_copy.start()
+    for copy in z_copies:
+        copy.start()
+
+    xmid_copy.wait()
+    chunk = 32
+
+    def norm_rows(i, c):
+        sl = pl.ds(pl.multiple_of(i * chunk, chunk), chunk)
+        _, _, normed = layer_norm_fwd(xmid[sl, :], gain_ref[...], bias_ref[...])
+        h2[sl, :] = normed
+        return c
+
+    lax.fori_loop(0, rows // chunk, norm_rows, 0)
+    h2_gather = Gather(ring, h2, h2_hbm, h2_send_sem, h2_recv_sem)
+    h2_own = pltpu.make_async_copy(h2, h2_gather.block(OWN), local_sem.at[3])
+    h2_own.start()
+
+    pair, tile = 2 * rows, 256
+
+    def mlp_pair(rel):
+        base = rel * rows
+        z_copies[rel].wait()
+        z_copies[rel + 1].wait()
+
+        def body(n, c):
+            cols = pl.ds(pl.multiple_of(n * tile, tile), tile)
+            act_value, act_slope = gelu_parts(zu[pl.ds(base, pair), cols].astype(jnp.float32))
+            zu[pl.ds(base, pair), cols] = act_value.astype(jnp.bfloat16)
+            grad_act = dot(dout_all[pl.ds(base, pair), :], w2[cols, :], NT)
+            dz[pl.ds(base, pair), cols] = (grad_act * act_slope).astype(jnp.bfloat16)
+            return c
+
+        lax.fori_loop(0, units // tile, body, 0)
+        copy = pltpu.make_async_copy(dz.at[pl.ds(base, pair)], dz_hbm.at[pl.ds(base, pair)], out_sem.at[rel // 2])
+        copy.start()
+        return copy
+
+    own_copy.wait()
+    w2_copy.wait()
+    gather.recv(0)
+    dz_copies = [mlp_pair(OWN)]
+    gather.first_halves()
+    gather.second_halves()
+    h2_gather.start()
+    gather.recv(7, 8, 9, 10)
+    dz_copies.append(mlp_pair(LEFT))
+    dz_copies.append(mlp_pair(RIGHT))
+    gather.opposite()
+    gather.recv(11, 12)
+    dz_copies.append(mlp_pair(OPP))
+
+    n_tiles = units // tile
+
+    def dw2_copy(i, slot):
+        return pltpu.make_async_copy(dw2_tile.at[slot], dw2_hbm.at[pl.ds(pl.multiple_of(i * tile, tile), tile)], out_sem.at[4 + slot])
+
+    def dw2_body(i, c):
+        slot = i % 2
+
+        @pl.when(i >= 2)
+        def _():
+            dw2_copy(i - 2, slot).wait()
+
+        @pl.when(i == n_tiles // 2)
+        def _():
+            h2_gather.first_halves()
+
+        dw2_tile[slot] = dot(zu[:, pl.ds(pl.multiple_of(i * tile, tile), tile)], dout_all[...], TN)
+        dw2_copy(i, slot).start()
+        return c
+
+    lax.fori_loop(0, n_tiles, dw2_body, 0)
+    h2_gather.second_halves()
+    h2_own.wait()
+    for copy in dz_copies:
+        copy.wait()
+    for i in (n_tiles - 2, n_tiles - 1):
+        dw2_copy(i, i % 2).wait()
+    h2_gather.opposite()
+    h2_gather.recv(0, 7, 8, 9, 10, 11, 12)
+    gather.drain()
+    h2_gather.drain()
+
+
+def gather_mlp(axis_name, size, d_out, z_rows, w_fc2, x_mid, gain, bias, collective_id):
+    rows, d_model = d_out.shape
+    seq, units = z_rows.shape
+    bf, f32, dma = jnp.bfloat16, jnp.float32, pltpu.SemaphoreType.DMA
+    vm = pl.BlockSpec(memory_space=pltpu.VMEM)
+    return pl.pallas_call(
+        functools.partial(gather_mlp_kernel, axis_name, size),
+        in_specs=[ANY] * 4 + [vm, vm],
+        out_specs=[ANY] * 3,
+        out_shape=[jax.ShapeDtypeStruct((seq, units), bf), jax.ShapeDtypeStruct((seq, d_model), bf),
+                   jax.ShapeDtypeStruct((units, d_model), f32)],
+        scratch_shapes=[pltpu.VMEM((seq, d_model), bf), pltpu.VMEM((seq, units), bf), pltpu.VMEM((seq, units), bf),
+                        pltpu.VMEM((units, d_model), bf), pltpu.VMEM((rows, d_model), bf), pltpu.VMEM((rows, d_model), bf),
+                        pltpu.VMEM((2, 256, d_model), f32), dma((4 + size,)),
+                        dma((Gather.N_COPIES,)), dma((Gather.N_COPIES,)), dma((Gather.N_COPIES,)), dma((Gather.N_COPIES,)), dma((6,))],
+        compiler_params=pltpu.CompilerParams(collective_id=collective_id, has_side_effects=True, vmem_limit_bytes=60 * 2 ** 20),
+        cost_estimate=pl.CostEstimate(flops=4 * seq * units * d_model, bytes_accessed=60 * 2 ** 20, transcendentals=seq * units),
+        name="gather_mlp",
+    )(d_out, z_rows, w_fc2, x_mid, gain.reshape(1, -1), bias.reshape(1, -1))
+
+
+def scatter_grads(ring, stage_fn, partial, peer_part, outbox, inbox, send_sem, recv_sem):
+    scatter = Scatter(ring, partial, peer_part, outbox, inbox, send_sem, recv_sem)
+    stage_fn(OPP)
+    scatter.swap(OPP).start()
+    scatter.send_opposite()
+    stage_fn(LEFT)
+    scatter.swap(LEFT).start()
+    stage_fn(RIGHT)
+    scatter.swap(RIGHT).start()
+    scatter.send_direct()
+    stage_fn(OWN)
+    scatter.swap(OWN).start()
+    scatter.send_relayed()
+    return scatter
+
+
+def norm_backward(scatter, rows, x_rows, resid, gain, out, sums):
+    chunk = 16
+    half = rows // 2
+    sums[...] = jnp.zeros_like(sums)
+
+    def fold(vals):
+        total = vals[:8]
+        for i in range(1, chunk // 8):
+            total = total + vals[i * 8:(i + 1) * 8]
+        return total
+
+    for part in range(2):
+        def body(i, c):
+            inner = pl.ds(pl.multiple_of(i * chunk, chunk), chunk)
+            sl = pl.ds(pl.multiple_of(part * half + i * chunk, chunk), chunk)
+            grad_norm = scatter.own_sum(part, inner, sl)
+            x_hat, inv_std = norm_hat(x_rows[sl, :])
+            resid_f32 = resid[sl, :].astype(jnp.float32)
+            result = (resid_f32 + layer_norm_bwd(grad_norm, x_hat, inv_std, gain[...])).astype(jnp.bfloat16)
+            out[sl, :] = result
+            sums[0] += fold(grad_norm * x_hat)
+            sums[1] += fold(grad_norm)
+            sums[2] += fold(result.astype(jnp.float32))
+            sums[3] += fold(resid_f32)
+            return c
+
+        lax.fori_loop(0, half // chunk, body, 0)
+
+
+def norm_hat(token_rows):
+    rows_f32 = token_rows.astype(jnp.float32)
+    centered = rows_f32 - jnp.mean(rows_f32, axis=-1, keepdims=True)
+    inv_std = lax.rsqrt(jnp.mean(centered * centered, axis=-1, keepdims=True) + LN_EPS)
+    return centered * inv_std, inv_std
+
+
+def scatter_mlp_kernel(axis_name, size, dz_ref, w1_ref, h2_ref, xmid_ref, dout_ref, gain_ref,
+                       dmid_ref, sums_ref, dbfc1_ref, dw1_hbm,
+                       dz, w1, h2_tile, dw1_tile, xmid, dout, partial, peer_part, outbox, inbox,
+                       local_sem, send_sem, recv_sem, tile_sem):
+    ring = Ring(axis_name, size)
+    rows = xmid.shape[0]
+    d_model, units = w1.shape
+    pair, tile = 2 * rows, 256
+    ring.barrier()
+    dz_copies = {}
+    for rel in (OPP, LEFT, RIGHT, OWN):
+        sl = pl.ds(rel * rows, pair)
+        dz_copies[rel] = pltpu.make_async_copy(dz_ref.at[sl], dz.at[sl], local_sem.at[rel // 2])
+    w1_copy = pltpu.make_async_copy(w1_ref, w1, local_sem.at[4])
+    xmid_copy = pltpu.make_async_copy(xmid_ref, xmid, local_sem.at[5])
+    dout_copy = pltpu.make_async_copy(dout_ref, dout, local_sem.at[6])
+    dz_copies[OPP].start()
+    w1_copy.start()
+    for rel in (LEFT, RIGHT, OWN):
+        dz_copies[rel].start()
+    xmid_copy.start()
+    dout_copy.start()
+    w1_copy.wait()
+
+    def stage(rel):
+        dz_copies[rel].wait()
+        sl = pl.ds(rel * rows, pair)
+
+        def body(n, c):
+            cols = pl.ds(pl.multiple_of(n * tile, tile), tile)
+            partial[sl, cols] = dot(dz[sl, :], w1[cols, :], NT).astype(jnp.bfloat16)
+            return c
+
+        lax.fori_loop(0, d_model // tile, body, 0)
+
+    scatter = scatter_grads(ring, stage, partial, peer_part, outbox, inbox, send_sem, recv_sem)
+
+    n_tiles = d_model // tile
+
+    def tile_in(i, slot):
+        return pltpu.make_async_copy(h2_ref.at[:, pl.ds(pl.multiple_of(i * tile, tile), tile)], h2_tile.at[slot], tile_sem.at[slot])
+
+    def tile_out(i, slot):
+        return pltpu.make_async_copy(dw1_tile.at[slot], dw1_hbm.at[pl.ds(pl.multiple_of(i * tile, tile), tile)], tile_sem.at[2 + slot])
+
+    tile_in(0, 0).start()
+
+    def dw1_body(i, c):
+        slot = i % 2
+
+        @pl.when(i + 1 < n_tiles)
+        def _():
+            tile_in(i + 1, 1 - slot).start()
+
+        @pl.when(i >= 2)
+        def _():
+            tile_out(i - 2, slot).wait()
+
+        tile_in(i, slot).wait()
+        dw1_tile[slot] = dot(h2_tile[slot], dz[...], TN)
+        tile_out(i, slot).start()
+        return c
+
+    lax.fori_loop(0, n_tiles, dw1_body, 0)
+    dbfc1_ref[...] = jnp.zeros_like(dbfc1_ref)
+
+    def bias_body(i, c):
+        vals = dz[pl.ds(pl.multiple_of(i * 64, 64), 64), :].astype(jnp.float32)
+        for j in range(8):
+            dbfc1_ref[...] += vals[j * 8:(j + 1) * 8]
+        return c
+
+    lax.fori_loop(0, dz.shape[0] // 64, bias_body, 0)
+    for i in (n_tiles - 2, n_tiles - 1):
+        tile_out(i, i % 2).wait()
+    xmid_copy.wait()
+    dout_copy.wait()
+    scatter.arrive()
+    norm_backward(scatter, rows, xmid, dout, gain_ref, dmid_ref, sums_ref)
+    scatter.drain()
+
+
+def scatter_scratch(size, rows, d_model):
+    bf = jnp.bfloat16
+    return [pltpu.VMEM((size * rows, d_model), bf), pltpu.VMEM((size // 2 * rows, d_model), bf),
+            pltpu.VMEM((6, rows // 2, d_model), bf), pltpu.VMEM((6, rows // 2, d_model), bf)]
+
+
+def scatter_mlp(axis_name, size, dz_rel, w_fc1, h2_rel, x_mid, d_out, gain, collective_id):
+    rows, d_model = d_out.shape
+    seq, units = dz_rel.shape
+    bf, f32, dma = jnp.bfloat16, jnp.float32, pltpu.SemaphoreType.DMA
+    vm = pl.BlockSpec(memory_space=pltpu.VMEM)
+    return pl.pallas_call(
+        functools.partial(scatter_mlp_kernel, axis_name, size),
+        in_specs=[ANY] * 5 + [vm],
+        out_specs=[vm, vm, vm, ANY],
+        out_shape=[jax.ShapeDtypeStruct((rows, d_model), bf), jax.ShapeDtypeStruct((4, 8, d_model), f32),
+                   jax.ShapeDtypeStruct((8, units), f32), jax.ShapeDtypeStruct((d_model, units), f32)],
+        scratch_shapes=[pltpu.VMEM((seq, units), bf), pltpu.VMEM((d_model, units), bf), pltpu.VMEM((2, seq, 256), bf),
+                        pltpu.VMEM((2, 256, units), f32), pltpu.VMEM((rows, d_model), bf), pltpu.VMEM((rows, d_model), bf)]
+        + scatter_scratch(size, rows, d_model)
+        + [dma((7,)), dma((Scatter.N_COPIES,)), dma((Scatter.N_COPIES,)), dma((4,))],
+        compiler_params=pltpu.CompilerParams(collective_id=collective_id, has_side_effects=True, vmem_limit_bytes=63 * 2 ** 20),
+        cost_estimate=pl.CostEstimate(flops=4 * seq * units * d_model, bytes_accessed=60 * 2 ** 20, transcendentals=0),
+        name="scatter_mlp",
+    )(dz_rel, w_fc1, h2_rel, x_mid, d_out, gain.reshape(1, -1))
+
+
 def solution(mesh):
     def local_backward(x_in, x_mid, d_out, q_saved, k_saved, v_saved, z_saved, ln1_gain, ln1_bias, ln2_gain, ln2_bias, w_qkv, w_proj, w_fc1, w_fc2):
-        norm2_hat, norm2_rstd, h2_local = layer_norm_fwd(x_mid, ln2_gain, ln2_bias)
-        h2_full = lax.all_gather(h2_local, 'tp', axis=1, tiled=True)
-        dout_full = lax.all_gather(d_out, 'tp', axis=1, tiled=True)
-        act_value, act_slope = gelu_parts(z_saved.astype(jnp.float32))
-        grad_wfc2 = jnp.einsum('bsf,bsd->fd', act_value.astype(jnp.bfloat16), dout_full, preferred_element_type=jnp.float32)
-        grad_pre = (jnp.einsum('bsd,fd->bsf', dout_full, w_fc2, preferred_element_type=jnp.float32) * act_slope).astype(jnp.bfloat16)
-        grad_wfc1 = jnp.einsum('bsd,bsf->df', h2_full, grad_pre, preferred_element_type=jnp.float32)
-        grad_bfc1 = jnp.sum(grad_pre, axis=(0, 1), dtype=jnp.float32)
-        h2_partial = jnp.einsum('bsf,df->bsd', grad_pre, w_fc1, preferred_element_type=jnp.float32).astype(jnp.bfloat16)
-        grad_h2 = lax.psum_scatter(h2_partial, 'tp', scatter_dimension=1, tiled=True).astype(jnp.float32)
-        grad_mid = (d_out.astype(jnp.float32) + layer_norm_bwd(grad_h2, norm2_hat, norm2_rstd, ln2_gain)).astype(jnp.bfloat16)
+        size = mesh.shape['tp']
+        dz_rel, h2_rel, grad_wfc2 = gather_mlp('tp', size, d_out[0], z_saved[0], w_fc2, x_mid[0], ln2_gain, ln2_bias, 0)
+        grad_mid, sums2, bias_sums, grad_wfc1 = scatter_mlp('tp', size, dz_rel, w_fc1, h2_rel, x_mid[0], d_out[0], ln2_gain, 1)
+        grad_mid = grad_mid[None]
+        sums2 = jnp.sum(sums2, axis=1)
+        grad_bfc1 = jnp.sum(bias_sums, axis=0)
         mid_full = lax.all_gather(grad_mid, 'tp', axis=1, tiled=True)
         norm1_hat, norm1_rstd, h1_local = layer_norm_fwd(x_in, ln1_gain, ln1_bias)
         h1_full = lax.all_gather(h1_local, 'tp', axis=1, tiled=True)
@@ -195,10 +636,7 @@
         vec_partial = jnp.stack([
             jnp.sum(grad_h1 * norm1_hat, axis=(0, 1)),
             jnp.sum(grad_h1, axis=(0, 1)),
-            jnp.sum(grad_h2 * norm2_hat, axis=(0, 1)),
-            jnp.sum(grad_h2, axis=(0, 1)),
-            jnp.sum(grad_mid, axis=(0, 1), dtype=jnp.float32),
-            jnp.sum(d_out, axis=(0, 1), dtype=jnp.float32),
+            sums2[0], sums2[1], sums2[2], sums2[3],
         ])
         grad_vecs = lax.psum(vec_partial, 'tp')
         return grad_x, grad_wqkv, grad_bqkv, grad_wproj, grad_wfc1, grad_bfc1, grad_wfc2, grad_vecs

time: 684 us -> 625 us (0.914); the launches traced: 673 us -> 622 us
  Pallas kernels: 111 us -> 301 us
  waiting for transfers between devices: 303 us -> 179 us
  matrix products: 171 us -> 49.7 us
  local copies, waits for them, and re-layouts: 39.4 us -> 64 us
  starting transfers between devices: 12.8 us -> 0.66 us
  other arithmetic: 20.8 us -> 13.8 us
    pallas_call x0 -> x2, Pallas kernels: none -> 189 us  [the longest x1 111 us: gather_mlp(): pl.pallas_call(functools.partial(gather_mlp_kernel, axis_name, size), in_...]
    dot_general x4 -> x0, matrix products: 121 us -> none  [the longest x1 35.9 us: local_backward(): jnp.einsum('bsf,bsd->fd', act_value.astype(jnp.bfloat16), dout_full, pref...]
    all_gather x2 -> x0, waiting for transfers between devices: 71.1 us -> none  [the longest x1 68.1 us: local_backward(): dout_full = lax.all_gather(d_out, 'tp', axis=1, tiled=True)]
    reduce_scatter x1 -> x0, waiting for transfers between devices: 55.1 us -> none  [local_backward(): lax.psum_scatter(h2_partial, 'tp', scatter_dimension=1, tiled=True)]
    unnamed x38 -> x36, local copies, waits for them, and re-layouts: 20.5 us -> 45.8 us
    all_gather x1, starting transfers between devices: 12 us -> 0.06 us  [local_backward(): mid_full = lax.all_gather(grad_mid, 'tp', axis=1, tiled=True)]
  transfers between devices with their start and end apart: 7 -> 4, of which waited for: 7 -> 4; matrix products, arithmetic and copies ran while one was open for 20% -> 11% of each run, Pallas kernels for 0% -> 0%
where the time goes in v2:
time: 625 us; the launch traced here: 622 us
  Pallas kernels  301 us (48%)
  waiting for transfers between devices  179 us (29%)
  local copies, waits for them, and re-layouts  64 us (10%)
  matrix products  49.7 us (8%)
  between operations  13.9 us (2%)
  other arithmetic  13.8 us (2%)
    pallas_call x1, Pallas kernels, gather_mlp(): pl.pallas_call(functools.partial(gather_mlp_kernel, axis_name, size), in_...  111 us
    pallas_call x1, Pallas kernels, attention_grads(): pl.pallas_call(functools.partial(attention_kernel, head_dim), grid=(n_blk...  111 us
    pallas_call x1, Pallas kernels, scatter_mlp(): pl.pallas_call(functools.partial(scatter_mlp_kernel, axis_name, size), in...  78.1 us
    reduce_scatter x1, waiting for transfers between devices, local_backward(): lax.psum_scatter(h1_partial, 'tp', scatter_dimension=1, tiled=True)  65.8 us
    all_gather x1, waiting for transfers between devices, local_backward(): mid_full = lax.all_gather(grad_mid, 'tp', axis=1, tiled=True)  46.4 us
    unnamed x36, local copies, waits for them, and re-layouts  45.8 us
    all_gather x1, waiting for transfers between devices, local_backward(): h1_full = lax.all_gather(h1_local, 'tp', axis=1, tiled=True)  36.1 us
    psum x1, waiting for transfers between devices, local_backward(): grad_vecs = lax.psum(vec_partial, 'tp')  30.7 us
  transfers between devices with their start and end apart: 4, of which 4 were waited for; matrix products, arithmetic and copies ran while one was open for 11% of the time, Pallas kernels for 0%

profile of v2, /device:TPU:113, one launch (start us, length us, event | category | flops | bytes accessed | tf_op | source)
XLA Modules:
  0.0 621.9 jit_solution(10951823184265273880)
XLA Ops:
  7.2 0.1 all-gather.6.cloned.1.call-start
  7.2 111.3 %gather_mlp.1 = (bf16[2048,1536]{1,0:T(8,128)(2,1)}, bf16[2048,3072]{1,0:T(8,128)(2,1)}, f32[1536,3072]{1,0:T(8,128)}) custom-call(bf16[256,3072]{1,0:T(8,128)(2,1)} %bitcast.57, bf16[2048,1536]{1,0:T(8,128)(2,1)} %bitcast.56, bf16[1536,3072]{1,0:T(8,128)(2,1)} %w2_ref.1, bf16[256,3072]{1,0:T(8,128)(2,1)} %bitcast.59, f32[1,3072]{1,0:T(1,128)} %bitcast.62, ...), custom_call_target="tpu_custom_call" | custom-call | flops 38654705664 | bytes 62914560 | tf_op jit(solution)/shard_map/gather_mlp/pallas_call | solution.py:435
  118.6 78.1 %scatter_mlp.1 = (bf16[256,3072]{1,0:T(8,128)(2,1)}, f32[4,8,3072]{2,1,0:T(8,128)}, f32[8,1536]{1,0:T(8,128)}, f32[3072,1536]{1,0:T(8,128)}) custom-call(bf16[2048,1536]{1,0:T(8,128)(2,1)} %get-tuple-element.19.dz_ref, bf16[3072,1536]{1,0:T(8,128)(2,1)} %w1_ref.1, bf16[2048,3072]{1,0:T(8,128)(2,1)} %get-tuple-element.20.h2_ref, bf16[256,3072]{1,0:T(8,128)(2,1)} %bitcast.60, ...), custom_call_target="tpu_custom_call" | custom-call | flops 38654705664 | bytes 62914560 | tf_op jit(solution)/shard_map/scatter_mlp/pallas_call | solution.py:596
  196.7 0.1 all-gather.6.cloned.1.call-update
  196.8 0.2 reduce-scatter.2.cloned.1.call-start
  197.0 3.7 copy.28
  200.7 2.9 copy.29
  203.7 3.3 pad.14.q_ref
  207.0 1.7 pad.15.k_ref
  208.7 2.9 copy.30
  211.7 0.0 copy-start.3
  211.7 1.7 pad.16.v_ref
  213.4 0.6 copy-done.3
  214.0 2.1 pad.17
  216.1 46.4 %all-gather.6.cloned.1.call-done.mid_ref = bf16[2048,3072]{1,0:T(8,128)(2,1)} async-done(((bf16[256,3072]{1,0:T(8,128)(2,1)}), bf16[2048,3072]{1,0:T(8,128)(2,1)}) %all-gather.6.cloned.1.call-update) | async-done | bytes 12582928 | tf_op jit(solution)/shard_map/all_gather | solution.py:620
  262.5 111.2 %attention_grads.1 = (bf16[2048,384]{1,0:T(8,128)(2,1)}, bf16[2048,384]{1,0:T(8,128)(2,1)}, bf16[2048,384]{1,0:T(8,128)(2,1)}, bf16[2048,384]{1,0:T(8,128)(2,1)}) custom-call(bf16[4,2048,128]{2,1,0:T(8,128)(2,1)} %pad.14.q_ref, bf16[4,2048,128]{2,1,0:T(8,128)(2,1)} %pad.15.k_ref, bf16[4,2048,128]{2,1,0:T(8,128)(2,1)} %pad.16.v_ref, ...), custom_call_target="tpu_custom_call" | custom-call | flops 19327352832 | bytes 41943040 | tf_op jit(solution)/shard_map/attention_grads/pallas_call | solution.py:147
  373.6 0.0 copy-start.6
  373.7 0.0 copy-start.5
  373.7 1.7 constant_dynamic-update-slice_fusion.2
  375.4 0.1 copy-done.6
  375.5 0.3 constant_dynamic-update-slice_fusion.1
  375.8 0.2 copy-done.5
  376.0 0.3 constant_dynamic-update-slice_fusion
  376.3 0.0 copy-start
  376.3 2.2 copy-done
  378.5 0.0 slice-done
  378.5 0.0 slice-done.1
  378.5 18.7 %convert_bitcast_fusion = bf16[1,2048,3072]{2,1,0:T(8,128)(2,1)} fusion(bf16[2048,1152]{1,0:T(8,128)(2,1)S(1)} %constant_dynamic-update-slice_fusion, bf16[1152,3072]{1,0:T(8,128)(2,1)S(1)} %bitcast.55), kind=kOutput, calls=%fused_computation.4 | convolution fusion | flops 14501806080 | bytes 24379392 | tf_op jit(solution)/shard_map/dot_general | solution.py:633
  397.2 0.1 reduce-scatter.2.cloned.1.call-update
  397.3 0.0 copy-start.10
  397.3 0.0 copy-start.11
  397.3 0.3 all-gather.4.cloned.1.call-start
  397.6 1.0 copy-done.1
  398.6 0.3 convert_reduce_fusion.2
  398.9 0.6 fusion.17
  399.5 0.0 copy-start.9
  399.5 0.0 copy-start.7
  399.5 65.8 %reduce-scatter.2.cloned.1.call-done = bf16[1,256,3072]{2,1,0:T(8,128)(2,1)} async-done(((bf16[1,2048,3072]{2,1,0:T(8,128)(2,1)}), bf16[1,256,3072]{2,1,0:T(8,128)(2,1)}) %reduce-scatter.2.cloned.1.call-update) | async-done | bytes 1572880 | tf_op jit(solution)/shard_map/reduce_scatter | solution.py:634
  465.3 0.0 copy-done.10
  465.3 0.0 copy-done.11
  465.3 4.3 fusion.19
  469.6 0.1 all-gather.4.cloned.1.call-update
  469.7 0.1 all-reduce.6.cloned.1.call-start
  469.8 0.0 copy-done.9
  469.8 0.6 reduce_sum.86
  470.4 0.0 copy-done.7
  470.4 0.1 reduce_sum.89
  470.5 0.0 copy-start.4
  470.5 6.7 %copy.31 = bf16[2048,1152]{0,1:T(8,128)(2,1)} copy(bf16[2048,1152]{1,0:T(8,128)(2,1)} %copy-done) | data formatting | bytes 9437184 | tf_op jit(solution)/shard_map/concatenate | solution.py:629
  477.3 0.0 copy-done.4
  477.3 1.6 copy.32
  478.9 3.0 convert_reduce_fusion
  481.9 0.7 reshape.98
  482.6 10.0 %fusion = f32[4,96,3072]{2,1,0:T(8,128)} fusion(bf16[4,96,2048]{2,1,0:T(8,128)(2,1)} %bitcast.50, bf16[2048,3072]{1,0:T(8,128)(2,1)} %all-gather.6.cloned.1.call-done.mid_ref), kind=kOutput, calls=%fused_computation | convolution fusion | flops 4831838208 | bytes 18874368 | tf_op jit(solution)/shard_map/se,sd->ed/dot_general | solution.py:628
  492.5 0.7 pad_maximum_fusion
  493.2 0.1 all-reduce.6.cloned.1.call-update
  493.3 0.0 copy-done.2
  493.3 4.2 fusion.14
  497.5 36.1 %all-gather.4.cloned.1.call-done = bf16[1,2048,3072]{2,1,0:T(8,128)(2,1)} async-done(((bf16[1,256,3072]{2,1,0:T(8,128)(2,1)}), bf16[1,2048,3072]{2,1,0:T(8,128)(2,1)}) %all-gather.4.cloned.1.call-update) | async-done | bytes 12582928 | tf_op jit(solution)/shard_map/all_gather | solution.py:622
  533.6 21.0 %fusion.2 = f32[3,384,3072]{2,1,0:T(8,128)} fusion(bf16[2048,3,384]{0,2,1:T(8,128)(2,1)} %bitcast.47, bf16[1,2048,3072]{2,1,0:T(8,128)(2,1)} %all-gather.4.cloned.1.call-done), kind=kOutput, calls=%fused_computation.2 | convolution fusion | flops 14495514624 | bytes 31457280 | tf_op jit(solution)/shard_map/sd,sie->ide/dot_general | solution.py:631
  554.7 30.7 %all-reduce.6.cloned.1.call-done = f32[6,3072]{1,0:T(8,128)} async-done(((f32[6,3072]{1,0:T(8,128)}), f32[6,3072]{1,0:T(8,128)}) %all-reduce.6.cloned.1.call-update) | async-done | bytes 73744 | tf_op jit(solution)/shard_map/psum | solution.py:641
  585.4 14.6 %copy.38 = f32[3072,1536]{1,0:T(8,128)} copy(f32[3072,1536]{1,0:T(8,128)} %get-tuple-element.49) | data formatting | bytes 37748736
  599.9 14.8 %copy.39 = f32[1536,3072]{1,0:T(8,128)} copy(f32[1536,3072]{1,0:T(8,128)} %get-tuple-element.51) | data formatting | bytes 37748736
  614.8 0.6 copy.40
  (10 shorter events, 0.0 us)
Async XLA Ops:
  7.2 255.3 %all-gather.6.cloned.1.call-start = ((), (), s32[]{:S(2)}) async-start(), calls=%async_computation.4 | async-start | bytes 14155776 | tf_op jit(solution)/shard_map/all_gather | solution.py:620
  196.8 268.6 %reduce-scatter.2.cloned.1.call-start = ((), (), s32[]{:S(2)}) async-start(), calls=%async_computation.1 | async-start | bytes 14155776 | tf_op jit(solution)/shard_map/reduce_scatter | solution.py:634
  211.7 2.4 copy-start.3
  214.0 164.5 %slice-start = ((s8[7077888]{0:T(1024)(128)(4,1)}), s8[2883584]{0:T(1024)(128)(4,1)S(1)}, s32[]{:S(2)}) async-start(s8[7077888]{0:T(1024)(128)(4,1)} %bitcast.53), calls=%async_computation.5 | async-start | bytes 5767168
  262.5 116.0 %slice-start.1 = ((s8[7077888]{0:T(1024)(128)(4,1)}), s8[4194304]{0:T(1024)(128)(4,1)S(1)}, s32[]{:S(2)}) async-start(s8[7077888]{0:T(1024)(128)(4,1)} %bitcast.53), calls=%async_computation.6 | async-start | bytes 8388608
  373.6 1.9 copy-start.6
  373.7 2.3 copy-start.5
  376.3 2.2 copy-start
  397.2 1.4 copy-start.1
  397.3 68.0 %copy-start.10 = (f32[3072]{0:T(1024)S(1)}, f32[3072]{0:T(1024)}, u32[]{:S(2)}) copy-start(f32[3072]{0:T(1024)} %param.22) | copy-start | bytes 36868
  397.3 68.0 %copy-start.11 = (f32[3072]{0:T(1024)S(1)}, f32[3072]{0:T(1024)}, u32[]{:S(2)}) copy-start(f32[3072]{0:T(1024)} %param.23) | copy-start | bytes 36868
  397.3 136.3 %all-gather.4.cloned.1.call-start = ((), (), s32[]{:S(2)}) async-start(), calls=%async_computation.2 | async-start | bytes 14155776 | tf_op jit(solution)/shard_map/all_gather | solution.py:622
  399.5 70.3 %copy-start.9 = (f32[8,1536]{1,0:T(8,128)S(1)}, f32[8,1536]{1,0:T(8,128)}, u32[]{:S(2)}) copy-start(f32[8,1536]{1,0:T(8,128)} %get-tuple-element.27) | copy-start | bytes 147460
  399.5 70.9 %copy-start.7 = (f32[4,8,3072]{2,1,0:T(8,128)S(1)}, f32[4,8,3072]{2,1,0:T(8,128)}, u32[]{:S(2)}) copy-start(f32[4,8,3072]{2,1,0:T(8,128)} %get-tuple-element.29) | copy-start | bytes 1179652
  469.7 115.7 %all-reduce.6.cloned.1.call-start = ((), (), s32[]{:S(2)}) async-start(), calls=%async_computation.3 | async-start | bytes 196608 | tf_op jit(solution)/shard_map/psum | solution.py:641
  470.5 6.8 %copy-start.4 = (bf16[2048,384]{1,0:T(8,128)(2,1)S(1)}, bf16[2048,384]{1,0:T(8,128)(2,1)}, u32[]{:S(2)}) copy-start(bf16[2048,384]{1,0:T(8,128)(2,1)} %get-tuple-element.25) | copy-start | bytes 4718596
  482.6 10.7 %copy-start.2 = (bf16[256,3072]{1,0:T(8,128)(2,1)S(1)}, bf16[256,3072]{1,0:T(8,128)(2,1)}, u32[]{:S(2)}) copy-start(bf16[256,3072]{1,0:T(8,128)(2,1)} %get-tuple-element.21) | copy-start | bytes 4718596
  599.9 14.8 %copy-start.8 = (f32[6,3072]{1,0:T(8,128)S(1)}, f32[6,3072]{1,0:T(8,128)}, u32[]{:S(2)}) copy-start(f32[6,3072]{1,0:T(8,128)} %all-reduce.6.cloned.1.call-done) | copy-start | bytes 221188
Sparse Core Ops, SparseCore 0:
  196.9 65.5 all-gather.5
  397.4 67.8 reduce-scatter.1
  469.8 63.7 all-gather.3
  536.4 48.9 all-reduce.5

commit v3 on v2

--- a/solution.py
+++ b/solution.py
@@ -39,132 +39,57 @@
 TN = (((0,), (0,)), ((), ()))
 
 
+MIB = 2 ** 20
+
+
+def loop(count, body):
+    def step(i, carry):
+        body(i)
+        return carry
+
+    lax.fori_loop(0, count, step, 0)
+
+
+def span(i, n):
+    return pl.ds(pl.multiple_of(i * n, n), n)
+
+
+def as_row(vec):
+    return vec.reshape(1, -1)
+
+
 def dot(lhs, rhs, dims):
     return lax.dot_general(lhs, rhs, dims, preferred_element_type=jnp.float32)
 
 
-def attention_kernel(head_dim, q_ref, k_ref, v_ref, mid_ref, wo_ref, ctx_ref, dq_ref, dk_ref, dv_ref,
-                     s_scr, dp_scr, dk_acc, dv_acc, dctx_scr, ctx_scr, dq_scr, m_scr, l_scr, d_scr):
-    n_heads, blk, _ = q_ref.shape
-    q_idx = pl.program_id(0)
-    scale = head_dim ** -0.5
-    exp_scale = scale * math.log2(math.e)
-
-    @pl.when(q_idx == 0)
-    def _():
-        dk_acc[...] = jnp.zeros_like(dk_acc)
-        dv_acc[...] = jnp.zeros_like(dv_acc)
-
-    dctx_all = dot(mid_ref[...], wo_ref[...], NT).astype(jnp.bfloat16)
-    for head in range(n_heads):
-        dctx_scr[head] = dctx_all[:, head * LANES:(head + 1) * LANES]
-
-    def lane_fold(vals, op):
-        out = vals[:, :LANES]
-        for piece in range(1, vals.shape[1] // LANES):
-            out = op(out, vals[:, piece * LANES:(piece + 1) * LANES])
-        return out
-
-    def per_head(head, carry):
-        q_blk = q_ref[head]
-        dctx_blk = dctx_scr[head]
-
-        def scores(j):
-            rows = pl.ds(pl.multiple_of(j * blk, blk), blk)
-            dp_scr[j] = dot(dctx_blk, v_ref[head, rows, :], NT)
-            return dot(q_blk, k_ref[head, rows, :], NT)
-
-        row_ids = lax.broadcasted_iota(jnp.int32, (blk, blk), 0)
-        col_ids = lax.broadcasted_iota(jnp.int32, (blk, blk), 1)
-        diag = jnp.where(row_ids >= col_ids, scores(q_idx), -1e30)
-        s_scr[q_idx] = diag
-        m_scr[...] = lane_fold(diag, jnp.maximum)
-
-        def pass_max(j, c):
-            s_blk = scores(j)
-            s_scr[j] = s_blk
-            m_scr[...] = jnp.maximum(m_scr[...], lane_fold(s_blk, jnp.maximum))
-            return c
-
-        lax.fori_loop(0, q_idx, pass_max, 0)
-        row_max = jnp.max(m_scr[...], axis=1, keepdims=True)
-        l_scr[...] = jnp.zeros_like(l_scr)
-        d_scr[...] = jnp.zeros_like(d_scr)
-
-        def pass_exp(j, c):
-            prob = jnp.exp2((s_scr[j] - row_max) * exp_scale)
-            s_scr[j] = prob
-            l_scr[...] += lane_fold(prob, jnp.add)
-            d_scr[...] += lane_fold(prob * dp_scr[j], jnp.add)
-            return c
-
-        lax.fori_loop(0, q_idx + 1, pass_exp, 0)
-        inv_sum = 1.0 / jnp.sum(l_scr[...], axis=1, keepdims=True)
-        delta = jnp.sum(d_scr[...], axis=1, keepdims=True) * inv_sum
-        ctx_scr[head] = jnp.zeros((blk, LANES), jnp.float32)
-        dq_scr[head] = jnp.zeros((blk, LANES), jnp.float32)
-
-        def pass_grad(j, c):
-            rows = pl.ds(pl.multiple_of(j * blk, blk), blk)
-            prob = s_scr[j] * inv_sum
-            prob_low = prob.astype(jnp.bfloat16)
-            ds_low = (prob * (dp_scr[j] - delta) * scale).astype(jnp.bfloat16)
-            ctx_scr[head] += dot(prob_low, v_ref[head, rows, :], NN)
-            dq_scr[head] += dot(ds_low, k_ref[head, rows, :], NN)
-            dk_acc[head, rows, :] += dot(ds_low, q_blk, TN)
-            dv_acc[head, rows, :] += dot(prob_low, dctx_blk, TN)
-            return c
-
-        lax.fori_loop(0, q_idx + 1, pass_grad, 0)
-        return carry
-
-    lax.fori_loop(0, n_heads, per_head, 0)
-
-    def pack(scr):
-        return jnp.concatenate([scr[head][:, :head_dim] for head in range(n_heads)], axis=1).astype(jnp.bfloat16)
-
-    ctx_ref[...] = pack(ctx_scr)
-    dq_ref[...] = pack(dq_scr)
-
-    @pl.when(q_idx == pl.num_programs(0) - 1)
-    def _():
-        dk_ref[...] = pack(dk_acc)
-        dv_ref[...] = pack(dv_acc)
-
-
-def attention_grads(q_heads, k_heads, v_heads, mid_rows, w_proj):
-    _, seq, n_heads, head_dim = q_heads.shape
-    d_model = mid_rows.shape[-1]
-    blk = 256
-    n_blk = seq // blk
-    pad = LANES - head_dim
-    qp, kp, vp = (jnp.pad(jnp.moveaxis(a[0], 1, 0), ((0, 0), (0, 0), (0, pad))) for a in (q_heads, k_heads, v_heads))
-    wo = jnp.pad(w_proj, ((0, 0), (0, pad), (0, 0))).reshape(n_heads * LANES, d_model)
-    width = n_heads * head_dim
-    out = jax.ShapeDtypeStruct((seq, width), jnp.bfloat16)
-    full = lambda *shape: pl.BlockSpec(shape, lambda i: (0,) * len(shape))
-    flops = 6 * n_heads * seq * seq * LANES + 2 * seq * d_model * n_heads * LANES
-    return pl.pallas_call(
-        functools.partial(attention_kernel, head_dim),
-        grid=(n_blk,),
-        in_specs=[pl.BlockSpec((n_heads, blk, LANES), lambda i: (0, i, 0)), full(n_heads, seq, LANES), full(n_heads, seq, LANES),
-                  pl.BlockSpec((blk, d_model), lambda i: (i, 0)), full(n_heads * LANES, d_model)],
-        out_specs=[pl.BlockSpec((blk, width), lambda i: (i, 0)), pl.BlockSpec((blk, width), lambda i: (i, 0)),
-                   full(seq, width), full(seq, width)],
-        out_shape=[out] * 4,
-        scratch_shapes=[pltpu.VMEM((n_blk, blk, blk), jnp.float32), pltpu.VMEM((n_blk, blk, blk), jnp.float32),
-                        pltpu.VMEM((n_heads, seq, LANES), jnp.float32), pltpu.VMEM((n_heads, seq, LANES), jnp.float32),
-                        pltpu.VMEM((n_heads, blk, LANES), jnp.bfloat16),
-                        pltpu.VMEM((n_heads, blk, LANES), jnp.float32), pltpu.VMEM((n_heads, blk, LANES), jnp.float32),
-                        pltpu.VMEM((blk, LANES), jnp.float32), pltpu.VMEM((blk, LANES), jnp.float32), pltpu.VMEM((blk, LANES), jnp.float32)],
-        compiler_params=pltpu.CompilerParams(dimension_semantics=("arbitrary",), vmem_limit_bytes=56 * 2 ** 20),
-        cost_estimate=pl.CostEstimate(flops=flops, bytes_accessed=40 * 2 ** 20, transcendentals=n_heads * seq * seq // 2),
-        name="attention_grads",
-    )(qp, kp, vp, mid_rows, wo)
-
-
 MESH_IDS = pl.DeviceIdType.MESH
 ANY = pl.BlockSpec(memory_space=pl.ANY)
+
+
+def comm_params(collective_id):
+    return pltpu.CompilerParams(collective_id=collective_id, has_side_effects=True, vmem_limit_bytes=63 * MIB)
+
+
+def norm_block(src, gain_ref, bias_ref, dst):
+    chunk = 32
+
+    def norm_rows(i):
+        _, _, normed = layer_norm_fwd(src[span(i, chunk), :], gain_ref[...], bias_ref[...])
+        dst[span(i, chunk), :] = normed
+
+    loop(src.shape[0] // chunk, norm_rows)
+
+
+def column_sums(src, dst):
+    dst[...] = jnp.zeros_like(dst)
+    fold, chunk = dst.shape[0], 64
+
+    def bias_body(i):
+        vals = src[span(i, chunk), :].astype(jnp.float32)
+        for j in range(chunk // fold):
+            dst[...] += vals[j * fold:(j + 1) * fold]
+
+    loop(src.shape[0] // chunk, bias_body)
 
 
 class Ring:
@@ -339,7 +264,7 @@
     own_copy.start()
     z_copies = []
     for rel in range(size):
-        src = z_ref.at[pl.ds(pl.multiple_of(ring.block_owner(rel) * rows, rows), rows)]
+        src = z_ref.at[span(ring.block_owner(rel), rows)]
         z_copies.append(pltpu.make_async_copy(src, zu.at[pl.ds(rel * rows, rows)], local_sem.at[4 + rel]))
     xmid_copy.start()
     w2_copy.start()
@@ -347,15 +272,7 @@
         copy.start()
 
     xmid_copy.wait()
-    chunk = 32
-
-    def norm_rows(i, c):
-        sl = pl.ds(pl.multiple_of(i * chunk, chunk), chunk)
-        _, _, normed = layer_norm_fwd(xmid[sl, :], gain_ref[...], bias_ref[...])
-        h2[sl, :] = normed
-        return c
-
-    lax.fori_loop(0, rows // chunk, norm_rows, 0)
+    norm_block(xmid, gain_ref, bias_ref, h2)
     h2_gather = Gather(ring, h2, h2_hbm, h2_send_sem, h2_recv_sem)
     h2_own = pltpu.make_async_copy(h2, h2_gather.block(OWN), local_sem.at[3])
     h2_own.start()
@@ -367,15 +284,14 @@
         z_copies[rel].wait()
         z_copies[rel + 1].wait()
 
-        def body(n, c):
-            cols = pl.ds(pl.multiple_of(n * tile, tile), tile)
+        def body(n):
+            cols = span(n, tile)
             act_value, act_slope = gelu_parts(zu[pl.ds(base, pair), cols].astype(jnp.float32))
             zu[pl.ds(base, pair), cols] = act_value.astype(jnp.bfloat16)
             grad_act = dot(dout_all[pl.ds(base, pair), :], w2[cols, :], NT)
             dz[pl.ds(base, pair), cols] = (grad_act * act_slope).astype(jnp.bfloat16)
-            return c
-
-        lax.fori_loop(0, units // tile, body, 0)
+
+        loop(units // tile, body)
         copy = pltpu.make_async_copy(dz.at[pl.ds(base, pair)], dz_hbm.at[pl.ds(base, pair)], out_sem.at[rel // 2])
         copy.start()
         return copy
@@ -397,9 +313,9 @@
     n_tiles = units // tile
 
     def dw2_copy(i, slot):
-        return pltpu.make_async_copy(dw2_tile.at[slot], dw2_hbm.at[pl.ds(pl.multiple_of(i * tile, tile), tile)], out_sem.at[4 + slot])
-
-    def dw2_body(i, c):
+        return pltpu.make_async_copy(dw2_tile.at[slot], dw2_hbm.at[span(i, tile)], out_sem.at[4 + slot])
+
+    def dw2_body(i):
         slot = i % 2
 
         @pl.when(i >= 2)
@@ -410,11 +326,10 @@
         def _():
             h2_gather.first_halves()
 
-        dw2_tile[slot] = dot(zu[:, pl.ds(pl.multiple_of(i * tile, tile), tile)], dout_all[...], TN)
+        dw2_tile[slot] = dot(zu[:, span(i, tile)], dout_all[...], TN)
         dw2_copy(i, slot).start()
-        return c
-
-    lax.fori_loop(0, n_tiles, dw2_body, 0)
+
+    loop(n_tiles, dw2_body)
     h2_gather.second_halves()
     h2_own.wait()
     for copy in dz_copies:
@@ -442,10 +357,10 @@
                         pltpu.VMEM((units, d_model), bf), pltpu.VMEM((rows, d_model), bf), pltpu.VMEM((rows, d_model), bf),
                         pltpu.VMEM((2, 256, d_model), f32), dma((4 + size,)),
                         dma((Gather.N_COPIES,)), dma((Gather.N_COPIES,)), dma((Gather.N_COPIES,)), dma((Gather.N_COPIES,)), dma((6,))],
-        compiler_params=pltpu.CompilerParams(collective_id=collective_id, has_side_effects=True, vmem_limit_bytes=60 * 2 ** 20),
-        cost_estimate=pl.CostEstimate(flops=4 * seq * units * d_model, bytes_accessed=60 * 2 ** 20, transcendentals=seq * units),
+        compiler_params=comm_params(collective_id),
+        cost_estimate=pl.CostEstimate(flops=4 * seq * units * d_model, bytes_accessed=60 * MIB, transcendentals=seq * units),
         name="gather_mlp",
-    )(d_out, z_rows, w_fc2, x_mid, gain.reshape(1, -1), bias.reshape(1, -1))
+    )(d_out, z_rows, w_fc2, x_mid, as_row(gain), as_row(bias))
 
 
 def scatter_grads(ring, stage_fn, partial, peer_part, outbox, inbox, send_sem, recv_sem):
@@ -476,9 +391,9 @@
         return total
 
     for part in range(2):
-        def body(i, c):
-            inner = pl.ds(pl.multiple_of(i * chunk, chunk), chunk)
-            sl = pl.ds(pl.multiple_of(part * half + i * chunk, chunk), chunk)
+        def body(i):
+            inner = span(i, chunk)
+            sl = span(part * (half // chunk) + i, chunk)
             grad_norm = scatter.own_sum(part, inner, sl)
             x_hat, inv_std = norm_hat(x_rows[sl, :])
             resid_f32 = resid[sl, :].astype(jnp.float32)
@@ -488,9 +403,8 @@
             sums[1] += fold(grad_norm)
             sums[2] += fold(result.astype(jnp.float32))
             sums[3] += fold(resid_f32)
-            return c
-
-        lax.fori_loop(0, half // chunk, body, 0)
+
+        loop(half // chunk, body)
 
 
 def norm_hat(token_rows):
@@ -528,26 +442,25 @@
         dz_copies[rel].wait()
         sl = pl.ds(rel * rows, pair)
 
-        def body(n, c):
-            cols = pl.ds(pl.multiple_of(n * tile, tile), tile)
+        def body(n):
+            cols = span(n, tile)
             partial[sl, cols] = dot(dz[sl, :], w1[cols, :], NT).astype(jnp.bfloat16)
-            return c
-
-        lax.fori_loop(0, d_model // tile, body, 0)
+
+        loop(d_model // tile, body)
 
     scatter = scatter_grads(ring, stage, partial, peer_part, outbox, inbox, send_sem, recv_sem)
 
     n_tiles = d_model // tile
 
     def tile_in(i, slot):
-        return pltpu.make_async_copy(h2_ref.at[:, pl.ds(pl.multiple_of(i * tile, tile), tile)], h2_tile.at[slot], tile_sem.at[slot])
+        return pltpu.make_async_copy(h2_ref.at[:, span(i, tile)], h2_tile.at[slot], tile_sem.at[slot])
 
     def tile_out(i, slot):
-        return pltpu.make_async_copy(dw1_tile.at[slot], dw1_hbm.at[pl.ds(pl.multiple_of(i * tile, tile), tile)], tile_sem.at[2 + slot])
+        return pltpu.make_async_copy(dw1_tile.at[slot], dw1_hbm.at[span(i, tile)], tile_sem.at[2 + slot])
 
     tile_in(0, 0).start()
 
-    def dw1_body(i, c):
+    def dw1_body(i):
         slot = i % 2
 
         @pl.when(i + 1 < n_tiles)
@@ -561,18 +474,9 @@
         tile_in(i, slot).wait()
         dw1_tile[slot] = dot(h2_tile[slot], dz[...], TN)
         tile_out(i, slot).start()
-        return c
-
-    lax.fori_loop(0, n_tiles, dw1_body, 0)
-    dbfc1_ref[...] = jnp.zeros_like(dbfc1_ref)
-
-    def bias_body(i, c):
-        vals = dz[pl.ds(pl.multiple_of(i * 64, 64), 64), :].astype(jnp.float32)
-        for j in range(8):
-            dbfc1_ref[...] += vals[j * 8:(j + 1) * 8]
-        return c
-
-    lax.fori_loop(0, dz.shape[0] // 64, bias_body, 0)
+
+    loop(n_tiles, dw1_body)
+    column_sums(dz, dbfc1_ref)
     for i in (n_tiles - 2, n_tiles - 1):
         tile_out(i, i % 2).wait()
     xmid_copy.wait()
@@ -603,10 +507,385 @@
                         pltpu.VMEM((2, 256, units), f32), pltpu.VMEM((rows, d_model), bf), pltpu.VMEM((rows, d_model), bf)]
         + scatter_scratch(size, rows, d_model)
         + [dma((7,)), dma((Scatter.N_COPIES,)), dma((Scatter.N_COPIES,)), dma((4,))],
-        compiler_params=pltpu.CompilerParams(collective_id=collective_id, has_side_effects=True, vmem_limit_bytes=63 * 2 ** 20),
-        cost_estimate=pl.CostEstimate(flops=4 * seq * units * d_model, bytes_accessed=60 * 2 ** 20, transcendentals=0),
+        compiler_params=comm_params(collective_id),
+        cost_estimate=pl.CostEstimate(flops=4 * seq * units * d_model, bytes_accessed=60 * MIB, transcendentals=0),
         name="scatter_mlp",
-    )(dz_rel, w_fc1, h2_rel, x_mid, d_out, gain.reshape(1, -1))
+    )(dz_rel, w_fc1, h2_rel, x_mid, d_out, as_row(gain))
+
+
+def gathered_block_owner(ring, rel):
+    pair = rel // 2
+    n_chips = ring.size // 2
+    chip = (ring.chip + 3 * pair + 3 * (pair // 2) + 2 * (pair // 3)) % n_chips
+    return 2 * chip + (ring.core + rel) % 2
+
+
+def lane_fold(vals, op):
+    out = vals[:, :LANES]
+    for piece in range(1, vals.shape[1] // LANES):
+        out = op(out, vals[:, piece * LANES:(piece + 1) * LANES])
+    return out
+
+
+def gather_attention_kernel(axis_name, size, head_dim, dmid_ref, q_ref, k_ref, v_ref, wo_ref, xin_ref, gain_ref, bias_ref,
+                            dqkv_hbm, ctx_hbm, dmid_hbm, h1_hbm,
+                            dmid, q_all, k_all, v_all, wo, xin, h1, s_scr, dp_scr, dk_acc, dv_acc, dctx_scr, ctx_scr, dq_scr,
+                            m_scr, l_scr, d_scr, rows_out, pack_out,
+                            local_sem, send_sem, recv_sem, h1_send_sem, h1_recv_sem, out_sem):
+    ring = Ring(axis_name, size)
+    rows = xin.shape[0]
+    n_heads = q_all.shape[0]
+    width = n_heads * head_dim
+    scale = head_dim ** -0.5
+    exp_scale = scale * math.log2(math.e)
+    group = 2
+    ring.barrier()
+    gather = Gather(ring, dmid_ref, dmid, send_sem, recv_sem)
+    gather.start()
+    own_copy = pltpu.make_async_copy(dmid_ref, gather.block(OWN), local_sem.at[0])
+    loads = [pltpu.make_async_copy(src, dst, local_sem.at[1 + i])
+             for i, (src, dst) in enumerate(((xin_ref, xin), (wo_ref, wo), (v_ref, v_all), (k_ref, k_all), (q_ref, q_all)))]
+    own_copy.start()
+    for copy in loads:
+        copy.start()
+    dk_acc[...] = jnp.zeros_like(dk_acc)
+    dv_acc[...] = jnp.zeros_like(dv_acc)
+    loads[0].wait()
+    norm_block(xin, gain_ref, bias_ref, h1)
+    h1_gather = Gather(ring, h1, h1_hbm, h1_send_sem, h1_recv_sem)
+    h1_own = pltpu.make_async_copy(h1, h1_gather.block(OWN), local_sem.at[6])
+    h1_own.start()
+    own_copy.wait()
+    for copy in loads[1:]:
+        copy.wait()
+
+    def dmid_out(rel):
+        sl = pl.ds(rel * rows, rows)
+        return pltpu.make_async_copy(dmid.at[sl], dmid_hbm.at[sl], out_sem.at[rel])
+
+    def ctx_out(r):
+        return pltpu.make_async_copy(rows_out.at[0, r % 2], ctx_hbm.at[span(r, rows)], out_sem.at[8 + r % 2])
+
+    def dq_out(r):
+        q_idx = gathered_block_owner(ring, r)
+        dst = dqkv_hbm.at[span(q_idx, rows), pl.ds(0, width)]
+        return pltpu.make_async_copy(rows_out.at[1, r % 2], dst, out_sem.at[10 + r % 2])
+
+    def pack(scr, sl):
+        return jnp.concatenate([scr[head, sl, :] for head in range(n_heads)], axis=1).astype(jnp.bfloat16)
+
+    def block_body(r):
+        @pl.when(r == 1)
+        def _():
+            gather.recv(0)
+            gather.first_halves()
+            h1_gather.start()
+
+        @pl.when(r == 2)
+        def _():
+            gather.second_halves()
+
+        @pl.when(r == 3)
+        def _():
+            gather.recv(7, 9)
+
+        @pl.when(r == 5)
+        def _():
+            gather.recv(8, 10)
+
+        @pl.when(r == 6)
+        def _():
+            gather.opposite()
+            h1_gather.first_halves()
+
+        @pl.when(r == 7)
+        def _():
+            gather.recv(11, 12)
+
+        @pl.when(r >= 2)
+        def _():
+            ctx_out(r - 2).wait()
+            dq_out(r - 2).wait()
+
+        q_idx = gathered_block_owner(ring, r)
+        q_rows = span(q_idx, rows)
+        dmid_rows = span(r, rows)
+        dctx_all = dot(dmid[dmid_rows, :], wo[...], NT).astype(jnp.bfloat16)
+        for head in range(n_heads):
+            dctx_scr[head] = dctx_all[:, head * head_dim:(head + 1) * head_dim]
+
+        def head_group(g):
+            heads = [g * group + i for i in range(group)]
+            row_ids = lax.broadcasted_iota(jnp.int32, (rows, rows), 0)
+            col_ids = lax.broadcasted_iota(jnp.int32, (rows, rows), 1)
+
+            def k_rows(j):
+                return span(j, rows)
+
+            for i, head in enumerate(heads):
+                dp_scr[i, q_idx] = dot(dctx_scr[head], v_all[head, q_rows, :], NT)
+                diag = jnp.where(row_ids >= col_ids, dot(q_all[head, q_rows, :], k_all[head, q_rows, :], NT), -1e30)
+                s_scr[i, q_idx] = diag
+                m_scr[i] = lane_fold(diag, jnp.maximum)
+
+            def pass_max(j):
+                for i, head in enumerate(heads):
+                    dp_scr[i, j] = dot(dctx_scr[head], v_all[head, k_rows(j), :], NT)
+                    s_blk = dot(q_all[head, q_rows, :], k_all[head, k_rows(j), :], NT)
+                    s_scr[i, j] = s_blk
+                    m_scr[i] = jnp.maximum(m_scr[i], lane_fold(s_blk, jnp.maximum))
+
+            loop(q_idx, pass_max)
+            for i in range(group):
+                m_scr[i] = jnp.broadcast_to(jnp.max(m_scr[i], axis=1, keepdims=True), (rows, LANES))
+                l_scr[i] = jnp.zeros((rows, LANES), jnp.float32)
+                d_scr[i] = jnp.zeros((rows, LANES), jnp.float32)
+
+            def wide(stat):
+                return jnp.concatenate([stat] * (rows // LANES), axis=1)
+
+            def pass_exp(j):
+                for i in range(group):
+                    prob = jnp.exp2((s_scr[i, j] - wide(m_scr[i])) * exp_scale)
+                    s_scr[i, j] = prob
+                    l_scr[i] += lane_fold(prob, jnp.add)
+                    d_scr[i] += lane_fold(prob * dp_scr[i, j], jnp.add)
+
+            loop(q_idx + 1, pass_exp)
+            for i, head in enumerate(heads):
+                inv_sum = 1.0 / jnp.sum(l_scr[i], axis=1, keepdims=True)
+                delta = jnp.sum(d_scr[i], axis=1, keepdims=True) * inv_sum
+                l_scr[i] = jnp.broadcast_to(inv_sum, (rows, LANES))
+                d_scr[i] = jnp.broadcast_to(delta, (rows, LANES))
+                ctx_scr[head] = jnp.zeros((rows, head_dim), jnp.float32)
+                dq_scr[head] = jnp.zeros((rows, head_dim), jnp.float32)
+
+            def pass_grad(j):
+                for i, head in enumerate(heads):
+                    prob = s_scr[i, j] * wide(l_scr[i])
+                    prob_low = prob.astype(jnp.bfloat16)
+                    ds_low = (prob * (dp_scr[i, j] - wide(d_scr[i])) * scale).astype(jnp.bfloat16)
+                    ctx_scr[head] += dot(prob_low, v_all[head, k_rows(j), :], NN)
+                    dq_scr[head] += dot(ds_low, k_all[head, k_rows(j), :], NN)
+                    dk_acc[head, k_rows(j), :] += dot(ds_low, q_all[head, q_rows, :], TN)
+                    dv_acc[head, k_rows(j), :] += dot(prob_low, dctx_scr[head], TN)
+
+            loop(q_idx + 1, pass_grad)
+
+        loop(n_heads // group, head_group)
+        everything = pl.ds(0, rows)
+        rows_out[0, r % 2] = pack(ctx_scr, everything)
+        rows_out[1, r % 2] = pack(dq_scr, everything)
+        ctx_out(r).start()
+        dq_out(r).start()
+
+    loop(size, block_body)
+    h1_gather.second_halves()
+    for rel in range(size):
+        dmid_out(rel).start()
+
+    def pack_body(i):
+        sl = span(i, rows)
+        pack_out[0, sl, :] = pack(dk_acc, sl)
+        pack_out[1, sl, :] = pack(dv_acc, sl)
+
+    loop(size, pack_body)
+    packed = [pltpu.make_async_copy(pack_out.at[part], dqkv_hbm.at[:, pl.ds((1 + part) * width, width)], out_sem.at[12 + part]) for part in range(2)]
+    for copy in packed:
+        copy.start()
+    h1_gather.opposite()
+    for r in (size - 2, size - 1):
+        ctx_out(r).wait()
+        dq_out(r).wait()
+    for rel in range(size):
+        dmid_out(rel).wait()
+    for copy in packed:
+        copy.wait()
+    h1_own.wait()
+    h1_gather.recv(0, 7, 8, 9, 10, 11, 12)
+    gather.drain()
+    h1_gather.drain()
+
+
+def gather_attention(axis_name, size, grad_mid, q_heads, k_heads, v_heads, w_proj, x_in, gain, bias, collective_id):
+    seq, n_heads, head_dim = q_heads.shape
+    rows, d_model = grad_mid.shape
+    qp, kp, vp = (jnp.moveaxis(a, 1, 0) for a in (q_heads, k_heads, v_heads))
+    width = n_heads * head_dim
+    wo = w_proj.reshape(width, d_model)
+    bf, f32, dma = jnp.bfloat16, jnp.float32, pltpu.SemaphoreType.DMA
+    vm = pl.BlockSpec(memory_space=pltpu.VMEM)
+    acc = lambda *shape: pltpu.VMEM(shape, f32)
+    heads = pltpu.VMEM((n_heads, seq, head_dim), bf)
+    flops = 6 * n_heads * seq * seq * LANES + 2 * seq * d_model * width
+    return pl.pallas_call(
+        functools.partial(gather_attention_kernel, axis_name, size, head_dim),
+        in_specs=[ANY] * 6 + [vm, vm],
+        out_specs=[ANY] * 4,
+        out_shape=[jax.ShapeDtypeStruct((seq, 3 * width), bf), jax.ShapeDtypeStruct((seq, width), bf),
+                   jax.ShapeDtypeStruct((seq, d_model), bf), jax.ShapeDtypeStruct((seq, d_model), bf)],
+        scratch_shapes=[pltpu.VMEM((seq, d_model), bf), heads, heads, heads, pltpu.VMEM((width, d_model), bf),
+                        pltpu.VMEM((rows, d_model), bf), pltpu.VMEM((rows, d_model), bf),
+                        acc(2, size, rows, rows), acc(2, size, rows, rows), acc(n_heads, seq, head_dim), acc(n_heads, seq, head_dim),
+                        pltpu.VMEM((n_heads, rows, head_dim), bf), acc(n_heads, rows, head_dim), acc(n_heads, rows, head_dim),
+                        acc(2, rows, LANES), acc(2, rows, LANES), acc(2, rows, LANES),
+                        pltpu.VMEM((2, 2, rows, width), bf), pltpu.VMEM((2, seq, width), bf),
+                        dma((7,)), dma((Gather.N_COPIES,)), dma((Gather.N_COPIES,)), dma((Gather.N_COPIES,)), dma((Gather.N_COPIES,)), dma((14,))],
+        compiler_params=comm_params(collective_id),
+        cost_estimate=pl.CostEstimate(flops=flops, bytes_accessed=60 * MIB, transcendentals=n_heads * seq * seq // 2),
+        name="gather_attention",
+    )(grad_mid, qp, kp, vp, wo, x_in, as_row(gain), as_row(bias))
+
+
+def sum_rows8(vals):
+    return jnp.sum(vals, axis=0, keepdims=True)
+
+
+def scatter_qkv_kernel(axis_name, size, dqkv_ref, wqkv_ref, h1_ref, ctx_ref, dmid_ref, xin_ref, dmid_own_ref, gain_ref, sums2_ref,
+                       gradx_ref, vecs_ref, dbqkv_ref, dwqkv_hbm, dwo_hbm,
+                       dqkv, wqkv, ctx, h1_tile, dmid_tile, dwqkv_tile, dwo_tile, xin, dmid_own, sums1, early_box, late_box,
+                       partial, peer_part, outbox, inbox,
+                       local_sem, send_sem, recv_sem, tile_sem, early_send, early_recv, late_send, late_recv):
+    ring = Ring(axis_name, size)
+    rows = xin.shape[0]
+    d_model = wqkv.shape[1]
+    pair, tile = 2 * rows, 256
+    sem = pltpu.get_barrier_semaphore()
+    for step in range(1, size):
+        pl.semaphore_signal(sem, inc=1, device_id={axis_name: (ring.me + step) % size}, device_id_type=MESH_IDS)
+    pl.semaphore_wait(sem, size - 1)
+
+    dqkv_copies = {}
+    for rel in (6, 7, 2, 3, 4, 5, 0, 1):
+        src = dqkv_ref.at[span(ring.block_owner(rel), rows)]
+        dqkv_copies[rel] = pltpu.make_async_copy(src, dqkv.at[pl.ds(rel * rows, rows)], local_sem.at[rel])
+    w_copy = pltpu.make_async_copy(wqkv_ref, wqkv, local_sem.at[8])
+    ctx_copy = pltpu.make_async_copy(ctx_ref, ctx, local_sem.at[9])
+    xin_copy = pltpu.make_async_copy(xin_ref, xin, local_sem.at[10])
+    own_copy = pltpu.make_async_copy(dmid_own_ref, dmid_own, local_sem.at[11])
+    dqkv_copies[6].start()
+    dqkv_copies[7].start()
+    w_copy.start()
+    for rel in (2, 3, 4, 5, 0, 1):
+        dqkv_copies[rel].start()
+    for copy in (ctx_copy, xin_copy, own_copy):
+        copy.start()
+
+    def share(box, send, recv, step):
+        return ring.copy(box.at[ring.me], box.at[ring.me], send.at[step], recv.at[ring.me], (ring.me + step) % size)
+
+    def shared(box, send, recv, step):
+        owner = (ring.me + step) % size
+        return ring.copy(box.at[owner], box.at[owner], send.at[step], recv.at[owner], owner)
+
+    for i in range(4):
+        early_box[ring.me, pl.ds(i, 1), :] = sum_rows8(sums2_ref[i])
+    w_copy.wait()
+
+    def stage(rel):
+        dqkv_copies[rel].wait()
+        dqkv_copies[rel + 1].wait()
+        sl = pl.ds(rel * rows, pair)
+
+        def body(n):
+            cols = span(n, tile)
+            partial[sl, cols] = dot(dqkv[sl, :], wqkv[:, cols], NN).astype(jnp.bfloat16)
+
+        loop(d_model // tile, body)
+
+    scatter = scatter_grads(ring, stage, partial, peer_part, outbox, inbox, send_sem, recv_sem)
+    for step in range(1, size):
+        share(early_box, early_send, early_recv, step).start()
+
+    n_tiles = d_model // tile
+
+    def tile_in(i, slot):
+        cols = span(i, tile)
+        return (pltpu.make_async_copy(h1_ref.at[:, cols], h1_tile.at[slot], tile_sem.at[slot]),
+                pltpu.make_async_copy(dmid_ref.at[:, cols], dmid_tile.at[slot], tile_sem.at[2 + slot]))
+
+    def tile_out(i, slot):
+        cols = span(i, tile)
+        return (pltpu.make_async_copy(dwqkv_tile.at[slot], dwqkv_hbm.at[:, cols], tile_sem.at[4 + slot]),
+                pltpu.make_async_copy(dwo_tile.at[slot], dwo_hbm.at[:, cols], tile_sem.at[6 + slot]))
+
+    for copy in tile_in(0, 0):
+        copy.start()
+    ctx_copy.wait()
+
+    def dw_body(i):
+        slot = i % 2
+
+        @pl.when(i + 1 < n_tiles)
+        def _():
+            for copy in tile_in(i + 1, 1 - slot):
+                copy.start()
+
+        @pl.when(i >= 2)
+        def _():
+            for copy in tile_out(i - 2, slot):
+                copy.wait()
+
+        for copy in tile_in(i, slot):
+            copy.wait()
+        dwqkv_tile[slot] = dot(dqkv[...], h1_tile[slot], TN)
+        dwo_tile[slot] = dot(ctx[...], dmid_tile[slot], TN)
+        for copy in tile_out(i, slot):
+            copy.start()
+
+    loop(n_tiles, dw_body)
+    column_sums(dqkv, dbqkv_ref)
+    for i in (n_tiles - 2, n_tiles - 1):
+        for copy in tile_out(i, i % 2):
+            copy.wait()
+    xin_copy.wait()
+    own_copy.wait()
+    scatter.arrive()
+    norm_backward(scatter, rows, xin, dmid_own, gain_ref, gradx_ref, sums1)
+    for i in range(2):
+        late_box[ring.me, pl.ds(i, 1), :] = sum_rows8(sums1[i])
+    for step in range(1, size):
+        share(late_box, late_send, late_recv, step).start()
+    for step in range(1, size):
+        shared(early_box, early_send, early_recv, step).wait_recv()
+    scatter.drain()
+    for step in range(1, size):
+        shared(late_box, late_send, late_recv, step).wait_recv()
+    late, early = late_box[0], early_box[0]
+    for src in range(1, size):
+        late = late + late_box[src]
+        early = early + early_box[src]
+    vecs_ref[pl.ds(0, 2), :] = late
+    vecs_ref[pl.ds(2, 4), :] = early
+    for step in range(1, size):
+        share(early_box, early_send, early_recv, step).wait_send()
+        share(late_box, late_send, late_recv, step).wait_send()
+
+
+def scatter_qkv(axis_name, size, dqkv, wqkv_rows, h1_rel, ctx_rel, dmid_rel, x_in, grad_mid, gain, sums2, collective_id):
+    rows, d_model = x_in.shape
+    seq, width3 = dqkv.shape
+    width = width3 // 3
+    bf, f32, dma = jnp.bfloat16, jnp.float32, pltpu.SemaphoreType.DMA
+    vm = pl.BlockSpec(memory_space=pltpu.VMEM)
+    return pl.pallas_call(
+        functools.partial(scatter_qkv_kernel, axis_name, size),
+        in_specs=[ANY] * 7 + [vm, vm],
+        out_specs=[vm, vm, vm, ANY, ANY],
+        out_shape=[jax.ShapeDtypeStruct((rows, d_model), bf), jax.ShapeDtypeStruct((6, d_model), f32),
+                   jax.ShapeDtypeStruct((8, width3), f32), jax.ShapeDtypeStruct((width3, d_model), f32),
+                   jax.ShapeDtypeStruct((width, d_model), f32)],
+        scratch_shapes=[pltpu.VMEM((seq, width3), bf), pltpu.VMEM((width3, d_model), bf), pltpu.VMEM((seq, width), bf),
+                        pltpu.VMEM((2, seq, 256), bf), pltpu.VMEM((2, seq, 256), bf),
+                        pltpu.VMEM((2, width3, 256), f32), pltpu.VMEM((2, width, 256), f32),
+                        pltpu.VMEM((rows, d_model), bf), pltpu.VMEM((rows, d_model), bf), pltpu.VMEM((4, 8, d_model), f32),
+                        pltpu.VMEM((size, 4, d_model), f32), pltpu.VMEM((size, 2, d_model), f32)]
+        + scatter_scratch(size, rows, d_model)
+        + [dma((12,)), dma((Scatter.N_COPIES,)), dma((Scatter.N_COPIES,)), dma((8,)), dma((size,)), dma((size,)), dma((size,)), dma((size,))],
+        compiler_params=comm_params(collective_id),
+        cost_estimate=pl.CostEstimate(flops=4 * seq * width3 * d_model, bytes_accessed=60 * MIB, transcendentals=0),
+        name="scatter_qkv",
+    )(dqkv, wqkv_rows, h1_rel, ctx_rel, dmid_rel, x_in, grad_mid, as_row(gain), sums2)
 
 
 def solution(mesh):
@@ -614,31 +893,17 @@
         size = mesh.shape['tp']
         dz_rel, h2_rel, grad_wfc2 = gather_mlp('tp', size, d_out[0], z_saved[0], w_fc2, x_mid[0], ln2_gain, ln2_bias, 0)
         grad_mid, sums2, bias_sums, grad_wfc1 = scatter_mlp('tp', size, dz_rel, w_fc1, h2_rel, x_mid[0], d_out[0], ln2_gain, 1)
-        grad_mid = grad_mid[None]
-        sums2 = jnp.sum(sums2, axis=1)
+        n_heads, head_dim = q_saved.shape[2:]
+        d_model = d_out.shape[-1]
+        width = n_heads * head_dim
+        dqkv, ctx_rel, dmid_rel, h1_rel = gather_attention('tp', size, grad_mid, q_saved[0], k_saved[0], v_saved[0], w_proj, x_in[0], ln1_gain, ln1_bias, 2)
+        wqkv_rows = jnp.moveaxis(w_qkv, 1, 3).reshape(3 * width, d_model)
+        grad_x, grad_vecs, qkv_bias, dwqkv, dwo = scatter_qkv('tp', size, dqkv, wqkv_rows, h1_rel, ctx_rel, dmid_rel, x_in[0], grad_mid, ln1_gain, sums2, 3)
+        grad_x = grad_x[None]
         grad_bfc1 = jnp.sum(bias_sums, axis=0)
-        mid_full = lax.all_gather(grad_mid, 'tp', axis=1, tiled=True)
-        norm1_hat, norm1_rstd, h1_local = layer_norm_fwd(x_in, ln1_gain, ln1_bias)
-        h1_full = lax.all_gather(h1_local, 'tp', axis=1, tiled=True)
-        mid_rows = mid_full[0]
-        context, grad_q, grad_k, grad_v = attention_grads(q_saved, k_saved, v_saved, mid_rows, w_proj)
-        n_heads, head_dim = q_saved.shape[2:]
-        width = n_heads * head_dim
-        d_model = mid_rows.shape[-1]
-        grad_wproj = jnp.einsum('se,sd->ed', context, mid_rows, preferred_element_type=jnp.float32).reshape(n_heads, head_dim, d_model)
-        qkv_grads = jnp.concatenate([grad_q, grad_k, grad_v], axis=1)
-        wqkv_rows = jnp.moveaxis(w_qkv.reshape(3, d_model, width), 1, 2).reshape(3 * width, d_model)
-        grad_wqkv = jnp.einsum('sd,sie->ide', h1_full[0], qkv_grads.reshape(-1, 3, width), preferred_element_type=jnp.float32).reshape(3, d_model, n_heads, head_dim)
-        grad_bqkv = jnp.sum(qkv_grads, axis=0, dtype=jnp.float32).reshape(3, n_heads, head_dim)
-        h1_partial = jnp.dot(qkv_grads, wqkv_rows, preferred_element_type=jnp.float32).astype(jnp.bfloat16)[None]
-        grad_h1 = lax.psum_scatter(h1_partial, 'tp', scatter_dimension=1, tiled=True).astype(jnp.float32)
-        grad_x = (grad_mid.astype(jnp.float32) + layer_norm_bwd(grad_h1, norm1_hat, norm1_rstd, ln1_gain)).astype(jnp.bfloat16)
-        vec_partial = jnp.stack([
-            jnp.sum(grad_h1 * norm1_hat, axis=(0, 1)),
-            jnp.sum(grad_h1, axis=(0, 1)),
-            sums2[0], sums2[1], sums2[2], sums2[3],
-        ])
-        grad_vecs = lax.psum(vec_partial, 'tp')
+        grad_bqkv = jnp.sum(qkv_bias, axis=0).reshape(3, n_heads, head_dim)
+        grad_wqkv = jnp.moveaxis(dwqkv.reshape(3, n_heads, head_dim, d_model), 3, 1)
+        grad_wproj = dwo.reshape(n_heads, head_dim, d_model)
         return grad_x, grad_wqkv, grad_bqkv, grad_wproj, grad_wfc1, grad_bfc1, grad_wfc2, grad_vecs
 
     tok_spec = P('dp', 'tp', None)

time: 625 us -> 446 us (0.71)
  waiting for transfers between devices: 179 us -> 0 us
  Pallas kernels: 301 us -> 386 us
  matrix products: 49.7 us -> 0 us
  between operations: 13.9 us -> 0.71 us
  other arithmetic: 13.8 us -> 2.2 us
  local copies, waits for them, and re-layouts: 64 us -> 55.1 us
    pallas_call x1 -> x2, Pallas kernels: 111 us -> 197 us  [the longest x1 115 us: gather_attention(): pl.pallas_call(functools.partial(gather_attention_kernel, axis_name, size...]
    all_gather x2 -> x0, waiting for transfers between devices: 82.5 us -> none  [the longest x1 46.4 us: local_backward(): mid_full = lax.all_gather(grad_mid, 'tp', axis=1, tiled=True)]
    reduce_scatter x1 -> x0, waiting for transfers between devices: 65.8 us -> none  [local_backward(): lax.psum_scatter(h1_partial, 'tp', scatter_dimension=1, tiled=True)]
    dot_general x3 -> x0, matrix products: 49.7 us -> none  [the longest x1 21 us: local_backward(): jnp.einsum('sd,sie->ide', h1_full[0], qkv_grads.reshape(-1, 3, width), pr...]
    psum x1 -> x0, waiting for transfers between devices: 30.7 us -> none  [local_backward(): grad_vecs = lax.psum(vec_partial, 'tp')]
    pad x4 -> x0, local copies, waits for them, and re-layouts: 8.83 us -> none  [the longest x3 6.77 us: attention_grads(): jnp.pad(jnp.moveaxis(a[0], 1, 0), ((0, 0), (0, 0), (0, pad)))]
    unnamed x36 -> x25, local copies, waits for them, and re-layouts: 45.8 us -> 54.4 us
    reduce_sum x5 -> x1, other arithmetic: 8.28 us -> 0.79 us  [local_backward(): grad_bqkv = jnp.sum(qkv_bias, axis=0).reshape(3, n_heads, head_dim)]
  transfers between devices with their start and end apart: 4 -> 0, of which waited for: 4 -> 0; matrix products, arithmetic and copies ran while one was open for 11% -> 0% of each run, Pallas kernels for 0% -> 0%
where the time goes in v3:
time: 446 us; the launch traced here: 445 us
  Pallas kernels  386 us (87%)
  local copies, waits for them, and re-layouts  55.1 us (12%)
    pallas_call x1, Pallas kernels, gather_attention(): pl.pallas_call(functools.partial(gather_attention_kernel, axis_name, size...  115 us
    pallas_call x1, Pallas kernels, gather_mlp(): pl.pallas_call(functools.partial(gather_mlp_kernel, axis_name, size), in_...  111 us
    pallas_call x1, Pallas kernels, scatter_qkv(): pl.pallas_call(functools.partial(scatter_qkv_kernel, axis_name, size), in...  81.3 us
    pallas_call x1, Pallas kernels, scatter_mlp(): pl.pallas_call(functools.partial(scatter_mlp_kernel, axis_name, size), in...  78.4 us
    unnamed x25, local copies, waits for them, and re-layouts  54.4 us

profile of v3, /device:TPU:113, one launch (start us, length us, event | category | flops | bytes accessed | tf_op | source)
XLA Modules:
  0.0 444.5 jit_solution(16644542829757396377)
XLA Ops:
  0.6 0.0 copy-start.1
  0.6 0.0 copy-start
  0.7 3.9 copy.23
  4.5 0.0 copy-done
  4.5 2.4 copy.24
  6.9 0.0 copy-done.1
  6.9 2.4 copy.25
  9.3 111.3 %gather_mlp.1 = (bf16[2048,1536]{1,0:T(8,128)(2,1)}, bf16[2048,3072]{1,0:T(8,128)(2,1)}, f32[1536,3072]{1,0:T(8,128)}) custom-call(bf16[256,3072]{1,0:T(8,128)(2,1)} %bitcast.37, bf16[2048,1536]{1,0:T(8,128)(2,1)} %bitcast.35, bf16[1536,3072]{1,0:T(8,128)(2,1)} %w2_ref.1, bf16[256,3072]{1,0:T(8,128)(2,1)} %bitcast.39, f32[1,3072]{1,0:T(1,128)} %bitcast.44, ...), custom_call_target="tpu_custom_call" | custom-call | flops 38654705664 | bytes 62914560 | tf_op jit(solution)/shard_map/gather_mlp/pallas_call | solution.py:350
  120.6 78.4 %scatter_mlp.1 = (bf16[256,3072]{1,0:T(8,128)(2,1)}, f32[4,8,3072]{2,1,0:T(8,128)}, f32[8,1536]{1,0:T(8,128)}, f32[3072,1536]{1,0:T(8,128)}) custom-call(bf16[2048,1536]{1,0:T(8,128)(2,1)} %get-tuple-element.24.dz_ref, bf16[3072,1536]{1,0:T(8,128)(2,1)} %w1_ref.1, bf16[2048,3072]{1,0:T(8,128)(2,1)} %get-tuple-element.25.h2_ref, bf16[256,3072]{1,0:T(8,128)(2,1)} %bitcast.40, ...), custom_call_target="tpu_custom_call" | custom-call | flops 38654705664 | bytes 62914560 | tf_op jit(solution)/shard_map/scatter_mlp/pallas_call | solution.py:500
  199.0 1.4 reduce_sum.19
  200.4 115.5 %gather_attention.1 = (bf16[2048,1152]{1,0:T(8,128)(2,1)}, bf16[2048,384]{1,0:T(8,128)(2,1)}, bf16[2048,3072]{1,0:T(8,128)(2,1)}, bf16[2048,3072]{1,0:T(8,128)(2,1)}) custom-call(bf16[256,3072]{1,0:T(8,128)(2,1)} %get-tuple-element.26.dmid_ref.dmid_own_ref, bf16[4,2048,96]{2,1,0:T(8,128)(2,1)} %bitcast.30, bf16[4,2048,96]{2,1,0:T(8,128)(2,1)} %bitcast.31, ...), custom_call_target="tpu_custom_call" | custom-call | flops 17716740096 | bytes 62914560 | tf_op jit(solution)/shard_map/gather_attention/pallas_call | solution.py:721
  315.9 81.3 %scatter_qkv.1 = (bf16[256,3072]{1,0:T(8,128)(2,1)}, f32[6,3072]{1,0:T(8,128)}, f32[8,1152]{1,0:T(8,128)}, f32[1152,3072]{1,0:T(8,128)}, f32[384,3072]{1,0:T(8,128)}) custom-call(bf16[2048,1152]{1,0:T(8,128)(2,1)} %get-tuple-element.27.dqkv_ref, bf16[1152,3072]{1,0:T(8,128)(2,1)} %bitcast.34, bf16[2048,3072]{1,0:T(8,128)(2,1)} %get-tuple-element.28.h1_ref, ...), custom_call_target="tpu_custom_call" | custom-call | flops 28991029248 | bytes 62914560 | tf_op jit(solution)/shard_map/scatter_qkv/pallas_call | solution.py:871
  397.2 0.8 reduce_sum.18
  398.0 0.7 reshape.52
  398.7 2.7 copy.32
  401.4 12.4 %copy.33 = f32[3,3072,4,96]{1,3,2,0:T(8,128)} copy(f32[3,3072,4,96]{1,3,2,0:T(8,128)} %bitcast.28) | data formatting | bytes 28311552
  413.7 0.0 slice-start
  413.7 5.2 %copy.34 = f32[4,96,3072]{2,1,0:T(8,128)} copy(f32[4,96,3072]{2,1,0:T(8,128)} %bitcast.29) | data formatting | bytes 9437184
  418.9 0.0 slice-start.1
  418.9 0.0 slice-start.2
  418.9 0.0 slice-start.3
  418.9 0.0 slice-start.4
  418.9 16.6 %copy.35 = f32[3072,1536]{1,0:T(8,128)} copy(f32[3072,1536]{1,0:T(8,128)} %get-tuple-element.52) | data formatting | bytes 37748736
  435.5 0.0 slice-done
  435.5 0.0 slice-done.1
  435.5 0.0 slice-done.2
  435.5 0.0 slice-done.3
  435.5 1.5 slice-done.4
  437.0 0.0 copy-start.2
  437.0 6.8 %copy.36 = f32[1536,3072]{1,0:T(8,128)} copy(f32[1536,3072]{1,0:T(8,128)S(1)} %bitcast.27) | data formatting | bytes 37748736
  443.9 0.0 copy-done.2
  443.9 0.6 copy.37
  (1 shorter events, 0.0 us)
Async XLA Ops:
  0.6 6.3 %copy-start.1 = (bf16[1,2048,4,96]{1,3,2,0:T(8,128)(2,1)S(1)}, bf16[1,2048,4,96]{1,3,2,0:T(8,128)(2,1)}, u32[]{:S(2)}) copy-start(bf16[1,2048,4,96]{1,3,2,0:T(8,128)(2,1)} %param.20) | copy-start | bytes 4718596
  0.6 3.9 copy-start
  413.7 21.8 %slice-start = ((s8[18874368]{0:T(1024)(128)(4,1)}), s8[2097152]{0:T(1024)(128)(4,1)S(1)}, s32[]{:S(2)}) async-start(s8[18874368]{0:T(1024)(128)(4,1)} %bitcast.26), calls=%async_computation | async-start | bytes 4194304
  418.9 16.6 %slice-start.1 = ((s8[18874368]{0:T(1024)(128)(4,1)}), s8[4194304]{0:T(1024)(128)(4,1)S(1)}, s32[]{:S(2)}) async-start(s8[18874368]{0:T(1024)(128)(4,1)} %bitcast.26), calls=%async_computation.1 | async-start | bytes 8388608
  418.9 16.6 %slice-start.2 = ((s8[18874368]{0:T(1024)(128)(4,1)}), s8[4194304]{0:T(1024)(128)(4,1)S(1)}, s32[]{:S(2)}) async-start(s8[18874368]{0:T(1024)(128)(4,1)} %bitcast.26), calls=%async_computation.2 | async-start | bytes 8388608
  418.9 16.6 %slice-start.3 = ((s8[18874368]{0:T(1024)(128)(4,1)}), s8[4194304]{0:T(1024)(128)(4,1)S(1)}, s32[]{:S(2)}) async-start(s8[18874368]{0:T(1024)(128)(4,1)} %bitcast.26), calls=%async_computation.3 | async-start | bytes 8388608
  418.9 18.1 %slice-start.4 = ((s8[18874368]{0:T(1024)(128)(4,1)}), s8[4194304]{0:T(1024)(128)(4,1)S(1)}, s32[]{:S(2)}) async-start(s8[18874368]{0:T(1024)(128)(4,1)} %bitcast.26), calls=%async_computation.4 | async-start | bytes 8388608
  437.0 6.9 %copy-start.2 = (f32[6,3072]{1,0:T(8,128)S(1)}, f32[6,3072]{1,0:T(8,128)}, u32[]{:S(2)}) copy-start(f32[6,3072]{1,0:T(8,128)} %get-tuple-element.55) | copy-start | bytes 221188

commit v4 on v3

--- a/solution.py
+++ b/solution.py
@@ -40,6 +40,7 @@
 
 
 MIB = 2 ** 20
+PARTS = range(2)
 
 
 def loop(count, body):
@@ -52,6 +53,10 @@
 
 def span(i, n):
     return pl.ds(pl.multiple_of(i * n, n), n)
+
+
+def local_copies(pairs, sems):
+    return [pltpu.make_async_copy(src, dst, sems.at[i]) for i, (src, dst) in enumerate(pairs)]
 
 
 def as_row(vec):
@@ -126,8 +131,8 @@
 class Gather:
     N_COPIES = 13
 
-    def __init__(self, ring, src, dst, send_sem, recv_sem):
-        self.ring, self.src, self.dst, self.send_sem, self.recv_sem = ring, src, dst, send_sem, recv_sem
+    def __init__(self, ring, src, dst, send_sem, recv_sem, relay=True):
+        self.ring, self.src, self.dst, self.send_sem, self.recv_sem, self.relay = ring, src, dst, send_sem, recv_sem, relay
         self.rows = src.shape[0]
         self.half = self.rows // 2
 
@@ -169,7 +174,9 @@
 
     def first_halves(self):
         self.recv(1, 3)
-        self.send(5, 6, 7, 8)
+        if self.relay:
+            self.send(5, 6)
+        self.send(7, 8)
 
     def second_halves(self):
         self.recv(2, 4)
@@ -181,7 +188,42 @@
 
     def drain(self):
         for idx in range(self.N_COPIES):
-            self.descriptor(idx).wait_send()
+            if self.relay or idx not in (5, 6, 11, 12):
+                self.descriptor(idx).wait_send()
+
+
+class Relay:
+    N_COPIES = 4
+
+    def __init__(self, ring, gathered, dst, send_sem, recv_sem):
+        self.ring, self.gathered, self.dst, self.send_sem, self.recv_sem = ring, gathered, dst, send_sem, recv_sem
+        self.rows = dst.shape[0] // 2
+        self.half = self.rows // 2
+
+    def descriptor(self, idx):
+        half = idx % 2
+        dst = self.dst.at[pl.ds(half * self.half, self.half)]
+        if idx < 2:
+            rel, peer = ((LEFT, self.ring.right), (RIGHT, self.ring.left))[half]
+            src = self.gathered.at[pl.ds(rel * self.rows + half * self.half, self.half)]
+        else:
+            src, dst, peer = dst, self.dst.at[pl.ds(self.rows + half * self.half, self.half)], self.ring.partner
+        return self.ring.copy(src, dst, self.send_sem.at[idx], self.recv_sem.at[idx], peer)
+
+    def run(self, kind, *ids):
+        for idx in ids:
+            getattr(self.descriptor(idx), kind)()
+
+    def start(self):
+        self.run("start", 0, 1)
+
+    def forward(self):
+        self.run("wait_recv", 0, 1)
+        self.run("start", 2, 3)
+
+    def finish(self):
+        self.run("wait_recv", 2, 3)
+        self.run("wait_send", 0, 1, 2, 3)
 
 
 class Scatter:
@@ -191,16 +233,22 @@
         self.ring, self.partial, self.peer_part, self.outbox, self.inbox = ring, partial, peer_part, outbox, inbox
         self.send_sem, self.recv_sem = send_sem, recv_sem
         self.rows = partial.shape[0] // ring.size
+        self.cols = partial.shape[1] // 2
         self.half = self.rows // 2
 
     def piece(self, rel, half):
         return pl.ds(rel * self.rows + half * self.half, self.half)
 
-    def swap(self, rel):
-        idx = 6 + rel // 2
-        rows = pl.ds((rel + 1) * self.rows, self.rows)
-        return self.ring.copy(self.partial.at[rows], self.peer_part.at[pl.ds(rel // 2 * self.rows, self.rows)],
+    def swap(self, rel, part):
+        idx = 6 + rel + part
+        rows, cols = pl.ds((rel + 1) * self.rows, self.rows), pl.ds(part * self.cols, self.cols)
+        return self.ring.copy(self.partial.at[rows, cols], self.peer_part.at[pl.ds(rel // 2 * self.rows, self.rows), cols],
                               self.send_sem.at[idx], self.recv_sem.at[idx], self.ring.partner)
+
+    def swapped(self, *rels):
+        for rel in rels:
+            for part in PARTS:
+                self.swap(rel, part).wait_recv()
 
     def hop(self, idx):
         peer = self.ring.right if idx % 2 == 0 else self.ring.left
@@ -216,13 +264,12 @@
         self.hop(idx).start()
 
     def send_opposite(self):
-        self.swap(OPP).wait_recv()
+        self.swapped(OPP)
         self.put(0, self.chip_sum(OPP, 0))
         self.put(1, self.chip_sum(OPP, 1))
 
     def send_direct(self):
-        self.swap(LEFT).wait_recv()
-        self.swap(RIGHT).wait_recv()
+        self.swapped(LEFT, RIGHT)
         self.put(2, self.chip_sum(RIGHT, 1))
         self.put(3, self.chip_sum(LEFT, 0))
 
@@ -233,7 +280,7 @@
         self.put(5, self.chip_sum(LEFT, 1) + self.inbox[1].astype(jnp.float32))
 
     def arrive(self):
-        self.swap(OWN).wait_recv()
+        self.swapped(OWN)
         for idx in (2, 3, 4, 5):
             self.hop(idx).wait_recv()
 
@@ -246,26 +293,24 @@
         for idx in range(6):
             self.hop(idx).wait_send()
         for rel in (OWN, LEFT, RIGHT, OPP):
-            self.swap(rel).wait_send()
+            for part in PARTS:
+                self.swap(rel, part).wait_send()
 
 
 def gather_mlp_kernel(axis_name, size, dout_ref, z_ref, w2_ref, xmid_ref, gain_ref, bias_ref,
                       dz_hbm, h2_hbm, dw2_hbm,
-                      dout_all, zu, dz, w2, xmid, h2, dw2_tile, local_sem, send_sem, recv_sem, h2_send_sem, h2_recv_sem, out_sem):
+                      dout_all, zu, dz, w2, xmid, h2, dw2_tile, local_sem, send_sem, recv_sem, h2_send_sem, h2_recv_sem, out_sem, own_sem):
     ring = Ring(axis_name, size)
     rows = dout_ref.shape[0]
     units = w2.shape[0]
     ring.barrier()
     gather = Gather(ring, dout_ref, dout_all, send_sem, recv_sem)
     gather.start()
-    own_copy = pltpu.make_async_copy(dout_ref, gather.block(OWN), local_sem.at[0])
-    w2_copy = pltpu.make_async_copy(w2_ref, w2, local_sem.at[1])
-    xmid_copy = pltpu.make_async_copy(xmid_ref, xmid, local_sem.at[2])
+    owners = [ring.block_owner(rel) for rel in range(size)]
+    own_copy, w2_copy, xmid_copy, *z_copies = local_copies(
+        [(dout_ref, gather.block(OWN)), (w2_ref, w2), (xmid_ref, xmid)]
+        + [(z_ref.at[span(owner, rows)], zu.at[pl.ds(rel * rows, rows)]) for rel, owner in enumerate(owners)], local_sem)
     own_copy.start()
-    z_copies = []
-    for rel in range(size):
-        src = z_ref.at[span(ring.block_owner(rel), rows)]
-        z_copies.append(pltpu.make_async_copy(src, zu.at[pl.ds(rel * rows, rows)], local_sem.at[4 + rel]))
     xmid_copy.start()
     w2_copy.start()
     for copy in z_copies:
@@ -273,8 +318,8 @@
 
     xmid_copy.wait()
     norm_block(xmid, gain_ref, bias_ref, h2)
-    h2_gather = Gather(ring, h2, h2_hbm, h2_send_sem, h2_recv_sem)
-    h2_own = pltpu.make_async_copy(h2, h2_gather.block(OWN), local_sem.at[3])
+    h2_gather = Gather(ring, h2, h2_hbm, h2_send_sem, h2_recv_sem, relay=False)
+    h2_own = pltpu.make_async_copy(h2, h2_gather.block(OWN), own_sem)
     h2_own.start()
 
     pair, tile = 2 * rows, 256
@@ -336,8 +381,7 @@
         copy.wait()
     for i in (n_tiles - 2, n_tiles - 1):
         dw2_copy(i, i % 2).wait()
-    h2_gather.opposite()
-    h2_gather.recv(0, 7, 8, 9, 10, 11, 12)
+    h2_gather.recv(0, 7, 8, 9, 10)
     gather.drain()
     h2_gather.drain()
 
@@ -351,12 +395,12 @@
         functools.partial(gather_mlp_kernel, axis_name, size),
         in_specs=[ANY] * 4 + [vm, vm],
         out_specs=[ANY] * 3,
-        out_shape=[jax.ShapeDtypeStruct((seq, units), bf), jax.ShapeDtypeStruct((seq, d_model), bf),
+        out_shape=[jax.ShapeDtypeStruct((seq, units), bf), jax.ShapeDtypeStruct((seq - 2 * rows, d_model), bf),
                    jax.ShapeDtypeStruct((units, d_model), f32)],
         scratch_shapes=[pltpu.VMEM((seq, d_model), bf), pltpu.VMEM((seq, units), bf), pltpu.VMEM((seq, units), bf),
                         pltpu.VMEM((units, d_model), bf), pltpu.VMEM((rows, d_model), bf), pltpu.VMEM((rows, d_model), bf),
                         pltpu.VMEM((2, 256, d_model), f32), dma((4 + size,)),
-                        dma((Gather.N_COPIES,)), dma((Gather.N_COPIES,)), dma((Gather.N_COPIES,)), dma((Gather.N_COPIES,)), dma((6,))],
+                        dma((Gather.N_COPIES,)), dma((Gather.N_COPIES,)), dma((Gather.N_COPIES,)), dma((Gather.N_COPIES,)), dma((6,)), dma(())],
         compiler_params=comm_params(collective_id),
         cost_estimate=pl.CostEstimate(flops=4 * seq * units * d_model, bytes_accessed=60 * MIB, transcendentals=seq * units),
         name="gather_mlp",
@@ -365,16 +409,18 @@
 
 def scatter_grads(ring, stage_fn, partial, peer_part, outbox, inbox, send_sem, recv_sem):
     scatter = Scatter(ring, partial, peer_part, outbox, inbox, send_sem, recv_sem)
-    stage_fn(OPP)
-    scatter.swap(OPP).start()
+
+    def stage(rel):
+        for part in PARTS:
+            stage_fn(rel, part)
+            scatter.swap(rel, part).start()
+
+    stage(OPP)
     scatter.send_opposite()
-    stage_fn(LEFT)
-    scatter.swap(LEFT).start()
-    stage_fn(RIGHT)
-    scatter.swap(RIGHT).start()
+    stage(LEFT)
+    stage(RIGHT)
     scatter.send_direct()
-    stage_fn(OWN)
-    scatter.swap(OWN).start()
+    stage(OWN)
     scatter.send_relayed()
     return scatter
 
@@ -390,7 +436,7 @@
             total = total + vals[i * 8:(i + 1) * 8]
         return total
 
-    for part in range(2):
+    for part in PARTS:
         def body(i):
             inner = span(i, chunk)
             sl = span(part * (half // chunk) + i, chunk)
@@ -416,40 +462,47 @@
 
 def scatter_mlp_kernel(axis_name, size, dz_ref, w1_ref, h2_ref, xmid_ref, dout_ref, gain_ref,
                        dmid_ref, sums_ref, dbfc1_ref, dw1_hbm,
-                       dz, w1, h2_tile, dw1_tile, xmid, dout, partial, peer_part, outbox, inbox,
-                       local_sem, send_sem, recv_sem, tile_sem):
+                       dz, w1, h2_tile, dw1_tile, xmid, dout, h2_opp, partial, peer_part, outbox, inbox,
+                       local_sem, send_sem, recv_sem, tile_sem, relay_send, relay_recv):
     ring = Ring(axis_name, size)
     rows = xmid.shape[0]
     d_model, units = w1.shape
     pair, tile = 2 * rows, 256
+    near = h2_ref.shape[0]
     ring.barrier()
-    dz_copies = {}
-    for rel in (OPP, LEFT, RIGHT, OWN):
-        sl = pl.ds(rel * rows, pair)
-        dz_copies[rel] = pltpu.make_async_copy(dz_ref.at[sl], dz.at[sl], local_sem.at[rel // 2])
-    w1_copy = pltpu.make_async_copy(w1_ref, w1, local_sem.at[4])
-    xmid_copy = pltpu.make_async_copy(xmid_ref, xmid, local_sem.at[5])
-    dout_copy = pltpu.make_async_copy(dout_ref, dout, local_sem.at[6])
+    relay = Relay(ring, h2_ref, h2_opp, relay_send, relay_recv)
+    relay.start()
+    w1_half = d_model // 2
+    halves = [pl.ds(part * w1_half, w1_half) for part in PARTS]
+    xmid_copy, dout_copy, *copies = local_copies(
+        [(xmid_ref, xmid), (dout_ref, dout)] + [(w1_ref.at[sl], w1.at[sl]) for sl in halves]
+        + [(dz_ref.at[pl.ds(rel * rows, pair)], dz.at[pl.ds(rel * rows, pair)]) for rel in (OWN, LEFT, RIGHT, OPP)], local_sem)
+    w1_copies, dz_copies = copies[:len(halves)], dict(zip((OWN, LEFT, RIGHT, OPP), copies[len(halves):]))
     dz_copies[OPP].start()
-    w1_copy.start()
+    for copy in w1_copies:
+        copy.start()
     for rel in (LEFT, RIGHT, OWN):
         dz_copies[rel].start()
     xmid_copy.start()
     dout_copy.start()
-    w1_copy.wait()
-
-    def stage(rel):
-        dz_copies[rel].wait()
+    tiles_per_part = w1_half // tile
+
+    def stage(rel, part):
+        if part == 0:
+            dz_copies[rel].wait()
+        if rel == OPP:
+            w1_copies[part].wait()
         sl = pl.ds(rel * rows, pair)
 
         def body(n):
-            cols = span(n, tile)
+            cols = span(part * tiles_per_part + n, tile)
             partial[sl, cols] = dot(dz[sl, :], w1[cols, :], NT).astype(jnp.bfloat16)
 
-        loop(d_model // tile, body)
+        loop(tiles_per_part, body)
 
     scatter = scatter_grads(ring, stage, partial, peer_part, outbox, inbox, send_sem, recv_sem)
 
+    relay.forward()
     n_tiles = d_model // tile
 
     def tile_in(i, slot):
@@ -459,6 +512,7 @@
         return pltpu.make_async_copy(dw1_tile.at[slot], dw1_hbm.at[span(i, tile)], tile_sem.at[2 + slot])
 
     tile_in(0, 0).start()
+    relay.finish()
 
     def dw1_body(i):
         slot = i % 2
@@ -472,7 +526,7 @@
             tile_out(i - 2, slot).wait()
 
         tile_in(i, slot).wait()
-        dw1_tile[slot] = dot(h2_tile[slot], dz[...], TN)
+        dw1_tile[slot] = dot(h2_tile[slot], dz[pl.ds(0, near), :], TN) + dot(h2_opp[:, span(i, tile)], dz[pl.ds(near, pair), :], TN)
         tile_out(i, slot).start()
 
     loop(n_tiles, dw1_body)
@@ -503,10 +557,11 @@
         out_specs=[vm, vm, vm, ANY],
         out_shape=[jax.ShapeDtypeStruct((rows, d_model), bf), jax.ShapeDtypeStruct((4, 8, d_model), f32),
                    jax.ShapeDtypeStruct((8, units), f32), jax.ShapeDtypeStruct((d_model, units), f32)],
-        scratch_shapes=[pltpu.VMEM((seq, units), bf), pltpu.VMEM((d_model, units), bf), pltpu.VMEM((2, seq, 256), bf),
-                        pltpu.VMEM((2, 256, units), f32), pltpu.VMEM((rows, d_model), bf), pltpu.VMEM((rows, d_model), bf)]
+        scratch_shapes=[pltpu.VMEM((seq, units), bf), pltpu.VMEM((d_model, units), bf), pltpu.VMEM((2, seq - 2 * rows, 256), bf),
+                        pltpu.VMEM((2, 256, units), f32), pltpu.VMEM((rows, d_model), bf), pltpu.VMEM((rows, d_model), bf),
+                        pltpu.VMEM((2 * rows, d_model), bf)]
         + scatter_scratch(size, rows, d_model)
-        + [dma((7,)), dma((Scatter.N_COPIES,)), dma((Scatter.N_COPIES,)), dma((4,))],
+        + [dma((9,)), dma((Scatter.N_COPIES,)), dma((Scatter.N_COPIES,)), dma((4,)), dma((Relay.N_COPIES,)), dma((Relay.N_COPIES,))],
         compiler_params=comm_params(collective_id),
         cost_estimate=pl.CostEstimate(flops=4 * seq * units * d_model, bytes_accessed=60 * MIB, transcendentals=0),
         name="scatter_mlp",
@@ -531,7 +586,7 @@
                             dqkv_hbm, ctx_hbm, dmid_hbm, h1_hbm,
                             dmid, q_all, k_all, v_all, wo, xin, h1, s_scr, dp_scr, dk_acc, dv_acc, dctx_scr, ctx_scr, dq_scr,
                             m_scr, l_scr, d_scr, rows_out, pack_out,
-                            local_sem, send_sem, recv_sem, h1_send_sem, h1_recv_sem, out_sem):
+                            local_sem, send_sem, recv_sem, h1_send_sem, h1_recv_sem, out_sem, own_sem):
     ring = Ring(axis_name, size)
     rows = xin.shape[0]
     n_heads = q_all.shape[0]
@@ -542,9 +597,7 @@
     ring.barrier()
     gather = Gather(ring, dmid_ref, dmid, send_sem, recv_sem)
     gather.start()
-    own_copy = pltpu.make_async_copy(dmid_ref, gather.block(OWN), local_sem.at[0])
-    loads = [pltpu.make_async_copy(src, dst, local_sem.at[1 + i])
-             for i, (src, dst) in enumerate(((xin_ref, xin), (wo_ref, wo), (v_ref, v_all), (k_ref, k_all), (q_ref, q_all)))]
+    own_copy, *loads = local_copies([(dmid_ref, gather.block(OWN)), (xin_ref, xin), (wo_ref, wo), (v_ref, v_all), (k_ref, k_all), (q_ref, q_all)], local_sem)
     own_copy.start()
     for copy in loads:
         copy.start()
@@ -552,8 +605,8 @@
     dv_acc[...] = jnp.zeros_like(dv_acc)
     loads[0].wait()
     norm_block(xin, gain_ref, bias_ref, h1)
-    h1_gather = Gather(ring, h1, h1_hbm, h1_send_sem, h1_recv_sem)
-    h1_own = pltpu.make_async_copy(h1, h1_gather.block(OWN), local_sem.at[6])
+    h1_gather = Gather(ring, h1, h1_hbm, h1_send_sem, h1_recv_sem, relay=False)
+    h1_own = pltpu.make_async_copy(h1, h1_gather.block(OWN), own_sem)
     h1_own.start()
     own_copy.wait()
     for copy in loads[1:]:
@@ -690,10 +743,9 @@
         pack_out[1, sl, :] = pack(dv_acc, sl)
 
     loop(size, pack_body)
-    packed = [pltpu.make_async_copy(pack_out.at[part], dqkv_hbm.at[:, pl.ds((1 + part) * width, width)], out_sem.at[12 + part]) for part in range(2)]
+    packed = [pltpu.make_async_copy(pack_out.at[part], dqkv_hbm.at[:, pl.ds((1 + part) * width, width)], out_sem.at[12 + part]) for part in PARTS]
     for copy in packed:
         copy.start()
-    h1_gather.opposite()
     for r in (size - 2, size - 1):
         ctx_out(r).wait()
         dq_out(r).wait()
@@ -702,7 +754,7 @@
     for copy in packed:
         copy.wait()
     h1_own.wait()
-    h1_gather.recv(0, 7, 8, 9, 10, 11, 12)
+    h1_gather.recv(0, 7, 8, 9, 10)
     gather.drain()
     h1_gather.drain()
 
@@ -723,14 +775,14 @@
         in_specs=[ANY] * 6 + [vm, vm],
         out_specs=[ANY] * 4,
         out_shape=[jax.ShapeDtypeStruct((seq, 3 * width), bf), jax.ShapeDtypeStruct((seq, width), bf),
-                   jax.ShapeDtypeStruct((seq, d_model), bf), jax.ShapeDtypeStruct((seq, d_model), bf)],
+                   jax.ShapeDtypeStruct((seq, d_model), bf), jax.ShapeDtypeStruct((seq - 2 * rows, d_model), bf)],
         scratch_shapes=[pltpu.VMEM((seq, d_model), bf), heads, heads, heads, pltpu.VMEM((width, d_model), bf),
                         pltpu.VMEM((rows, d_model), bf), pltpu.VMEM((rows, d_model), bf),
                         acc(2, size, rows, rows), acc(2, size, rows, rows), acc(n_heads, seq, head_dim), acc(n_heads, seq, head_dim),
                         pltpu.VMEM((n_heads, rows, head_dim), bf), acc(n_heads, rows, head_dim), acc(n_heads, rows, head_dim),
                         acc(2, rows, LANES), acc(2, rows, LANES), acc(2, rows, LANES),
                         pltpu.VMEM((2, 2, rows, width), bf), pltpu.VMEM((2, seq, width), bf),
-                        dma((7,)), dma((Gather.N_COPIES,)), dma((Gather.N_COPIES,)), dma((Gather.N_COPIES,)), dma((Gather.N_COPIES,)), dma((14,))],
+                        dma((7,)), dma((Gather.N_COPIES,)), dma((Gather.N_COPIES,)), dma((Gather.N_COPIES,)), dma((Gather.N_COPIES,)), dma((14,)), dma(())],
         compiler_params=comm_params(collective_id),
         cost_estimate=pl.CostEstimate(flops=flops, bytes_accessed=60 * MIB, transcendentals=n_heads * seq * seq // 2),
         name="gather_attention",
@@ -743,9 +795,9 @@
 
 def scatter_qkv_kernel(axis_name, size, dqkv_ref, wqkv_ref, h1_ref, ctx_ref, dmid_ref, xin_ref, dmid_own_ref, gain_ref, sums2_ref,
                        gradx_ref, vecs_ref, dbqkv_ref, dwqkv_hbm, dwo_hbm,
-                       dqkv, wqkv, ctx, h1_tile, dmid_tile, dwqkv_tile, dwo_tile, xin, dmid_own, sums1, early_box, late_box,
+                       dqkv, wqkv, ctx, h1_tile, dmid_tile, dwqkv_tile, dwo_tile, xin, dmid_own, h1_opp, sums1, early_box, late_box,
                        partial, peer_part, outbox, inbox,
-                       local_sem, send_sem, recv_sem, tile_sem, early_send, early_recv, late_send, late_recv):
+                       local_sem, send_sem, recv_sem, tile_sem, relay_send, relay_recv, early_send, early_recv, late_send, late_recv):
     ring = Ring(axis_name, size)
     rows = xin.shape[0]
     d_model = wqkv.shape[1]
@@ -754,20 +806,23 @@
     for step in range(1, size):
         pl.semaphore_signal(sem, inc=1, device_id={axis_name: (ring.me + step) % size}, device_id_type=MESH_IDS)
     pl.semaphore_wait(sem, size - 1)
-
-    dqkv_copies = {}
-    for rel in (6, 7, 2, 3, 4, 5, 0, 1):
-        src = dqkv_ref.at[span(ring.block_owner(rel), rows)]
-        dqkv_copies[rel] = pltpu.make_async_copy(src, dqkv.at[pl.ds(rel * rows, rows)], local_sem.at[rel])
-    w_copy = pltpu.make_async_copy(wqkv_ref, wqkv, local_sem.at[8])
-    ctx_copy = pltpu.make_async_copy(ctx_ref, ctx, local_sem.at[9])
-    xin_copy = pltpu.make_async_copy(xin_ref, xin, local_sem.at[10])
-    own_copy = pltpu.make_async_copy(dmid_own_ref, dmid_own, local_sem.at[11])
-    dqkv_copies[6].start()
-    dqkv_copies[7].start()
-    w_copy.start()
-    for rel in (2, 3, 4, 5, 0, 1):
-        dqkv_copies[rel].start()
+    relay = Relay(ring, h1_ref, h1_opp, relay_send, relay_recv)
+    relay.start()
+    near = h1_ref.shape[0]
+
+    w_half = d_model // 2
+    halves = [pl.ds(part * w_half, w_half) for part in PARTS]
+    owners = [ring.block_owner(rel) for rel in range(size)]
+    ctx_copy, xin_copy, own_copy, *copies = local_copies(
+        [(ctx_ref, ctx), (xin_ref, xin), (dmid_own_ref, dmid_own)] + [(wqkv_ref.at[:, sl], wqkv.at[:, sl]) for sl in halves]
+        + [(dqkv_ref.at[span(owner, rows)], dqkv.at[pl.ds(rel * rows, rows)]) for rel, owner in enumerate(owners)], local_sem)
+    w_copies, dqkv_copies = copies[:len(halves)], copies[len(halves):]
+    for copy in dqkv_copies[OPP:]:
+        copy.start()
+    for copy in w_copies:
+        copy.start()
+    for copy in dqkv_copies[LEFT:OPP] + dqkv_copies[:LEFT]:
+        copy.start()
     for copy in (ctx_copy, xin_copy, own_copy):
         copy.start()
 
@@ -780,23 +835,26 @@
 
     for i in range(4):
         early_box[ring.me, pl.ds(i, 1), :] = sum_rows8(sums2_ref[i])
-    w_copy.wait()
-
-    def stage(rel):
-        dqkv_copies[rel].wait()
-        dqkv_copies[rel + 1].wait()
+    tiles_per_part = w_half // tile
+
+    def stage(rel, part):
+        if part == 0:
+            dqkv_copies[rel].wait()
+            dqkv_copies[rel + 1].wait()
+        if rel == OPP:
+            w_copies[part].wait()
         sl = pl.ds(rel * rows, pair)
 
         def body(n):
-            cols = span(n, tile)
+            cols = span(part * tiles_per_part + n, tile)
             partial[sl, cols] = dot(dqkv[sl, :], wqkv[:, cols], NN).astype(jnp.bfloat16)
 
-        loop(d_model // tile, body)
+        loop(tiles_per_part, body)
 
     scatter = scatter_grads(ring, stage, partial, peer_part, outbox, inbox, send_sem, recv_sem)
     for step in range(1, size):
         share(early_box, early_send, early_recv, step).start()
-
+    relay.forward()
     n_tiles = d_model // tile
 
     def tile_in(i, slot):
@@ -812,6 +870,7 @@
     for copy in tile_in(0, 0):
         copy.start()
     ctx_copy.wait()
+    relay.finish()
 
     def dw_body(i):
         slot = i % 2
@@ -828,7 +887,7 @@
 
         for copy in tile_in(i, slot):
             copy.wait()
-        dwqkv_tile[slot] = dot(dqkv[...], h1_tile[slot], TN)
+        dwqkv_tile[slot] = dot(dqkv[pl.ds(0, near), :], h1_tile[slot], TN) + dot(dqkv[pl.ds(near, pair), :], h1_opp[:, span(i, tile)], TN)
         dwo_tile[slot] = dot(ctx[...], dmid_tile[slot], TN)
         for copy in tile_out(i, slot):
             copy.start()
@@ -842,7 +901,7 @@
     own_copy.wait()
     scatter.arrive()
     norm_backward(scatter, rows, xin, dmid_own, gain_ref, gradx_ref, sums1)
-    for i in range(2):
+    for i in PARTS:
         late_box[ring.me, pl.ds(i, 1), :] = sum_rows8(sums1[i])
     for step in range(1, size):
         share(late_box, late_send, late_recv, step).start()
@@ -876,16 +935,47 @@
                    jax.ShapeDtypeStruct((8, width3), f32), jax.ShapeDtypeStruct((width3, d_model), f32),
                    jax.ShapeDtypeStruct((width, d_model), f32)],
         scratch_shapes=[pltpu.VMEM((seq, width3), bf), pltpu.VMEM((width3, d_model), bf), pltpu.VMEM((seq, width), bf),
-                        pltpu.VMEM((2, seq, 256), bf), pltpu.VMEM((2, seq, 256), bf),
+                        pltpu.VMEM((2, seq - 2 * rows, 256), bf), pltpu.VMEM((2, seq, 256), bf),
                         pltpu.VMEM((2, width3, 256), f32), pltpu.VMEM((2, width, 256), f32),
-                        pltpu.VMEM((rows, d_model), bf), pltpu.VMEM((rows, d_model), bf), pltpu.VMEM((4, 8, d_model), f32),
+                        pltpu.VMEM((rows, d_model), bf), pltpu.VMEM((rows, d_model), bf), pltpu.VMEM((2 * rows, d_model), bf), pltpu.VMEM((4, 8, d_model), f32),
                         pltpu.VMEM((size, 4, d_model), f32), pltpu.VMEM((size, 2, d_model), f32)]
         + scatter_scratch(size, rows, d_model)
-        + [dma((12,)), dma((Scatter.N_COPIES,)), dma((Scatter.N_COPIES,)), dma((8,)), dma((size,)), dma((size,)), dma((size,)), dma((size,))],
+        + [dma((17,)), dma((Scatter.N_COPIES,)), dma((Scatter.N_COPIES,)), dma((8,)), dma((Relay.N_COPIES,)), dma((Relay.N_COPIES,)), dma((size,)), dma((size,)), dma((size,)), dma((size,))],
         compiler_params=comm_params(collective_id),
         cost_estimate=pl.CostEstimate(flops=4 * seq * width3 * d_model, bytes_accessed=60 * MIB, transcendentals=0),
         name="scatter_qkv",
     )(dqkv, wqkv_rows, h1_rel, ctx_rel, dmid_rel, x_in, grad_mid, as_row(gain), sums2)
+
+
+def emit_kernel(n_parts, *refs):
+    n = len(n_parts)
+    srcs, dsts, bufs, sems = refs[:n], refs[n:2 * n], refs[2 * n:3 * n], refs[3 * n:]
+    moves = []
+    for src, dst, buf, sem, parts in zip(srcs, dsts, bufs, sems, n_parts):
+        rows = src.shape[0] // parts
+        for i in range(parts):
+            sl = pl.ds(i * rows, rows)
+            moves.append((pltpu.make_async_copy(src.at[sl], buf.at[sl], sem.at[0, i]),
+                          pltpu.make_async_copy(buf.at[sl], dst.at[sl], sem.at[1, i])))
+    for load, _ in moves:
+        load.start()
+    for load, store in moves:
+        load.wait()
+        store.start()
+    for _, store in moves:
+        store.wait()
+
+
+def emit(arrays, n_parts):
+    return pl.pallas_call(
+        functools.partial(emit_kernel, n_parts),
+        in_specs=[ANY] * len(arrays),
+        out_specs=[ANY] * len(arrays),
+        out_shape=[jax.ShapeDtypeStruct(a.shape, a.dtype) for a in arrays],
+        scratch_shapes=[pltpu.VMEM(a.shape, a.dtype) for a in arrays] + [pltpu.SemaphoreType.DMA((2, parts)) for parts in n_parts],
+        compiler_params=pltpu.CompilerParams(vmem_limit_bytes=63 * MIB),
+        name="emit",
+    )(*arrays)
 
 
 def solution(mesh):
@@ -899,6 +989,7 @@
         dqkv, ctx_rel, dmid_rel, h1_rel = gather_attention('tp', size, grad_mid, q_saved[0], k_saved[0], v_saved[0], w_proj, x_in[0], ln1_gain, ln1_bias, 2)
         wqkv_rows = jnp.moveaxis(w_qkv, 1, 3).reshape(3 * width, d_model)
         grad_x, grad_vecs, qkv_bias, dwqkv, dwo = scatter_qkv('tp', size, dqkv, wqkv_rows, h1_rel, ctx_rel, dmid_rel, x_in[0], grad_mid, ln1_gain, sums2, 3)
+        grad_wfc2, grad_wfc1, dwqkv, dwo, grad_x, grad_vecs = emit((grad_wfc2, grad_wfc1, dwqkv, dwo, grad_x, grad_vecs), (8, 8, 6, 2, 1, 1))
         grad_x = grad_x[None]
         grad_bfc1 = jnp.sum(bias_sums, axis=0)
         grad_bqkv = jnp.sum(qkv_bias, axis=0).reshape(3, n_heads, head_dim)

time: 446 us -> 423 us (0.948)
  local copies, waits for them, and re-layouts: 55.1 us -> 9.33 us
  Pallas kernels: 386 us -> 410 us
    unnamed x25 -> x9, local copies, waits for them, and re-layouts: 54.4 us -> 8.65 us
    pallas_call x0 -> x1, Pallas kernels: none -> 36.1 us  [emit(): pl.pallas_call(functools.partial(emit_kernel, n_parts), in_specs=[ANY] *...]
    pallas_call x1, Pallas kernels: 111 us -> 94.5 us  [gather_mlp(): pl.pallas_call(functools.partial(gather_mlp_kernel, axis_name, size), in_...]
    pallas_call x1, Pallas kernels: 81.3 us -> 87.3 us  [scatter_qkv(): pl.pallas_call(functools.partial(scatter_qkv_kernel, axis_name, size), in...]
where the time goes in v4:
time: 423 us; the launch traced here: 422 us
  Pallas kernels  410 us (97%)
  local copies, waits for them, and re-layouts  9.33 us (2%)
    pallas_call x1, Pallas kernels, gather_attention(): pl.pallas_call(functools.partial(gather_attention_kernel, axis_name, size...  113 us
    pallas_call x1, Pallas kernels, gather_mlp(): pl.pallas_call(functools.partial(gather_mlp_kernel, axis_name, size), in_...  94.5 us
    pallas_call x1, Pallas kernels, scatter_qkv(): pl.pallas_call(functools.partial(scatter_qkv_kernel, axis_name, size), in...  87.3 us
    pallas_call x1, Pallas kernels, scatter_mlp(): pl.pallas_call(functools.partial(scatter_mlp_kernel, axis_name, size), in...  79.1 us
    pallas_call x1, Pallas kernels, emit(): pl.pallas_call(functools.partial(emit_kernel, n_parts), in_specs=[ANY] *...  36.1 us
    unnamed x9, local copies, waits for them, and re-layouts  8.65 us

profile of v4, /device:TPU:113, one launch (start us, length us, event | category | flops | bytes accessed | tf_op | source)
XLA Modules:
  0.0 421.9 jit_solution(665769205281453308)
XLA Ops:
  0.6 0.0 copy-start.1
  0.6 0.0 copy-start
  0.7 3.9 copy.23
  4.5 0.0 copy-done
  4.5 2.4 copy.24
  6.9 0.0 copy-done.1
  6.9 2.4 copy.25
  9.3 94.5 %gather_mlp.1 = (bf16[2048,1536]{1,0:T(8,128)(2,1)}, bf16[1536,3072]{1,0:T(8,128)(2,1)}, f32[1536,3072]{1,0:T(8,128)}) custom-call(bf16[256,3072]{1,0:T(8,128)(2,1)} %bitcast.34, bf16[2048,1536]{1,0:T(8,128)(2,1)} %bitcast.31, bf16[1536,3072]{1,0:T(8,128)(2,1)} %w2_ref.1, bf16[256,3072]{1,0:T(8,128)(2,1)} %bitcast.36, f32[1,3072]{1,0:T(1,128)} %bitcast.42, ...), custom_call_target="tpu_custom_call" | custom-call | flops 38654705664 | bytes 62914560 | tf_op jit(solution)/shard_map/gather_mlp/pallas_call | solution.py:394
  103.8 79.1 %scatter_mlp.1 = (bf16[256,3072]{1,0:T(8,128)(2,1)}, f32[4,8,3072]{2,1,0:T(8,128)}, f32[8,1536]{1,0:T(8,128)}, f32[3072,1536]{1,0:T(8,128)}) custom-call(bf16[2048,1536]{1,0:T(8,128)(2,1)} %get-tuple-element.31.dz_ref, bf16[3072,1536]{1,0:T(8,128)(2,1)} %w1_ref.1, bf16[1536,3072]{1,0:T(8,128)(2,1)} %get-tuple-element.32.h2_ref, bf16[256,3072]{1,0:T(8,128)(2,1)} %bitcast.37, ...), custom_call_target="tpu_custom_call" | custom-call | flops 38654705664 | bytes 62914560 | tf_op jit(solution)/shard_map/scatter_mlp/pallas_call | solution.py:554
  182.9 1.4 reduce_sum.19
  184.3 113.4 %gather_attention.1 = (bf16[2048,1152]{1,0:T(8,128)(2,1)}, bf16[2048,384]{1,0:T(8,128)(2,1)}, bf16[2048,3072]{1,0:T(8,128)(2,1)}, bf16[1536,3072]{1,0:T(8,128)(2,1)}) custom-call(bf16[256,3072]{1,0:T(8,128)(2,1)} %get-tuple-element.34.dmid_ref.dmid_own_ref, bf16[4,2048,96]{2,1,0:T(8,128)(2,1)} %bitcast.26, bf16[4,2048,96]{2,1,0:T(8,128)(2,1)} %bitcast.27, ...), custom_call_target="tpu_custom_call" | custom-call | flops 17716740096 | bytes 62914560 | tf_op jit(solution)/shard_map/gather_attention/pallas_call | solution.py:773
  297.7 87.3 %scatter_qkv.1 = (bf16[256,3072]{1,0:T(8,128)(2,1)}, f32[6,3072]{1,0:T(8,128)}, f32[8,1152]{1,0:T(8,128)}, f32[1152,3072]{1,0:T(8,128)}, f32[384,3072]{1,0:T(8,128)}) custom-call(bf16[2048,1152]{1,0:T(8,128)(2,1)} %get-tuple-element.35.dqkv_ref, bf16[1152,3072]{1,0:T(8,128)(2,1)} %bitcast.30, bf16[1536,3072]{1,0:T(8,128)(2,1)} %get-tuple-element.36.h1_ref, ...), custom_call_target="tpu_custom_call" | custom-call | flops 28991029248 | bytes 62914560 | tf_op jit(solution)/shard_map/scatter_qkv/pallas_call | solution.py:930
  385.1 0.0 copy-start.2
  385.1 36.1 %emit.1 = (f32[1536,3072]{1,0:T(8,128)}, f32[3072,1536]{1,0:T(8,128)}, f32[1152,3072]{1,0:T(8,128)}, f32[384,3072]{1,0:T(8,128)}, bf16[256,3072]{1,0:T(8,128)(2,1)}, /*index=5*/f32[6,3072]{1,0:T(8,128)}) custom-call(f32[1536,3072]{1,0:T(8,128)} %get-tuple-element.30.refs_0_, f32[3072,1536]{1,0:T(8,128)} %get-tuple-element.33.refs_1_, ...), custom_call_target="tpu_custom_call" | custom-call | tf_op jit(solution)/shard_map/emit/pallas_call | solution.py:970
  421.2 0.0 copy-done.2
  421.2 0.7 reshape.52
  (1 shorter events, 0.0 us)
Async XLA Ops:
  0.6 6.3 %copy-start.1 = (bf16[1,2048,4,96]{1,3,2,0:T(8,128)(2,1)S(1)}, bf16[1,2048,4,96]{1,3,2,0:T(8,128)(2,1)}, u32[]{:S(2)}) copy-start(bf16[1,2048,4,96]{1,3,2,0:T(8,128)(2,1)} %param.20) | copy-start | bytes 4718596
  0.6 3.9 copy-start
  385.1 36.1 %copy-start.2 = (f32[8,1152]{1,0:T(8,128)S(1)}, f32[8,1152]{1,0:T(8,128)}, u32[]{:S(2)}) copy-start(f32[8,1152]{1,0:T(8,128)} %get-tuple-element.46) | copy-start | bytes 110596

commit v5 on v4

--- a/solution.py
+++ b/solution.py
@@ -584,7 +584,7 @@
 
 def gather_attention_kernel(axis_name, size, head_dim, dmid_ref, q_ref, k_ref, v_ref, wo_ref, xin_ref, gain_ref, bias_ref,
                             dqkv_hbm, ctx_hbm, dmid_hbm, h1_hbm,
-                            dmid, q_all, k_all, v_all, wo, xin, h1, s_scr, dp_scr, dk_acc, dv_acc, dctx_scr, ctx_scr, dq_scr,
+                            dmid, q_all, k_all, v_all, wo, xin, h1, s_scr, dp_scr, dk_acc, dv_acc, dctx_scr, q_blk, dctx_blk, ctx_scr, dq_scr,
                             m_scr, l_scr, d_scr, rows_out, pack_out,
                             local_sem, send_sem, recv_sem, h1_send_sem, h1_recv_sem, out_sem, own_sem):
     ring = Ring(axis_name, size)
@@ -624,8 +624,11 @@
         dst = dqkv_hbm.at[span(q_idx, rows), pl.ds(0, width)]
         return pltpu.make_async_copy(rows_out.at[1, r % 2], dst, out_sem.at[10 + r % 2])
 
-    def pack(scr, sl):
-        return jnp.concatenate([scr[head, sl, :] for head in range(n_heads)], axis=1).astype(jnp.bfloat16)
+    def pack(scr):
+        return jnp.concatenate([scr[head] for head in range(n_heads)], axis=1).astype(jnp.bfloat16)
+
+    def pack_turned(scr, sl):
+        return jnp.concatenate([scr[head, :, sl] for head in range(n_heads)], axis=0).T.astype(jnp.bfloat16)
 
     def block_body(r):
         @pl.when(r == 1)
@@ -663,9 +666,9 @@
         q_idx = gathered_block_owner(ring, r)
         q_rows = span(q_idx, rows)
         dmid_rows = span(r, rows)
-        dctx_all = dot(dmid[dmid_rows, :], wo[...], NT).astype(jnp.bfloat16)
+        dctx_all = dot(wo[...], dmid[dmid_rows, :], NT).astype(jnp.bfloat16)
         for head in range(n_heads):
-            dctx_scr[head] = dctx_all[:, head * head_dim:(head + 1) * head_dim]
+            dctx_scr[head] = dctx_all[head * head_dim:(head + 1) * head_dim, :]
 
         def head_group(g):
             heads = [g * group + i for i in range(group)]
@@ -676,15 +679,17 @@
                 return span(j, rows)
 
             for i, head in enumerate(heads):
-                dp_scr[i, q_idx] = dot(dctx_scr[head], v_all[head, q_rows, :], NT)
-                diag = jnp.where(row_ids >= col_ids, dot(q_all[head, q_rows, :], k_all[head, q_rows, :], NT), -1e30)
+                q_blk[i] = q_all[head, :, q_rows].T
+                dctx_blk[i] = dctx_scr[head].T
+                dp_scr[i, q_idx] = dot(dctx_blk[i], v_all[head, :, q_rows], NN)
+                diag = jnp.where(row_ids >= col_ids, dot(q_blk[i], k_all[head, :, q_rows], NN), -1e30)
                 s_scr[i, q_idx] = diag
                 m_scr[i] = lane_fold(diag, jnp.maximum)
 
             def pass_max(j):
                 for i, head in enumerate(heads):
-                    dp_scr[i, j] = dot(dctx_scr[head], v_all[head, k_rows(j), :], NT)
-                    s_blk = dot(q_all[head, q_rows, :], k_all[head, k_rows(j), :], NT)
+                    dp_scr[i, j] = dot(dctx_blk[i], v_all[head, :, k_rows(j)], NN)
+                    s_blk = dot(q_blk[i], k_all[head, :, k_rows(j)], NN)
                     s_scr[i, j] = s_blk
                     m_scr[i] = jnp.maximum(m_scr[i], lane_fold(s_blk, jnp.maximum))
 
@@ -718,17 +723,16 @@
                     prob = s_scr[i, j] * wide(l_scr[i])
                     prob_low = prob.astype(jnp.bfloat16)
                     ds_low = (prob * (dp_scr[i, j] - wide(d_scr[i])) * scale).astype(jnp.bfloat16)
-                    ctx_scr[head] += dot(prob_low, v_all[head, k_rows(j), :], NN)
-                    dq_scr[head] += dot(ds_low, k_all[head, k_rows(j), :], NN)
-                    dk_acc[head, k_rows(j), :] += dot(ds_low, q_all[head, q_rows, :], TN)
-                    dv_acc[head, k_rows(j), :] += dot(prob_low, dctx_scr[head], TN)
+                    ctx_scr[head] += dot(prob_low, v_all[head, :, k_rows(j)], NT)
+                    dq_scr[head] += dot(ds_low, k_all[head, :, k_rows(j)], NT)
+                    dk_acc[head, :, k_rows(j)] += dot(q_all[head, :, q_rows], ds_low, NN)
+                    dv_acc[head, :, k_rows(j)] += dot(dctx_scr[head], prob_low, NN)
 
             loop(q_idx + 1, pass_grad)
 
         loop(n_heads // group, head_group)
-        everything = pl.ds(0, rows)
-        rows_out[0, r % 2] = pack(ctx_scr, everything)
-        rows_out[1, r % 2] = pack(dq_scr, everything)
+        rows_out[0, r % 2] = pack(ctx_scr)
+        rows_out[1, r % 2] = pack(dq_scr)
         ctx_out(r).start()
         dq_out(r).start()
 
@@ -739,8 +743,8 @@
 
     def pack_body(i):
         sl = span(i, rows)
-        pack_out[0, sl, :] = pack(dk_acc, sl)
-        pack_out[1, sl, :] = pack(dv_acc, sl)
+        pack_out[0, sl, :] = pack_turned(dk_acc, sl)
+        pack_out[1, sl, :] = pack_turned(dv_acc, sl)
 
     loop(size, pack_body)
     packed = [pltpu.make_async_copy(pack_out.at[part], dqkv_hbm.at[:, pl.ds((1 + part) * width, width)], out_sem.at[12 + part]) for part in PARTS]
@@ -762,13 +766,13 @@
 def gather_attention(axis_name, size, grad_mid, q_heads, k_heads, v_heads, w_proj, x_in, gain, bias, collective_id):
     seq, n_heads, head_dim = q_heads.shape
     rows, d_model = grad_mid.shape
-    qp, kp, vp = (jnp.moveaxis(a, 1, 0) for a in (q_heads, k_heads, v_heads))
+    qp, kp, vp = (jnp.moveaxis(a, 0, 2) for a in (q_heads, k_heads, v_heads))
     width = n_heads * head_dim
     wo = w_proj.reshape(width, d_model)
     bf, f32, dma = jnp.bfloat16, jnp.float32, pltpu.SemaphoreType.DMA
     vm = pl.BlockSpec(memory_space=pltpu.VMEM)
     acc = lambda *shape: pltpu.VMEM(shape, f32)
-    heads = pltpu.VMEM((n_heads, seq, head_dim), bf)
+    heads = pltpu.VMEM((n_heads, head_dim, seq), bf)
     flops = 6 * n_heads * seq * seq * LANES + 2 * seq * d_model * width
     return pl.pallas_call(
         functools.partial(gather_attention_kernel, axis_name, size, head_dim),
@@ -778,8 +782,8 @@
                    jax.ShapeDtypeStruct((seq, d_model), bf), jax.ShapeDtypeStruct((seq - 2 * rows, d_model), bf)],
         scratch_shapes=[pltpu.VMEM((seq, d_model), bf), heads, heads, heads, pltpu.VMEM((width, d_model), bf),
                         pltpu.VMEM((rows, d_model), bf), pltpu.VMEM((rows, d_model), bf),
-                        acc(2, size, rows, rows), acc(2, size, rows, rows), acc(n_heads, seq, head_dim), acc(n_heads, seq, head_dim),
-                        pltpu.VMEM((n_heads, rows, head_dim), bf), acc(n_heads, rows, head_dim), acc(n_heads, rows, head_dim),
+                        acc(2, size, rows, rows), acc(2, size, rows, rows), acc(n_heads, head_dim, seq), acc(n_heads, head_dim, seq),
+                        pltpu.VMEM((n_heads, head_dim, rows), bf), pltpu.VMEM((2, rows, head_dim), bf), pltpu.VMEM((2, rows, head_dim), bf), acc(n_heads, rows, head_dim), acc(n_heads, rows, head_dim),
                         acc(2, rows, LANES), acc(2, rows, LANES), acc(2, rows, LANES),
                         pltpu.VMEM((2, 2, rows, width), bf), pltpu.VMEM((2, seq, width), bf),
                         dma((7,)), dma((Gather.N_COPIES,)), dma((Gather.N_COPIES,)), dma((Gather.N_COPIES,)), dma((Gather.N_COPIES,)), dma((14,)), dma(())],

time: 423 us -> 407 us (0.962)
  local copies, waits for them, and re-layouts: 9.33 us -> 0.68 us
  Pallas kernels: 410 us -> 403 us
    unnamed x9 -> x2, local copies, waits for them, and re-layouts: 8.65 us -> 0.01 us
    pallas_call x1, Pallas kernels: 113 us -> 106 us  [gather_attention(): pl.pallas_call(functools.partial(gather_attention_kernel, axis_name, size...]
where the time goes in v5:
time: 407 us; the launch traced here: 406 us
  Pallas kernels  403 us (99%)
    pallas_call x1, Pallas kernels, gather_attention(): pl.pallas_call(functools.partial(gather_attention_kernel, axis_name, size...  106 us
    pallas_call x1, Pallas kernels, gather_mlp(): pl.pallas_call(functools.partial(gather_mlp_kernel, axis_name, size), in_...  94.5 us
    pallas_call x1, Pallas kernels, scatter_qkv(): pl.pallas_call(functools.partial(scatter_qkv_kernel, axis_name, size), in...  87.3 us
    pallas_call x1, Pallas kernels, scatter_mlp(): pl.pallas_call(functools.partial(scatter_mlp_kernel, axis_name, size), in...  79.3 us
    pallas_call x1, Pallas kernels, emit(): pl.pallas_call(functools.partial(emit_kernel, n_parts), in_specs=[ANY] *...  36.1 us

profile of v5, /device:TPU:113, one launch (start us, length us, event | category | flops | bytes accessed | tf_op | source)
XLA Modules:
  0.0 405.7 jit_solution(167807501375820543)
XLA Ops:
  0.6 94.5 %gather_mlp.1 = (bf16[2048,1536]{1,0:T(8,128)(2,1)}, bf16[1536,3072]{1,0:T(8,128)(2,1)}, f32[1536,3072]{1,0:T(8,128)}) custom-call(bf16[256,3072]{1,0:T(8,128)(2,1)} %bitcast.31, bf16[2048,1536]{1,0:T(8,128)(2,1)} %bitcast.28, bf16[1536,3072]{1,0:T(8,128)(2,1)} %w2_ref.1, bf16[256,3072]{1,0:T(8,128)(2,1)} %bitcast.33, f32[1,3072]{1,0:T(1,128)} %bitcast.42, ...), custom_call_target="tpu_custom_call" | custom-call | flops 38654705664 | bytes 62914560 | tf_op jit(solution)/shard_map/gather_mlp/pallas_call | solution.py:394
  95.1 79.3 %scatter_mlp.1 = (bf16[256,3072]{1,0:T(8,128)(2,1)}, f32[4,8,3072]{2,1,0:T(8,128)}, f32[8,1536]{1,0:T(8,128)}, f32[3072,1536]{1,0:T(8,128)}) custom-call(bf16[2048,1536]{1,0:T(8,128)(2,1)} %get-tuple-element.31.dz_ref, bf16[3072,1536]{1,0:T(8,128)(2,1)} %w1_ref.1, bf16[1536,3072]{1,0:T(8,128)(2,1)} %get-tuple-element.32.h2_ref, bf16[256,3072]{1,0:T(8,128)(2,1)} %bitcast.34, ...), custom_call_target="tpu_custom_call" | custom-call | flops 38654705664 | bytes 62914560 | tf_op jit(solution)/shard_map/scatter_mlp/pallas_call | solution.py:554
  174.4 1.4 reduce_sum.19
  175.8 105.8 %gather_attention.1 = (bf16[2048,1152]{1,0:T(8,128)(2,1)}, bf16[2048,384]{1,0:T(8,128)(2,1)}, bf16[2048,3072]{1,0:T(8,128)(2,1)}, bf16[1536,3072]{1,0:T(8,128)(2,1)}) custom-call(bf16[256,3072]{1,0:T(8,128)(2,1)} %get-tuple-element.34.dmid_ref.dmid_own_ref, bf16[4,96,2048]{2,1,0:T(8,128)(2,1)} %bitcast.35, bf16[4,96,2048]{2,1,0:T(8,128)(2,1)} %bitcast.36, ...), custom_call_target="tpu_custom_call" | custom-call | flops 17716740096 | bytes 62914560 | tf_op jit(solution)/shard_map/gather_attention/pallas_call | solution.py:777
  281.6 87.3 %scatter_qkv.1 = (bf16[256,3072]{1,0:T(8,128)(2,1)}, f32[6,3072]{1,0:T(8,128)}, f32[8,1152]{1,0:T(8,128)}, f32[1152,3072]{1,0:T(8,128)}, f32[384,3072]{1,0:T(8,128)}) custom-call(bf16[2048,1152]{1,0:T(8,128)(2,1)} %get-tuple-element.35.dqkv_ref, bf16[1152,3072]{1,0:T(8,128)(2,1)} %bitcast.27, bf16[1536,3072]{1,0:T(8,128)(2,1)} %get-tuple-element.36.h1_ref, ...), custom_call_target="tpu_custom_call" | custom-call | flops 28991029248 | bytes 62914560 | tf_op jit(solution)/shard_map/scatter_qkv/pallas_call | solution.py:934
  368.9 0.0 copy-start
  368.9 36.1 %emit.1 = (f32[1536,3072]{1,0:T(8,128)}, f32[3072,1536]{1,0:T(8,128)}, f32[1152,3072]{1,0:T(8,128)}, f32[384,3072]{1,0:T(8,128)}, bf16[256,3072]{1,0:T(8,128)(2,1)}, /*index=5*/f32[6,3072]{1,0:T(8,128)}) custom-call(f32[1536,3072]{1,0:T(8,128)} %get-tuple-element.30.refs_0_, f32[3072,1536]{1,0:T(8,128)} %get-tuple-element.33.refs_1_, ...), custom_call_target="tpu_custom_call" | custom-call | tf_op jit(solution)/shard_map/emit/pallas_call | solution.py:974
  405.0 0.0 copy-done
  405.1 0.7 reshape.52
  (1 shorter events, 0.0 us)
Async XLA Ops:
  368.9 36.1 %copy-start = (f32[8,1152]{1,0:T(8,128)S(1)}, f32[8,1152]{1,0:T(8,128)}, u32[]{:S(2)}) copy-start(f32[8,1152]{1,0:T(8,128)} %get-tuple-element.46) | copy-start | bytes 110596

commit v6 on v5

--- a/solution.py
+++ b/solution.py
@@ -95,6 +95,7 @@
             dst[...] += vals[j * fold:(j + 1) * fold]
 
     loop(src.shape[0] // chunk, bias_body)
+    dst[...] = jnp.broadcast_to(sum_rows8(dst[...]), dst.shape)
 
 
 class Ring:
@@ -635,11 +636,11 @@
         def _():
             gather.recv(0)
             gather.first_halves()
+
+        @pl.when(r == 2)
+        def _():
+            gather.second_halves()
             h1_gather.start()
-
-        @pl.when(r == 2)
-        def _():
-            gather.second_halves()
 
         @pl.when(r == 3)
         def _():
@@ -993,10 +994,11 @@
         dqkv, ctx_rel, dmid_rel, h1_rel = gather_attention('tp', size, grad_mid, q_saved[0], k_saved[0], v_saved[0], w_proj, x_in[0], ln1_gain, ln1_bias, 2)
         wqkv_rows = jnp.moveaxis(w_qkv, 1, 3).reshape(3 * width, d_model)
         grad_x, grad_vecs, qkv_bias, dwqkv, dwo = scatter_qkv('tp', size, dqkv, wqkv_rows, h1_rel, ctx_rel, dmid_rel, x_in[0], grad_mid, ln1_gain, sums2, 3)
-        grad_wfc2, grad_wfc1, dwqkv, dwo, grad_x, grad_vecs = emit((grad_wfc2, grad_wfc1, dwqkv, dwo, grad_x, grad_vecs), (8, 8, 6, 2, 1, 1))
+        grad_wfc2, grad_wfc1, dwqkv, dwo, grad_x, grad_vecs, bias_sums, qkv_bias = emit(
+            (grad_wfc2, grad_wfc1, dwqkv, dwo, grad_x, grad_vecs, bias_sums, qkv_bias), (8, 8, 6, 2, 1, 1, 1, 1))
         grad_x = grad_x[None]
-        grad_bfc1 = jnp.sum(bias_sums, axis=0)
-        grad_bqkv = jnp.sum(qkv_bias, axis=0).reshape(3, n_heads, head_dim)
+        grad_bfc1 = bias_sums[0]
+        grad_bqkv = qkv_bias[0].reshape(3, n_heads, head_dim)
         grad_wqkv = jnp.moveaxis(dwqkv.reshape(3, n_heads, head_dim, d_model), 3, 1)
         grad_wproj = dwo.reshape(n_heads, head_dim, d_model)
         return grad_x, grad_wqkv, grad_bqkv, grad_wproj, grad_wfc1, grad_bfc1, grad_wfc2, grad_vecs

time: 407 us -> 407 us (level)
  no operation moved by 1% of the time
where the time goes in v6:
time: 407 us
  Pallas kernels  403 us (99%)
    pallas_call x1, Pallas kernels, gather_attention(): pl.pallas_call(functools.partial(gather_attention_kernel, axis_name, size...  106 us
    pallas_call x1, Pallas kernels, gather_mlp(): pl.pallas_call(functools.partial(gather_mlp_kernel, axis_name, size), in_...  94.5 us
    pallas_call x1, Pallas kernels, scatter_qkv(): pl.pallas_call(functools.partial(scatter_qkv_kernel, axis_name, size), in...  87.3 us
    pallas_call x1, Pallas kernels, scatter_mlp(): pl.pallas_call(functools.partial(scatter_mlp_kernel, axis_name, size), in...  79.3 us
    pallas_call x1, Pallas kernels, emit(): pl.pallas_call(functools.partial(emit_kernel, n_parts), in_specs=[ANY] *...  36.2 us

profile of v6, /device:TPU:113, one launch (start us, length us, event | category | flops | bytes accessed | tf_op | source)
XLA Modules:
  0.0 406.6 jit_solution(1045723909704769457)
XLA Ops:
  0.6 94.5 %gather_mlp.1 = (bf16[2048,1536]{1,0:T(8,128)(2,1)}, bf16[1536,3072]{1,0:T(8,128)(2,1)}, f32[1536,3072]{1,0:T(8,128)}) custom-call(bf16[256,3072]{1,0:T(8,128)(2,1)} %bitcast.31, bf16[2048,1536]{1,0:T(8,128)(2,1)} %bitcast.28, bf16[1536,3072]{1,0:T(8,128)(2,1)} %w2_ref.1, bf16[256,3072]{1,0:T(8,128)(2,1)} %bitcast.33, f32[1,3072]{1,0:T(1,128)} %bitcast.42, ...), custom_call_target="tpu_custom_call" | custom-call | flops 38654705664 | bytes 62914560 | tf_op jit(solution)/shard_map/gather_mlp/pallas_call | solution.py:395
  95.1 79.3 %scatter_mlp.1 = (bf16[256,3072]{1,0:T(8,128)(2,1)}, f32[4,8,3072]{2,1,0:T(8,128)}, f32[8,1536]{1,0:T(8,128)}, f32[3072,1536]{1,0:T(8,128)}) custom-call(bf16[2048,1536]{1,0:T(8,128)(2,1)} %get-tuple-element.33.dz_ref, bf16[3072,1536]{1,0:T(8,128)(2,1)} %w1_ref.1, bf16[1536,3072]{1,0:T(8,128)(2,1)} %get-tuple-element.34.h2_ref, bf16[256,3072]{1,0:T(8,128)(2,1)} %bitcast.34, ...), custom_call_target="tpu_custom_call" | custom-call | flops 38654705664 | bytes 62914560 | tf_op jit(solution)/shard_map/scatter_mlp/pallas_call | solution.py:555
  174.5 105.8 %gather_attention.1 = (bf16[2048,1152]{1,0:T(8,128)(2,1)}, bf16[2048,384]{1,0:T(8,128)(2,1)}, bf16[2048,3072]{1,0:T(8,128)(2,1)}, bf16[1536,3072]{1,0:T(8,128)(2,1)}) custom-call(bf16[256,3072]{1,0:T(8,128)(2,1)} %get-tuple-element.36.dmid_ref.dmid_own_ref, bf16[4,96,2048]{2,1,0:T(8,128)(2,1)} %bitcast.35, bf16[4,96,2048]{2,1,0:T(8,128)(2,1)} %bitcast.36, ...), custom_call_target="tpu_custom_call" | custom-call | flops 17716740096 | bytes 62914560 | tf_op jit(solution)/shard_map/gather_attention/pallas_call | solution.py:778
  280.3 87.3 %scatter_qkv.1 = (bf16[256,3072]{1,0:T(8,128)(2,1)}, f32[6,3072]{1,0:T(8,128)}, f32[8,1152]{1,0:T(8,128)}, f32[1152,3072]{1,0:T(8,128)}, f32[384,3072]{1,0:T(8,128)}) custom-call(bf16[2048,1152]{1,0:T(8,128)(2,1)} %get-tuple-element.37.dqkv_ref, bf16[1152,3072]{1,0:T(8,128)(2,1)} %bitcast.27, bf16[1536,3072]{1,0:T(8,128)(2,1)} %get-tuple-element.38.h1_ref, ...), custom_call_target="tpu_custom_call" | custom-call | flops 28991029248 | bytes 62914560 | tf_op jit(solution)/shard_map/scatter_qkv/pallas_call | solution.py:935
  367.5 36.2 %emit.1 = (f32[1536,3072]{1,0:T(8,128)}, f32[3072,1536]{1,0:T(8,128)}, f32[1152,3072]{1,0:T(8,128)}, f32[384,3072]{1,0:T(8,128)}, bf16[256,3072]{1,0:T(8,128)(2,...) custom-call(f32[1536,3072]{1,0:T(8,128)} %get-tuple-element.32.refs_0_, ...), custom_call_target="tpu_custom_call" | custom-call | tf_op jit(solution)/shard_map/emit/pallas_call | solution.py:975
  403.8 0.8 slice_reduce_fusion.1
  404.5 0.7 reshape_squeeze.3
  405.2 1.4 slice_reduce_fusion

commit v7 on v5

--- a/solution.py
+++ b/solution.py
@@ -593,7 +593,7 @@
     width = n_heads * head_dim
     scale = head_dim ** -0.5
     exp_scale = scale * math.log2(math.e)
-    group = 2
+    group = n_heads
     ring.barrier()
     gather = Gather(ring, dmid_ref, dmid, send_sem, recv_sem)
     gather.start()
@@ -616,13 +616,27 @@
         sl = pl.ds(rel * rows, rows)
         return pltpu.make_async_copy(dmid.at[sl], dmid_hbm.at[sl], out_sem.at[rel])
 
-    def ctx_out(r):
-        return pltpu.make_async_copy(rows_out.at[0, r % 2], ctx_hbm.at[span(r, rows)], out_sem.at[8 + r % 2])
-
-    def dq_out(r):
-        q_idx = gathered_block_owner(ring, r)
-        dst = dqkv_hbm.at[span(q_idx, rows), pl.ds(0, width)]
-        return pltpu.make_async_copy(rows_out.at[1, r % 2], dst, out_sem.at[10 + r % 2])
+    tile = rows // 2
+
+    def place(t):
+        stage, i = t // 4, t % 4
+        first, last = (3 - stage) // 3, stage // 3
+        middle, third = 1 - first - last, stage // 2 - last
+        rel = first * (i // 2) + middle * (2 + i) + last * (OPP + i % 2)
+        half = first * (i % 2) + (middle - third + last) * (i // 2) + third * (1 - i // 2)
+        return rel, half
+
+    def gathered_rows(t):
+        rel, half = place(t)
+        return span(2 * rel + half, tile)
+
+    def ctx_out(t):
+        return pltpu.make_async_copy(rows_out.at[0, t % 2], ctx_hbm.at[gathered_rows(t)], out_sem.at[8 + t % 2])
+
+    def dq_out(t):
+        rel, half = place(t)
+        dst = dqkv_hbm.at[span(2 * gathered_block_owner(ring, rel) + half, tile), pl.ds(0, width)]
+        return pltpu.make_async_copy(rows_out.at[1, t % 2], dst, out_sem.at[10 + t % 2])
 
     def pack(scr):
         return jnp.concatenate([scr[head] for head in range(n_heads)], axis=1).astype(jnp.bfloat16)
@@ -630,59 +644,62 @@
     def pack_turned(scr, sl):
         return jnp.concatenate([scr[head, :, sl] for head in range(n_heads)], axis=0).T.astype(jnp.bfloat16)
 
-    def block_body(r):
-        @pl.when(r == 1)
+    def tile_body(t):
+        @pl.when(t == 0)
         def _():
             gather.recv(0)
+
+        @pl.when(t == 4)
+        def _():
             gather.first_halves()
+            gather.recv(7, 8)
+
+        @pl.when(t == 8)
+        def _():
+            gather.second_halves()
             h1_gather.start()
-
-        @pl.when(r == 2)
-        def _():
-            gather.second_halves()
-
-        @pl.when(r == 3)
-        def _():
-            gather.recv(7, 9)
-
-        @pl.when(r == 5)
-        def _():
-            gather.recv(8, 10)
-
-        @pl.when(r == 6)
+            gather.recv(9, 10)
+
+        @pl.when(t == 12)
         def _():
             gather.opposite()
+            gather.recv(11, 12)
+
+        @pl.when(t == 14)
+        def _():
             h1_gather.first_halves()
 
-        @pl.when(r == 7)
-        def _():
-            gather.recv(11, 12)
-
-        @pl.when(r >= 2)
-        def _():
-            ctx_out(r - 2).wait()
-            dq_out(r - 2).wait()
-
-        q_idx = gathered_block_owner(ring, r)
-        q_rows = span(q_idx, rows)
-        dmid_rows = span(r, rows)
-        dctx_all = dot(wo[...], dmid[dmid_rows, :], NT).astype(jnp.bfloat16)
-        for head in range(n_heads):
-            dctx_scr[head] = dctx_all[head * head_dim:(head + 1) * head_dim, :]
+        @pl.when(t >= 2)
+        def _():
+            ctx_out(t - 2).wait()
+            dq_out(t - 2).wait()
+
+        @pl.when(t % 2 == 0)
+        def _():
+            both = jnp.concatenate([dmid[gathered_rows(t), :], dmid[gathered_rows(t + 1), :]], axis=0)
+            dctx_all = dot(wo[...], both, NT).astype(jnp.bfloat16)
+            for head in range(n_heads):
+                for side in PARTS:
+                    dctx_scr[side, head] = dctx_all[head * head_dim:(head + 1) * head_dim, side * tile:(side + 1) * tile]
+
+        rel, half = place(t)
+        q_idx = gathered_block_owner(ring, rel)
+        q_rows = span(2 * q_idx + half, tile)
+        k_diag = span(q_idx, rows)
 
         def head_group(g):
             heads = [g * group + i for i in range(group)]
-            row_ids = lax.broadcasted_iota(jnp.int32, (rows, rows), 0)
-            col_ids = lax.broadcasted_iota(jnp.int32, (rows, rows), 1)
+            row_ids = half * tile + lax.broadcasted_iota(jnp.int32, (tile, rows), 0)
+            col_ids = lax.broadcasted_iota(jnp.int32, (tile, rows), 1)
 
             def k_rows(j):
                 return span(j, rows)
 
             for i, head in enumerate(heads):
                 q_blk[i] = q_all[head, :, q_rows].T
-                dctx_blk[i] = dctx_scr[head].T
-                dp_scr[i, q_idx] = dot(dctx_blk[i], v_all[head, :, q_rows], NN)
-                diag = jnp.where(row_ids >= col_ids, dot(q_blk[i], k_all[head, :, q_rows], NN), -1e30)
+                dctx_blk[i] = dctx_scr[t % 2, head].T
+                dp_scr[i, q_idx] = dot(dctx_blk[i], v_all[head, :, k_diag], NN)
+                diag = jnp.where(row_ids >= col_ids, dot(q_blk[i], k_all[head, :, k_diag], NN), -1e30)
                 s_scr[i, q_idx] = diag
                 m_scr[i] = lane_fold(diag, jnp.maximum)
 
@@ -695,9 +712,9 @@
 
             loop(q_idx, pass_max)
             for i in range(group):
-                m_scr[i] = jnp.broadcast_to(jnp.max(m_scr[i], axis=1, keepdims=True), (rows, LANES))
-                l_scr[i] = jnp.zeros((rows, LANES), jnp.float32)
-                d_scr[i] = jnp.zeros((rows, LANES), jnp.float32)
+                m_scr[i] = jnp.broadcast_to(jnp.max(m_scr[i], axis=1, keepdims=True), (tile, LANES))
+                l_scr[i] = jnp.zeros((tile, LANES), jnp.float32)
+                d_scr[i] = jnp.zeros((tile, LANES), jnp.float32)
 
             def wide(stat):
                 return jnp.concatenate([stat] * (rows // LANES), axis=1)
@@ -713,10 +730,10 @@
             for i, head in enumerate(heads):
                 inv_sum = 1.0 / jnp.sum(l_scr[i], axis=1, keepdims=True)
                 delta = jnp.sum(d_scr[i], axis=1, keepdims=True) * inv_sum
-                l_scr[i] = jnp.broadcast_to(inv_sum, (rows, LANES))
-                d_scr[i] = jnp.broadcast_to(delta, (rows, LANES))
-                ctx_scr[head] = jnp.zeros((rows, head_dim), jnp.float32)
-                dq_scr[head] = jnp.zeros((rows, head_dim), jnp.float32)
+                l_scr[i] = jnp.broadcast_to(inv_sum, (tile, LANES))
+                d_scr[i] = jnp.broadcast_to(delta, (tile, LANES))
+                ctx_scr[head] = jnp.zeros((tile, head_dim), jnp.float32)
+                dq_scr[head] = jnp.zeros((tile, head_dim), jnp.float32)
 
             def pass_grad(j):
                 for i, head in enumerate(heads):
@@ -726,17 +743,18 @@
                     ctx_scr[head] += dot(prob_low, v_all[head, :, k_rows(j)], NT)
                     dq_scr[head] += dot(ds_low, k_all[head, :, k_rows(j)], NT)
                     dk_acc[head, :, k_rows(j)] += dot(q_all[head, :, q_rows], ds_low, NN)
-                    dv_acc[head, :, k_rows(j)] += dot(dctx_scr[head], prob_low, NN)
+                    dv_acc[head, :, k_rows(j)] += dot(dctx_scr[t % 2, head], prob_low, NN)
 
             loop(q_idx + 1, pass_grad)
 
         loop(n_heads // group, head_group)
-        rows_out[0, r % 2] = pack(ctx_scr)
-        rows_out[1, r % 2] = pack(dq_scr)
-        ctx_out(r).start()
-        dq_out(r).start()
-
-    loop(size, block_body)
+        rows_out[0, t % 2] = pack(ctx_scr)
+        rows_out[1, t % 2] = pack(dq_scr)
+        ctx_out(t).start()
+        dq_out(t).start()
+
+    n_tiles = 2 * size
+    loop(n_tiles, tile_body)
     h1_gather.second_halves()
     for rel in range(size):
         dmid_out(rel).start()
@@ -750,9 +768,9 @@
     packed = [pltpu.make_async_copy(pack_out.at[part], dqkv_hbm.at[:, pl.ds((1 + part) * width, width)], out_sem.at[12 + part]) for part in PARTS]
     for copy in packed:
         copy.start()
-    for r in (size - 2, size - 1):
-        ctx_out(r).wait()
-        dq_out(r).wait()
+    for t in (n_tiles - 2, n_tiles - 1):
+        ctx_out(t).wait()
+        dq_out(t).wait()
     for rel in range(size):
         dmid_out(rel).wait()
     for copy in packed:
@@ -773,6 +791,8 @@
     vm = pl.BlockSpec(memory_space=pltpu.VMEM)
     acc = lambda *shape: pltpu.VMEM(shape, f32)
     heads = pltpu.VMEM((n_heads, head_dim, seq), bf)
+    tile = rows // 2
+    turned = pltpu.VMEM((n_heads, tile, head_dim), bf)
     flops = 6 * n_heads * seq * seq * LANES + 2 * seq * d_model * width
     return pl.pallas_call(
         functools.partial(gather_attention_kernel, axis_name, size, head_dim),
@@ -782,10 +802,10 @@
                    jax.ShapeDtypeStruct((seq, d_model), bf), jax.ShapeDtypeStruct((seq - 2 * rows, d_model), bf)],
         scratch_shapes=[pltpu.VMEM((seq, d_model), bf), heads, heads, heads, pltpu.VMEM((width, d_model), bf),
                         pltpu.VMEM((rows, d_model), bf), pltpu.VMEM((rows, d_model), bf),
-                        acc(2, size, rows, rows), acc(2, size, rows, rows), acc(n_heads, head_dim, seq), acc(n_heads, head_dim, seq),
-                        pltpu.VMEM((n_heads, head_dim, rows), bf), pltpu.VMEM((2, rows, head_dim), bf), pltpu.VMEM((2, rows, head_dim), bf), acc(n_heads, rows, head_dim), acc(n_heads, rows, head_dim),
-                        acc(2, rows, LANES), acc(2, rows, LANES), acc(2, rows, LANES),
-                        pltpu.VMEM((2, 2, rows, width), bf), pltpu.VMEM((2, seq, width), bf),
+                        acc(n_heads, size, tile, rows), acc(n_heads, size, tile, rows), acc(n_heads, head_dim, seq), acc(n_heads, head_dim, seq),
+                        pltpu.VMEM((2, n_heads, head_dim, tile), bf), turned, turned, acc(n_heads, tile, head_dim), acc(n_heads, tile, head_dim),
+                        acc(n_heads, tile, LANES), acc(n_heads, tile, LANES), acc(n_heads, tile, LANES),
+                        pltpu.VMEM((2, 2, tile, width), bf), pltpu.VMEM((2, seq, width), bf),
                         dma((7,)), dma((Gather.N_COPIES,)), dma((Gather.N_COPIES,)), dma((Gather.N_COPIES,)), dma((Gather.N_COPIES,)), dma((14,)), dma(())],
         compiler_params=comm_params(collective_id),
         cost_estimate=pl.CostEstimate(flops=flops, bytes_accessed=60 * MIB, transcendentals=n_heads * seq * seq // 2),
@@ -806,8 +826,9 @@
     rows = xin.shape[0]
     d_model = wqkv.shape[1]
     pair, tile = 2 * rows, 256
+    steps = range(1, size)
     sem = pltpu.get_barrier_semaphore()
-    for step in range(1, size):
+    for step in steps:
         pl.semaphore_signal(sem, inc=1, device_id={axis_name: (ring.me + step) % size}, device_id_type=MESH_IDS)
     pl.semaphore_wait(sem, size - 1)
     relay = Relay(ring, h1_ref, h1_opp, relay_send, relay_recv)
@@ -856,7 +877,7 @@
         loop(tiles_per_part, body)
 
     scatter = scatter_grads(ring, stage, partial, peer_part, outbox, inbox, send_sem, recv_sem)
-    for step in range(1, size):
+    for step in steps:
         share(early_box, early_send, early_recv, step).start()
     relay.forward()
     n_tiles = d_model // tile
@@ -907,20 +928,20 @@
     norm_backward(scatter, rows, xin, dmid_own, gain_ref, gradx_ref, sums1)
     for i in PARTS:
         late_box[ring.me, pl.ds(i, 1), :] = sum_rows8(sums1[i])
-    for step in range(1, size):
+    for step in steps:
         share(late_box, late_send, late_recv, step).start()
-    for step in range(1, size):
+    for step in steps:
         shared(early_box, early_send, early_recv, step).wait_recv()
     scatter.drain()
-    for step in range(1, size):
+    for step in steps:
         shared(late_box, late_send, late_recv, step).wait_recv()
     late, early = late_box[0], early_box[0]
-    for src in range(1, size):
+    for src in steps:
         late = late + late_box[src]
         early = early + early_box[src]
     vecs_ref[pl.ds(0, 2), :] = late
     vecs_ref[pl.ds(2, 4), :] = early
-    for step in range(1, size):
+    for step in steps:
         share(early_box, early_send, early_recv, step).wait_send()
         share(late_box, late_send, late_recv, step).wait_send()
 

time: 407 us -> 404 us (level)
  no operation moved by 1% of the time
where the time goes in v7:
time: 404 us
  Pallas kernels  401 us (99%)
    pallas_call x1, Pallas kernels, gather_attention(): pl.pallas_call(functools.partial(gather_attention_kernel, axis_name, size...  106 us
    pallas_call x1, Pallas kernels, gather_mlp(): pl.pallas_call(functools.partial(gather_mlp_kernel, axis_name, size), in_...  94.5 us
    pallas_call x1, Pallas kernels, scatter_qkv(): pl.pallas_call(functools.partial(scatter_qkv_kernel, axis_name, size), in...  84.9 us
    pallas_call x1, Pallas kernels, scatter_mlp(): pl.pallas_call(functools.partial(scatter_mlp_kernel, axis_name, size), in...  79.3 us
    pallas_call x1, Pallas kernels, emit(): pl.pallas_call(functools.partial(emit_kernel, n_parts), in_specs=[ANY] *...  36.1 us

profile of v7, /device:TPU:113, one launch (start us, length us, event | category | flops | bytes accessed | tf_op | source)
XLA Modules:
  0.0 403.5 jit_solution(6694834723584850895)
XLA Ops:
  0.6 94.5 %gather_mlp.1 = (bf16[2048,1536]{1,0:T(8,128)(2,1)}, bf16[1536,3072]{1,0:T(8,128)(2,1)}, f32[1536,3072]{1,0:T(8,128)}) custom-call(bf16[256,3072]{1,0:T(8,128)(2,1)} %bitcast.31, bf16[2048,1536]{1,0:T(8,128)(2,1)} %bitcast.28, bf16[1536,3072]{1,0:T(8,128)(2,1)} %w2_ref.1, bf16[256,3072]{1,0:T(8,128)(2,1)} %bitcast.33, f32[1,3072]{1,0:T(1,128)} %bitcast.42, ...), custom_call_target="tpu_custom_call" | custom-call | flops 38654705664 | bytes 62914560 | tf_op jit(solution)/shard_map/gather_mlp/pallas_call | solution.py:394
  95.1 79.3 %scatter_mlp.1 = (bf16[256,3072]{1,0:T(8,128)(2,1)}, f32[4,8,3072]{2,1,0:T(8,128)}, f32[8,1536]{1,0:T(8,128)}, f32[3072,1536]{1,0:T(8,128)}) custom-call(bf16[2048,1536]{1,0:T(8,128)(2,1)} %get-tuple-element.31.dz_ref, bf16[3072,1536]{1,0:T(8,128)(2,1)} %w1_ref.1, bf16[1536,3072]{1,0:T(8,128)(2,1)} %get-tuple-element.32.h2_ref, bf16[256,3072]{1,0:T(8,128)(2,1)} %bitcast.34, ...), custom_call_target="tpu_custom_call" | custom-call | flops 38654705664 | bytes 62914560 | tf_op jit(solution)/shard_map/scatter_mlp/pallas_call | solution.py:554
  174.4 1.4 reduce_sum.19
  175.8 105.9 %gather_attention.1 = (bf16[2048,1152]{1,0:T(8,128)(2,1)}, bf16[2048,384]{1,0:T(8,128)(2,1)}, bf16[2048,3072]{1,0:T(8,128)(2,1)}, bf16[1536,3072]{1,0:T(8,128)(2,1)}) custom-call(bf16[256,3072]{1,0:T(8,128)(2,1)} %get-tuple-element.34.dmid_ref.dmid_own_ref, bf16[4,96,2048]{2,1,0:T(8,128)(2,1)} %bitcast.35, bf16[4,96,2048]{2,1,0:T(8,128)(2,1)} %bitcast.36, ...), custom_call_target="tpu_custom_call" | custom-call | flops 17716740096 | bytes 62914560 | tf_op jit(solution)/shard_map/gather_attention/pallas_call | solution.py:797
  281.8 84.9 %scatter_qkv.1 = (bf16[256,3072]{1,0:T(8,128)(2,1)}, f32[6,3072]{1,0:T(8,128)}, f32[8,1152]{1,0:T(8,128)}, f32[1152,3072]{1,0:T(8,128)}, f32[384,3072]{1,0:T(8,128)}) custom-call(bf16[2048,1152]{1,0:T(8,128)(2,1)} %get-tuple-element.35.dqkv_ref, bf16[1152,3072]{1,0:T(8,128)(2,1)} %bitcast.27, bf16[1536,3072]{1,0:T(8,128)(2,1)} %get-tuple-element.36.h1_ref, ...), custom_call_target="tpu_custom_call" | custom-call | flops 28991029248 | bytes 62914560 | tf_op jit(solution)/shard_map/scatter_qkv/pallas_call | solution.py:955
  366.7 0.0 copy-start
  366.7 36.1 %emit.1 = (f32[1536,3072]{1,0:T(8,128)}, f32[3072,1536]{1,0:T(8,128)}, f32[1152,3072]{1,0:T(8,128)}, f32[384,3072]{1,0:T(8,128)}, bf16[256,3072]{1,0:T(8,128)(2,1)}, /*index=5*/f32[6,3072]{1,0:T(8,128)}) custom-call(f32[1536,3072]{1,0:T(8,128)} %get-tuple-element.30.refs_0_, f32[3072,1536]{1,0:T(8,128)} %get-tuple-element.33.refs_1_, ...), custom_call_target="tpu_custom_call" | custom-call | tf_op jit(solution)/shard_map/emit/pallas_call | solution.py:995
  402.8 0.0 copy-done
  402.8 0.7 reshape.52
  (1 shorter events, 0.0 us)
Async XLA Ops:
  366.7 36.1 %copy-start = (f32[8,1152]{1,0:T(8,128)S(1)}, f32[8,1152]{1,0:T(8,128)}, u32[]{:S(2)}) copy-start(f32[8,1152]{1,0:T(8,128)} %get-tuple-element.46) | copy-start | bytes 110596

commit v8 on v7

--- a/solution.py
+++ b/solution.py
@@ -195,19 +195,21 @@
 class Relay:
     N_COPIES = 4
 
-    def __init__(self, ring, gathered, dst, send_sem, recv_sem):
+    def __init__(self, ring, gathered, dst, send_sem, recv_sem, first, count):
         self.ring, self.gathered, self.dst, self.send_sem, self.recv_sem = ring, gathered, dst, send_sem, recv_sem
-        self.rows = dst.shape[0] // 2
-        self.half = self.rows // 2
+        self.rows, self.first, self.count = dst.shape[0] // 2, first, count
+
+    def piece(self, ref, block, half):
+        return ref.at[pl.ds(block * self.rows + half * (self.rows // 2) + self.first, self.count)]
 
     def descriptor(self, idx):
         half = idx % 2
-        dst = self.dst.at[pl.ds(half * self.half, self.half)]
+        dst = self.piece(self.dst, OWN, half)
         if idx < 2:
             rel, peer = ((LEFT, self.ring.right), (RIGHT, self.ring.left))[half]
-            src = self.gathered.at[pl.ds(rel * self.rows + half * self.half, self.half)]
+            src = self.piece(self.gathered, rel, half)
         else:
-            src, dst, peer = dst, self.dst.at[pl.ds(self.rows + half * self.half, self.half)], self.ring.partner
+            src, dst, peer = dst, self.piece(self.dst, PARTNER, half), self.ring.partner
         return self.ring.copy(src, dst, self.send_sem.at[idx], self.recv_sem.at[idx], peer)
 
     def run(self, kind, *ids):
@@ -223,7 +225,7 @@
 
     def finish(self):
         self.run("wait_recv", 2, 3)
-        self.run("wait_send", 0, 1, 2, 3)
+        self.run("wait_send", *range(self.N_COPIES))
 
 
 class Scatter:
@@ -470,7 +472,7 @@
     pair, tile = 2 * rows, 256
     near = h2_ref.shape[0]
     ring.barrier()
-    relay = Relay(ring, h2_ref, h2_opp, relay_send, relay_recv)
+    relay = Relay(ring, h2_ref, h2_opp, relay_send, relay_recv, 0, rows // 2)
     relay.start()
     w1_half = d_model // 2
     halves = [pl.ds(part * w1_half, w1_half) for part in PARTS]
@@ -583,10 +585,10 @@
 
 
 def gather_attention_kernel(axis_name, size, head_dim, dmid_ref, q_ref, k_ref, v_ref, wo_ref, xin_ref, gain_ref, bias_ref,
-                            dqkv_hbm, ctx_hbm, dmid_hbm, h1_hbm,
+                            dqkv_hbm, ctx_hbm, dmid_hbm, h1_hbm, h1_early,
                             dmid, q_all, k_all, v_all, wo, xin, h1, s_scr, dp_scr, dk_acc, dv_acc, dctx_scr, q_blk, dctx_blk, ctx_scr, dq_scr,
                             m_scr, l_scr, d_scr, rows_out, pack_out,
-                            local_sem, send_sem, recv_sem, h1_send_sem, h1_recv_sem, out_sem, own_sem):
+                            local_sem, send_sem, recv_sem, h1_send_sem, h1_recv_sem, out_sem, own_sem, relay_send, relay_recv):
     ring = Ring(axis_name, size)
     rows = xin.shape[0]
     n_heads = q_all.shape[0]
@@ -607,6 +609,7 @@
     norm_block(xin, gain_ref, bias_ref, h1)
     h1_gather = Gather(ring, h1, h1_hbm, h1_send_sem, h1_recv_sem, relay=False)
     h1_own = pltpu.make_async_copy(h1, h1_gather.block(OWN), own_sem)
+    relay = Relay(ring, h1_hbm, h1_early, relay_send, relay_recv, 0, rows // 4)
     h1_own.start()
     own_copy.wait()
     for copy in loads[1:]:
@@ -665,9 +668,10 @@
             gather.opposite()
             gather.recv(11, 12)
 
-        @pl.when(t == 14)
+        @pl.when(t == 13)
         def _():
             h1_gather.first_halves()
+            relay.start()
 
         @pl.when(t >= 2)
         def _():
@@ -756,6 +760,7 @@
     n_tiles = 2 * size
     loop(n_tiles, tile_body)
     h1_gather.second_halves()
+    relay.forward()
     for rel in range(size):
         dmid_out(rel).start()
 
@@ -777,6 +782,7 @@
         copy.wait()
     h1_own.wait()
     h1_gather.recv(0, 7, 8, 9, 10)
+    relay.finish()
     gather.drain()
     h1_gather.drain()
 
@@ -797,16 +803,16 @@
     return pl.pallas_call(
         functools.partial(gather_attention_kernel, axis_name, size, head_dim),
         in_specs=[ANY] * 6 + [vm, vm],
-        out_specs=[ANY] * 4,
+        out_specs=[ANY] * 5,
         out_shape=[jax.ShapeDtypeStruct((seq, 3 * width), bf), jax.ShapeDtypeStruct((seq, width), bf),
-                   jax.ShapeDtypeStruct((seq, d_model), bf), jax.ShapeDtypeStruct((seq - 2 * rows, d_model), bf)],
+                   jax.ShapeDtypeStruct((seq, d_model), bf), jax.ShapeDtypeStruct((seq - 2 * rows, d_model), bf), jax.ShapeDtypeStruct((2 * rows, d_model), bf)],
         scratch_shapes=[pltpu.VMEM((seq, d_model), bf), heads, heads, heads, pltpu.VMEM((width, d_model), bf),
                         pltpu.VMEM((rows, d_model), bf), pltpu.VMEM((rows, d_model), bf),
                         acc(n_heads, size, tile, rows), acc(n_heads, size, tile, rows), acc(n_heads, head_dim, seq), acc(n_heads, head_dim, seq),
                         pltpu.VMEM((2, n_heads, head_dim, tile), bf), turned, turned, acc(n_heads, tile, head_dim), acc(n_heads, tile, head_dim),
                         acc(n_heads, tile, LANES), acc(n_heads, tile, LANES), acc(n_heads, tile, LANES),
                         pltpu.VMEM((2, 2, tile, width), bf), pltpu.VMEM((2, seq, width), bf),
-                        dma((7,)), dma((Gather.N_COPIES,)), dma((Gather.N_COPIES,)), dma((Gather.N_COPIES,)), dma((Gather.N_COPIES,)), dma((14,)), dma(())],
+                        dma((7,)), dma((Gather.N_COPIES,)), dma((Gather.N_COPIES,)), dma((Gather.N_COPIES,)), dma((Gather.N_COPIES,)), dma((14,)), dma(()), dma((Relay.N_COPIES,)), dma((Relay.N_COPIES,))],
         compiler_params=comm_params(collective_id),
         cost_estimate=pl.CostEstimate(flops=flops, bytes_accessed=60 * MIB, transcendentals=n_heads * seq * seq // 2),
         name="gather_attention",
@@ -817,7 +823,7 @@
     return jnp.sum(vals, axis=0, keepdims=True)
 
 
-def scatter_qkv_kernel(axis_name, size, dqkv_ref, wqkv_ref, h1_ref, ctx_ref, dmid_ref, xin_ref, dmid_own_ref, gain_ref, sums2_ref,
+def scatter_qkv_kernel(axis_name, size, dqkv_ref, wqkv_ref, h1_ref, h1_early, ctx_ref, dmid_ref, xin_ref, dmid_own_ref, gain_ref, sums2_ref,
                        gradx_ref, vecs_ref, dbqkv_ref, dwqkv_hbm, dwo_hbm,
                        dqkv, wqkv, ctx, h1_tile, dmid_tile, dwqkv_tile, dwo_tile, xin, dmid_own, h1_opp, sums1, early_box, late_box,
                        partial, peer_part, outbox, inbox,
@@ -831,7 +837,8 @@
     for step in steps:
         pl.semaphore_signal(sem, inc=1, device_id={axis_name: (ring.me + step) % size}, device_id_type=MESH_IDS)
     pl.semaphore_wait(sem, size - 1)
-    relay = Relay(ring, h1_ref, h1_opp, relay_send, relay_recv)
+    late_rows = rows // 4
+    relay = Relay(ring, h1_ref, h1_opp, relay_send, relay_recv, late_rows, late_rows)
     relay.start()
     near = h1_ref.shape[0]
 
@@ -840,15 +847,16 @@
     owners = [ring.block_owner(rel) for rel in range(size)]
     ctx_copy, xin_copy, own_copy, *copies = local_copies(
         [(ctx_ref, ctx), (xin_ref, xin), (dmid_own_ref, dmid_own)] + [(wqkv_ref.at[:, sl], wqkv.at[:, sl]) for sl in halves]
-        + [(dqkv_ref.at[span(owner, rows)], dqkv.at[pl.ds(rel * rows, rows)]) for rel, owner in enumerate(owners)], local_sem)
-    w_copies, dqkv_copies = copies[:len(halves)], copies[len(halves):]
+        + [(dqkv_ref.at[span(owner, rows)], dqkv.at[pl.ds(rel * rows, rows)]) for rel, owner in enumerate(owners)]
+        + [(h1_early.at[sl], h1_opp.at[sl]) for sl in (pl.ds(i * 2 * late_rows, late_rows) for i in range(4))], local_sem)
+    w_copies, dqkv_copies, early_copies = copies[:len(halves)], copies[len(halves):len(halves) + size], copies[len(halves) + size:]
     for copy in dqkv_copies[OPP:]:
         copy.start()
     for copy in w_copies:
         copy.start()
     for copy in dqkv_copies[LEFT:OPP] + dqkv_copies[:LEFT]:
         copy.start()
-    for copy in (ctx_copy, xin_copy, own_copy):
+    for copy in (ctx_copy, xin_copy, own_copy, *early_copies):
         copy.start()
 
     def share(box, send, recv, step):
@@ -894,7 +902,8 @@
 
     for copy in tile_in(0, 0):
         copy.start()
-    ctx_copy.wait()
+    for copy in (ctx_copy, *early_copies):
+        copy.wait()
     relay.finish()
 
     def dw_body(i):
@@ -946,7 +955,7 @@
         share(late_box, late_send, late_recv, step).wait_send()
 
 
-def scatter_qkv(axis_name, size, dqkv, wqkv_rows, h1_rel, ctx_rel, dmid_rel, x_in, grad_mid, gain, sums2, collective_id):
+def scatter_qkv(axis_name, size, dqkv, wqkv_rows, h1_rel, h1_early, ctx_rel, dmid_rel, x_in, grad_mid, gain, sums2, collective_id):
     rows, d_model = x_in.shape
     seq, width3 = dqkv.shape
     width = width3 // 3
@@ -954,7 +963,7 @@
     vm = pl.BlockSpec(memory_space=pltpu.VMEM)
     return pl.pallas_call(
         functools.partial(scatter_qkv_kernel, axis_name, size),
-        in_specs=[ANY] * 7 + [vm, vm],
+        in_specs=[ANY] * 8 + [vm, vm],
         out_specs=[vm, vm, vm, ANY, ANY],
         out_shape=[jax.ShapeDtypeStruct((rows, d_model), bf), jax.ShapeDtypeStruct((6, d_model), f32),
                    jax.ShapeDtypeStruct((8, width3), f32), jax.ShapeDtypeStruct((width3, d_model), f32),
@@ -965,11 +974,11 @@
                         pltpu.VMEM((rows, d_model), bf), pltpu.VMEM((rows, d_model), bf), pltpu.VMEM((2 * rows, d_model), bf), pltpu.VMEM((4, 8, d_model), f32),
                         pltpu.VMEM((size, 4, d_model), f32), pltpu.VMEM((size, 2, d_model), f32)]
         + scatter_scratch(size, rows, d_model)
-        + [dma((17,)), dma((Scatter.N_COPIES,)), dma((Scatter.N_COPIES,)), dma((8,)), dma((Relay.N_COPIES,)), dma((Relay.N_COPIES,)), dma((size,)), dma((size,)), dma((size,)), dma((size,))],
+        + [dma((21,)), dma((Scatter.N_COPIES,)), dma((Scatter.N_COPIES,)), dma((8,)), dma((Relay.N_COPIES,)), dma((Relay.N_COPIES,)), dma((size,)), dma((size,)), dma((size,)), dma((size,))],
         compiler_params=comm_params(collective_id),
         cost_estimate=pl.CostEstimate(flops=4 * seq * width3 * d_model, bytes_accessed=60 * MIB, transcendentals=0),
         name="scatter_qkv",
-    )(dqkv, wqkv_rows, h1_rel, ctx_rel, dmid_rel, x_in, grad_mid, as_row(gain), sums2)
+    )(dqkv, wqkv_rows, h1_rel, h1_early, ctx_rel, dmid_rel, x_in, grad_mid, as_row(gain), sums2)
 
 
 def emit_kernel(n_parts, *refs):
@@ -1011,9 +1020,9 @@
         n_heads, head_dim = q_saved.shape[2:]
         d_model = d_out.shape[-1]
         width = n_heads * head_dim
-        dqkv, ctx_rel, dmid_rel, h1_rel = gather_attention('tp', size, grad_mid, q_saved[0], k_saved[0], v_saved[0], w_proj, x_in[0], ln1_gain, ln1_bias, 2)
+        dqkv, ctx_rel, dmid_rel, h1_rel, h1_early = gather_attention('tp', size, grad_mid, q_saved[0], k_saved[0], v_saved[0], w_proj, x_in[0], ln1_gain, ln1_bias, 2)
         wqkv_rows = jnp.moveaxis(w_qkv, 1, 3).reshape(3 * width, d_model)
-        grad_x, grad_vecs, qkv_bias, dwqkv, dwo = scatter_qkv('tp', size, dqkv, wqkv_rows, h1_rel, ctx_rel, dmid_rel, x_in[0], grad_mid, ln1_gain, sums2, 3)
+        grad_x, grad_vecs, qkv_bias, dwqkv, dwo = scatter_qkv('tp', size, dqkv, wqkv_rows, h1_rel, h1_early, ctx_rel, dmid_rel, x_in[0], grad_mid, ln1_gain, sums2, 3)
         grad_wfc2, grad_wfc1, dwqkv, dwo, grad_x, grad_vecs = emit((grad_wfc2, grad_wfc1, dwqkv, dwo, grad_x, grad_vecs), (8, 8, 6, 2, 1, 1))
         grad_x = grad_x[None]
         grad_bfc1 = jnp.sum(bias_sums, axis=0)
@@ -1022,11 +1031,9 @@
         grad_wproj = dwo.reshape(n_heads, head_dim, d_model)
         return grad_x, grad_wqkv, grad_bqkv, grad_wproj, grad_wfc1, grad_bfc1, grad_wfc2, grad_vecs
 
-    tok_spec = P('dp', 'tp', None)
-    head_spec = P('dp', None, 'tp', None)
-    in_specs = (tok_spec, tok_spec, tok_spec, head_spec, head_spec, head_spec, P('dp', None, 'tp'),
-                P(None), P(None), P(None), P(None),
-                P(None, None, 'tp', None), P('tp', None, None), P(None, 'tp'), P('tp', None))
-    out_specs = (tok_spec, P('dp', None, 'tp', None), P('dp', 'tp', None), P(('dp', 'tp'), None, None),
-                 P('dp', 'tp'), P(('dp', 'tp')), P(('dp', 'tp'), None), P('dp', None))
+    tok_spec = P('dp', 'tp')
+    head_spec = P('dp', None, 'tp')
+    in_specs = (tok_spec, tok_spec, tok_spec, head_spec, head_spec, head_spec, head_spec, P(), P(), P(), P(),
+                P(None, None, 'tp'), P('tp'), P(None, 'tp'), P('tp'))
+    out_specs = (tok_spec, head_spec, P('dp', 'tp'), P(('dp', 'tp')), P('dp', 'tp'), P(('dp', 'tp')), P(('dp', 'tp')), P('dp'))
     return jax.shard_map(local_backward, mesh=mesh, in_specs=in_specs, out_specs=out_specs, check_vma=False)

time: 404 us -> 400 us (0.990)
  Pallas kernels: 401 us -> 396 us
    pallas_call x1, Pallas kernels: 84.9 us -> 80.4 us  [scatter_qkv(): pl.pallas_call(functools.partial(scatter_qkv_kernel, axis_name, size), in...]
where the time goes in v8:
time: 400 us; the launch traced here: 399 us
  Pallas kernels  396 us (99%)
    pallas_call x1, Pallas kernels, gather_attention(): pl.pallas_call(functools.partial(gather_attention_kernel, axis_name, size...  106 us
    pallas_call x1, Pallas kernels, gather_mlp(): pl.pallas_call(functools.partial(gather_mlp_kernel, axis_name, size), in_...  94.5 us
    pallas_call x1, Pallas kernels, scatter_qkv(): pl.pallas_call(functools.partial(scatter_qkv_kernel, axis_name, size), in...  80.4 us
    pallas_call x1, Pallas kernels, scatter_mlp(): pl.pallas_call(functools.partial(scatter_mlp_kernel, axis_name, size), in...  79.3 us
    pallas_call x1, Pallas kernels, emit(): pl.pallas_call(functools.partial(emit_kernel, n_parts), in_specs=[ANY] *...  36.1 us

profile of v8, /device:TPU:113, one launch (start us, length us, event | category | flops | bytes accessed | tf_op | source)
XLA Modules:
  0.0 399.1 jit_solution(17120949593119420895)
XLA Ops:
  0.6 94.5 %gather_mlp.1 = (bf16[2048,1536]{1,0:T(8,128)(2,1)}, bf16[1536,3072]{1,0:T(8,128)(2,1)}, f32[1536,3072]{1,0:T(8,128)}) custom-call(bf16[256,3072]{1,0:T(8,128)(2,1)} %bitcast.31, bf16[2048,1536]{1,0:T(8,128)(2,1)} %bitcast.28, bf16[1536,3072]{1,0:T(8,128)(2,1)} %w2_ref.1, bf16[256,3072]{1,0:T(8,128)(2,1)} %bitcast.33, f32[1,3072]{1,0:T(1,128)} %bitcast.42, ...), custom_call_target="tpu_custom_call" | custom-call | flops 38654705664 | bytes 62914560 | tf_op jit(solution)/shard_map/gather_mlp/pallas_call | solution.py:396
  95.1 79.3 %scatter_mlp.1 = (bf16[256,3072]{1,0:T(8,128)(2,1)}, f32[4,8,3072]{2,1,0:T(8,128)}, f32[8,1536]{1,0:T(8,128)}, f32[3072,1536]{1,0:T(8,128)}) custom-call(bf16[2048,1536]{1,0:T(8,128)(2,1)} %get-tuple-element.32.dz_ref, bf16[3072,1536]{1,0:T(8,128)(2,1)} %w1_ref.1, bf16[1536,3072]{1,0:T(8,128)(2,1)} %get-tuple-element.33.h2_ref, bf16[256,3072]{1,0:T(8,128)(2,1)} %bitcast.34, ...), custom_call_target="tpu_custom_call" | custom-call | flops 38654705664 | bytes 62914560 | tf_op jit(solution)/shard_map/scatter_mlp/pallas_call | solution.py:556
  174.4 1.4 reduce_sum.19
  175.8 106.0 %gather_attention.1 = (bf16[2048,1152]{1,0:T(8,128)(2,1)}, bf16[2048,384]{1,0:T(8,128)(2,1)}, bf16[2048,3072]{1,0:T(8,128)(2,1)}, bf16[1536,3072]{1,0:T(8,128)(2,1)}, bf16[512,3072]{1,0:T(8,128)(2,1)}) custom-call(bf16[256,3072]{1,0:T(8,128)(2,1)} %get-tuple-element.35.dmid_ref.dmid_own_ref, bf16[4,96,2048]{2,1,0:T(8,128)(2,1)} %bitcast.35, ...), custom_call_target="tpu_custom_call" | custom-call | flops 17716740096 | bytes 62914560 | tf_op jit(solution)/shard_map/gather_attention/pallas_call | solution.py:803
  281.9 80.4 %scatter_qkv.1 = (bf16[256,3072]{1,0:T(8,128)(2,1)}, f32[6,3072]{1,0:T(8,128)}, f32[8,1152]{1,0:T(8,128)}, f32[1152,3072]{1,0:T(8,128)}, f32[384,3072]{1,0:T(8,128)}) custom-call(bf16[2048,1152]{1,0:T(8,128)(2,1)} %get-tuple-element.36.dqkv_ref, bf16[1152,3072]{1,0:T(8,128)(2,1)} %bitcast.27, bf16[1536,3072]{1,0:T(8,128)(2,1)} %get-tuple-element.37.h1_ref, ...), custom_call_target="tpu_custom_call" | custom-call | flops 28991029248 | bytes 62914560 | tf_op jit(solution)/shard_map/scatter_qkv/pallas_call | solution.py:964
  362.3 0.0 copy-start
  362.3 36.1 %emit.1 = (f32[1536,3072]{1,0:T(8,128)}, f32[3072,1536]{1,0:T(8,128)}, f32[1152,3072]{1,0:T(8,128)}, f32[384,3072]{1,0:T(8,128)}, bf16[256,3072]{1,0:T(8,128)(2,1)}, /*index=5*/f32[6,3072]{1,0:T(8,128)}) custom-call(f32[1536,3072]{1,0:T(8,128)} %get-tuple-element.31.refs_0_, f32[3072,1536]{1,0:T(8,128)} %get-tuple-element.34.refs_1_, ...), custom_call_target="tpu_custom_call" | custom-call | tf_op jit(solution)/shard_map/emit/pallas_call | solution.py:1004
  398.4 0.0 copy-done
  398.5 0.7 reshape.52
  (1 shorter events, 0.0 us)
Async XLA Ops:
  362.3 36.1 %copy-start = (f32[8,1152]{1,0:T(8,128)S(1)}, f32[8,1152]{1,0:T(8,128)}, u32[]{:S(2)}) copy-start(f32[8,1152]{1,0:T(8,128)} %get-tuple-element.48) | copy-start | bytes 110596

commit v9 on v8

--- a/solution.py
+++ b/solution.py
@@ -666,12 +666,11 @@
         @pl.when(t == 12)
         def _():
             gather.opposite()
-            gather.recv(11, 12)
-
-        @pl.when(t == 13)
-        def _():
             h1_gather.first_halves()
             relay.start()
+            gather.recv(11, 12)
+            for rel in range(size):
+                dmid_out(rel).start()
 
         @pl.when(t >= 2)
         def _():
@@ -761,8 +760,6 @@
     loop(n_tiles, tile_body)
     h1_gather.second_halves()
     relay.forward()
-    for rel in range(size):
-        dmid_out(rel).start()
 
     def pack_body(i):
         sl = span(i, rows)

time: 400 us -> 402 us (level)
  no operation moved by 1% of the time
where the time goes in v9:
time: 402 us; the launch traced here: 401 us
  Pallas kernels  398 us (99%)
    pallas_call x1, Pallas kernels, gather_attention(): pl.pallas_call(functools.partial(gather_attention_kernel, axis_name, size...  104 us
    pallas_call x1, Pallas kernels, gather_mlp(): pl.pallas_call(functools.partial(gather_mlp_kernel, axis_name, size), in_...  94.5 us
    pallas_call x1, Pallas kernels, scatter_qkv(): pl.pallas_call(functools.partial(scatter_qkv_kernel, axis_name, size), in...  83.8 us
    pallas_call x1, Pallas kernels, scatter_mlp(): pl.pallas_call(functools.partial(scatter_mlp_kernel, axis_name, size), in...  79.3 us
    pallas_call x1, Pallas kernels, emit(): pl.pallas_call(functools.partial(emit_kernel, n_parts), in_specs=[ANY] *...  36.1 us

profile of v9, /device:TPU:113, one launch (start us, length us, event | category | flops | bytes accessed | tf_op | source)
XLA Modules:
  0.0 401.0 jit_solution(1131558015739888899)
XLA Ops:
  0.6 94.5 %gather_mlp.1 = (bf16[2048,1536]{1,0:T(8,128)(2,1)}, bf16[1536,3072]{1,0:T(8,128)(2,1)}, f32[1536,3072]{1,0:T(8,128)}) custom-call(bf16[256,3072]{1,0:T(8,128)(2,1)} %bitcast.31, bf16[2048,1536]{1,0:T(8,128)(2,1)} %bitcast.28, bf16[1536,3072]{1,0:T(8,128)(2,1)} %w2_ref.1, bf16[256,3072]{1,0:T(8,128)(2,1)} %bitcast.33, f32[1,3072]{1,0:T(1,128)} %bitcast.42, ...), custom_call_target="tpu_custom_call" | custom-call | flops 38654705664 | bytes 62914560 | tf_op jit(solution)/shard_map/gather_mlp/pallas_call | solution.py:396
  95.1 79.3 %scatter_mlp.1 = (bf16[256,3072]{1,0:T(8,128)(2,1)}, f32[4,8,3072]{2,1,0:T(8,128)}, f32[8,1536]{1,0:T(8,128)}, f32[3072,1536]{1,0:T(8,128)}) custom-call(bf16[2048,1536]{1,0:T(8,128)(2,1)} %get-tuple-element.32.dz_ref, bf16[3072,1536]{1,0:T(8,128)(2,1)} %w1_ref.1, bf16[1536,3072]{1,0:T(8,128)(2,1)} %get-tuple-element.33.h2_ref, bf16[256,3072]{1,0:T(8,128)(2,1)} %bitcast.34, ...), custom_call_target="tpu_custom_call" | custom-call | flops 38654705664 | bytes 62914560 | tf_op jit(solution)/shard_map/scatter_mlp/pallas_call | solution.py:556
  174.4 1.4 reduce_sum.19
  175.8 104.5 %gather_attention.1 = (bf16[2048,1152]{1,0:T(8,128)(2,1)}, bf16[2048,384]{1,0:T(8,128)(2,1)}, bf16[2048,3072]{1,0:T(8,128)(2,1)}, bf16[1536,3072]{1,0:T(8,128)(2,1)}, bf16[512,3072]{1,0:T(8,128)(2,1)}) custom-call(bf16[256,3072]{1,0:T(8,128)(2,1)} %get-tuple-element.35.dmid_ref.dmid_own_ref, bf16[4,96,2048]{2,1,0:T(8,128)(2,1)} %bitcast.35, ...), custom_call_target="tpu_custom_call" | custom-call | flops 17716740096 | bytes 62914560 | tf_op jit(solution)/shard_map/gather_attention/pallas_call | solution.py:800
  280.3 83.8 %scatter_qkv.1 = (bf16[256,3072]{1,0:T(8,128)(2,1)}, f32[6,3072]{1,0:T(8,128)}, f32[8,1152]{1,0:T(8,128)}, f32[1152,3072]{1,0:T(8,128)}, f32[384,3072]{1,0:T(8,128)}) custom-call(bf16[2048,1152]{1,0:T(8,128)(2,1)} %get-tuple-element.36.dqkv_ref, bf16[1152,3072]{1,0:T(8,128)(2,1)} %bitcast.27, bf16[1536,3072]{1,0:T(8,128)(2,1)} %get-tuple-element.37.h1_ref, ...), custom_call_target="tpu_custom_call" | custom-call | flops 28991029248 | bytes 62914560 | tf_op jit(solution)/shard_map/scatter_qkv/pallas_call | solution.py:961
  364.1 0.0 copy-start
  364.1 36.1 %emit.1 = (f32[1536,3072]{1,0:T(8,128)}, f32[3072,1536]{1,0:T(8,128)}, f32[1152,3072]{1,0:T(8,128)}, f32[384,3072]{1,0:T(8,128)}, bf16[256,3072]{1,0:T(8,128)(2,1)}, /*index=5*/f32[6,3072]{1,0:T(8,128)}) custom-call(f32[1536,3072]{1,0:T(8,128)} %get-tuple-element.31.refs_0_, f32[3072,1536]{1,0:T(8,128)} %get-tuple-element.34.refs_1_, ...), custom_call_target="tpu_custom_call" | custom-call | tf_op jit(solution)/shard_map/emit/pallas_call | solution.py:1001
  400.3 0.0 copy-done
  400.3 0.7 reshape.52
  (1 shorter events, 0.0 us)
Async XLA Ops:
  364.1 36.1 %copy-start = (f32[8,1152]{1,0:T(8,128)S(1)}, f32[8,1152]{1,0:T(8,128)}, u32[]{:S(2)}) copy-start(f32[8,1152]{1,0:T(8,128)} %get-tuple-element.48) | copy-start | bytes 110596
